TPU v7x, 32 devices: a whole 2x2x4 slice. The times are simulated.
32 devices in a mesh: shard: 8 (over z, x), tp: 4 (over y, core).
Axes of the slice: x: 2, y: 2, z: 4, core: 2. Of those that a mesh axis runs over, the one named last changes fastest.
Arguments:
- one_gate: float32 [2048, 8192], P('shard', 'tp'), may hold values from -0.1875 to 0.1875
- other_gate: float32 [2048, 8192], P('shard', 'tp'), may hold values from -0.125 to 0.125
- one_up: float32 [2048, 8192], P('shard', 'tp'), may hold values from -0.1875 to 0.1875
- other_up: float32 [2048, 8192], P('shard', 'tp'), may hold values from -0.125 to 0.125
- mix_share: float32 [2048], P('shard'), may hold values from 0.2 to 0.8
- norm_train: float32 [2048], P(('shard', 'tp')), may hold values from 0.25 to 1.75
- norm_step: float32 [2048], P(('shard', 'tp')), may hold values from -0.3 to 0.3
Outputs:
- serve_gate: bfloat16 [2048, 8192], P(None, 'tp')
- serve_up: bfloat16 [2048, 8192], P(None, 'tp')
- factor_gate: float32 [8192], P('tp')
- factor_up: float32 [8192], P('tp')
- serve_norm: bfloat16 [2048], replicated
All inputs are finite; a program needn't handle non-finite values.
Results may differ from a plain program's by a relative error of at most 0.0004.
Values may be sent and summed in bfloat16 or wider, within the bound.
No kernel may reach another device: no remote copies, remote signals or barrier semaphores. Data moves between devices by JAX's collectives and lax.ppermute only.
A program may use at most 128 MiB of HBM per device.

v0:
```python
import jax
import jax.numpy as jnp
from jax import lax
from jax.sharding import PartitionSpec as P


def shards(one_gate, other_gate, one_up, other_up, mix_share, norm_train, norm_step):
    fresh_gate = mix_share[:, None] * one_gate + (1.0 - mix_share[:, None]) * other_gate
    fresh_up = mix_share[:, None] * one_up + (1.0 - mix_share[:, None]) * other_up
    total_gate, total_up = lax.psum(
        (jnp.sum(fresh_gate * fresh_gate, axis=0), jnp.sum(fresh_up * fresh_up, axis=0)), "shard"
    )
    factor_gate = jnp.sqrt(total_gate)
    factor_up = jnp.sqrt(total_up)
    narrow_gate, narrow_up = (
        (fresh_gate / factor_gate).astype(jnp.bfloat16),
        (fresh_up / factor_up).astype(jnp.bfloat16),
    )
    serve_gate, serve_up = (
        lax.all_gather(narrow_gate, "shard", axis=0, tiled=True),
        lax.all_gather(narrow_up, "shard", axis=0, tiled=True),
    )
    serve_norm = lax.all_gather(
        (norm_train + norm_step).astype(jnp.bfloat16), ("shard", "tp"), axis=0, tiled=True
    )
    return (serve_gate, serve_up, factor_gate, factor_up, serve_norm)


def solution(mesh):
    return jax.shard_map(
        shards,
        mesh=mesh,
        in_specs=(
            P("shard", "tp"),
            P("shard", "tp"),
            P("shard", "tp"),
            P("shard", "tp"),
            P("shard"),
            P(("shard", "tp")),
            P(("shard", "tp")),
        ),
        out_specs=(P(None, "tp"), P(None, "tp"), P("tp"), P("tp"), P()),
        check_vma=False,
    )
```

profile of v0, /device:TPU:0, one launch (start us, length us, event | category | flops | bytes accessed | tf_op | source)
XLA Modules:
  0.0 329.1 jit_solution(13324231435357254434)
XLA Ops:
  7.2 0.0 all-gather.3.cloned.1.call-start
  7.2 0.7 broadcast_subtract_fusion
  7.9 0.0 copy-start
  7.9 0.0 copy-start.3
  7.9 4.8 %multiply_reduce_fusion = (f32[2048]{0:T(1024)S(1)}, f32[2048]{0:T(1024)S(1)}) fusion(f32[256,2048]{1,0:T(8,128)} %param.10, f32[256]{0:T(256)S(1)} %broadcast_subtract_fusion, f32[256,2048]{1,0:T(8,128)} %param.9, f32[256]{0:T(256)} %param.11, f32[256,2048]{1,0:T(8,128)} %param.8, f32[256,2048]{1,0:T(8,128)} %param.7), kind=kLoop, calls=%fused_computation.1 | loop fusion | flops 5238784 | bytes 8407040 | tf_op jit(solution)/shard_map/reduce_sum | solution.py:11
  12.7 38.8 %all-reduce.1 = (f32[2048]{0:T(1024)S(1)}, f32[2048]{0:T(1024)S(1)}) all-reduce(f32[2048]{0:T(1024)S(1)} %get-tuple-element.6, f32[2048]{0:T(1024)S(1)} %get-tuple-element.5), channel_id=1, replica_groups=mesh['shard'=8,'tp'=4] {'shard'}, use_global_device_ids=true, to_apply=%region_1.0 | all-reduce | flops 4096 | bytes 32768 | tf_op jit(solution)/shard_map/psum | solution.py:10
  51.5 0.0 copy-start.1
  51.5 0.0 copy-done
  51.5 0.0 copy-done.3
  51.6 0.0 copy-start.2
  51.6 5.4 %divide_convert_fusion = (bf16[256,2048]{1,0:T(8,128)(2,1)}, bf16[256,2048]{1,0:T(8,128)(2,1)}) fusion(f32[2048]{0:T(1024)S(1)} %sqrt.7, f32[256,2048]{1,0:T(8,128)S(1)} %copy-done, f32[256]{0:T(256)S(1)} %broadcast_subtract_fusion, f32[256,2048]{1,0:T(8,128)} %param.9, f32[256]{0:T(256)S(1)} %copy-done.3, f32[2048]{0:T(1024)S(1)} %sqrt.6, ...), kind=kLoop, calls=%fused_computation | loop fusion | flops 5242880 | bytes 10504192 | tf_op jit(solution)/shard_map/convert_element_type | solution.py:17
  56.9 0.0 copy-done.1
  56.9 0.0 copy-done.2
  56.9 0.0 copy-start.4
  56.9 0.0 copy-start.5
  56.9 0.0 all-gather.3.cloned.1.call-update
  57.0 0.0 all-gather.5.cloned.1.call-start
  57.0 0.7 all-gather.5.cloned.1.call-update
  57.7 0.0 copy-done.4
  57.7 0.0 copy-done.5
  57.8 0.2 dynamic-update-slice
  58.0 41.0 %all-reduce = bf16[2048]{0:T(1024)(128)(2,1)} all-reduce(bf16[2048]{0:T(1024)(128)(2,1)S(1)} %dynamic-update-slice), channel_id=1, replica_groups=mesh['shard'=8,'tp'=4] {'shard','tp'}, use_global_device_ids=true, to_apply=%add | all-reduce | flops 2048 | bytes 8192
  99.0 81.0 %all-gather.3.cloned.1.call-done = bf16[2048,2048]{1,0:T(8,128)(2,1)} async-done(((bf16[256,2048]{1,0:T(8,128)(2,1)}), bf16[2048,2048]{1,0:T(8,128)(2,1)}) %all-gather.3.cloned.1.call-update) | async-done | bytes 8388624 | tf_op jit(solution)/shard_map/all_gather | solution.py:20
  180.0 125.4 %all-gather.5.cloned.1.call-done = bf16[2048,2048]{1,0:T(8,128)(2,1)} async-done(((bf16[256,2048]{1,0:T(8,128)(2,1)}), bf16[2048,2048]{1,0:T(8,128)(2,1)}) %all-gather.5.cloned.1.call-update) | async-done | bytes 8388624 | tf_op jit(solution)/shard_map/all_gather | solution.py:21
  305.3 8.4 %copy.15 = bf16[2048,2048]{1,0:T(8,128)(2,1)} copy(bf16[2048,2048]{1,0:T(8,128)(2,1)} %all-gather.3.cloned.1.call-done) | data formatting | bytes 16777216
  313.8 8.4 %copy.16 = bf16[2048,2048]{1,0:T(8,128)(2,1)} copy(bf16[2048,2048]{1,0:T(8,128)(2,1)} %all-gather.5.cloned.1.call-done) | data formatting | bytes 16777216
  (4 shorter events, 0.0 us)
Async XLA Ops:
  7.2 172.8 %all-gather.3.cloned.1.call-start = ((), (), s32[]{:S(2)}) async-start(), calls=%async_computation | async-start | bytes 9437184 | tf_op jit(solution)/shard_map/all_gather | solution.py:20
  7.9 43.6 %copy-start = (f32[256,2048]{1,0:T(8,128)S(1)}, f32[256,2048]{1,0:T(8,128)}, u32[]{:S(2)}) copy-start(f32[256,2048]{1,0:T(8,128)} %param.10) | copy-start | bytes 6291460
  7.9 43.7 %copy-start.3 = (f32[256]{0:T(256)S(1)}, f32[256]{0:T(256)}, u32[]{:S(2)}) copy-start(f32[256]{0:T(256)} %param.11) | copy-start | bytes 3076
  51.5 5.4 %copy-start.1 = (f32[2048]{0:T(1024)}, f32[2048]{0:T(1024)S(1)}, u32[]{:S(2)}) copy-start(f32[2048]{0:T(1024)S(1)} %sqrt.6) | copy-start | bytes 24580
  51.6 5.4 %copy-start.2 = (f32[2048]{0:T(1024)}, f32[2048]{0:T(1024)S(1)}, u32[]{:S(2)}) copy-start(f32[2048]{0:T(1024)S(1)} %sqrt.7) | copy-start | bytes 24580
  56.9 0.8 copy-start.4
  56.9 0.8 copy-start.5
  57.0 248.4 %all-gather.5.cloned.1.call-start = ((), (), s32[]{:S(2)}) async-start(), calls=%async_computation.1 | async-start | bytes 9437184 | tf_op jit(solution)/shard_map/all_gather | solution.py:21
Sparse Core Ops, SparseCore 0:
  57.1 122.8 all-gather.2
  182.7 122.6 all-gather.4
where the time goes:
time: 329 us
  waiting for transfers between devices  207 us (63%)
  blocking collectives  79.8 us (24%)
  local copies, waits for them, and re-layouts  17.2 us (5%)
  between operations  14.1 us (4%)
  other arithmetic  10.8 us (3%)
    all_gather x1, waiting for transfers between devices, shards(): lax.all_gather(narrow_up, 'shard', axis=0, tiled=True)  125 us
    all_gather x1, waiting for transfers between devices, shards(): lax.all_gather(narrow_gate, 'shard', axis=0, tiled=True)  81 us
    unnamed x1, blocking collectives  41 us
    psum x1, blocking collectives, shards(): lax.psum((jnp.sum(fresh_gate * fresh_gate, axis=0), jnp.sum(fresh_up * fr...  38.8 us
    unnamed x16, local copies, waits for them, and re-layouts  17.2 us
  transfers between devices with their start and end apart: 2, of which 2 were waited for; matrix products, arithmetic and copies ran while one was open for 0% of the time, Pallas kernels for 0%

commit v1 on v0

v1 whole, which is shorter than its diff:
```python
import functools

import jax
import jax.numpy as jnp
from jax import lax
from jax.experimental import pallas as pl
from jax.experimental.pallas import tpu as pltpu
from jax.sharding import PartitionSpec as P

WHOLE = pl.BlockSpec(memory_space=pltpu.VMEM)
OUTSIDE = pl.BlockSpec(memory_space=pl.ANY)
SCALARS = pl.BlockSpec(memory_space=pltpu.SMEM)


def grant(mib):
    return pltpu.CompilerParams(vmem_limit_bytes=mib << 20)


def ring_order(n):
    return list(range(0, n, 2)) + list(range(1, n, 2))[::-1]


def ring_neighbour(shard, distance, n):
    place = lax.rem(jnp.where(lax.rem(shard, 2) == 0, shard // 2, n - 1 - shard // 2) + distance + n, n)
    return jnp.where(place < n - n // 2, 2 * place, 2 * (n - 1 - place) + 1)


def cuts(rows):
    if rows < 256:
        return [(0, rows)]
    edges = [0, 5 * rows // 8, rows]
    return list(zip(edges[:-1], edges[1:]))


def sums_kernel(pieces, share, one_g, other_g, one_u, other_u, fresh_g, fresh_u, sums, held, shares, sems, share_sem):
    rows, cols = fresh_g.shape
    tall = rows // pieces
    sources = (one_g, other_g, one_u, other_u)

    def copy(k, p):
        span = pl.ds(p * tall, tall)
        return pltpu.make_async_copy(sources[k].at[span], held.at[k, span], sems.at[k, p])

    first = pltpu.make_async_copy(share, shares, share_sem)
    first.start()
    for p in range(pieces):
        for k in range(4):
            copy(k, p).start()
    first.wait()
    row = lax.broadcasted_iota(jnp.int32, (rows, rows), 0)
    lane = lax.broadcasted_iota(jnp.int32, (rows, rows), 1)
    mix = jnp.sum(jnp.where(row == lane, shares[...], 0.0), axis=1, keepdims=True)
    rest = 1.0 - mix
    total = [jnp.zeros((8, cols), jnp.float32) for _ in range(2)]
    for p in range(pieces):
        for k in range(4):
            copy(k, p).wait()
        for r in range(p * tall, (p + 1) * tall, 8):
            m, w = mix[r:r + 8], rest[r:r + 8]
            for side, fresh in ((0, fresh_g), (1, fresh_u)):
                value = m * held[2 * side, r:r + 8] + w * held[2 * side + 1, r:r + 8]
                fresh[r:r + 8] = value
                total[side] = total[side] + value * value
    sums[0:1] = jnp.sum(total[0], axis=0, keepdims=True)
    sums[1:2] = jnp.sum(total[1], axis=0, keepdims=True)


def sums_of(share, one_gate, other_gate, one_up, other_up):
    rows, cols = one_gate.shape
    pieces = max(1, rows // 32)
    wide = jax.ShapeDtypeStruct((rows, cols), jnp.float32)
    return pl.pallas_call(
        functools.partial(sums_kernel, pieces),
        in_specs=[OUTSIDE] * 5,
        out_specs=[WHOLE] * 3,
        out_shape=[wide, wide, jax.ShapeDtypeStruct((2, cols), jnp.float32)],
        scratch_shapes=[
            pltpu.VMEM((4, rows, cols), jnp.float32),
            pltpu.VMEM(share.shape, jnp.float32),
            pltpu.SemaphoreType.DMA((4, pieces)),
            pltpu.SemaphoreType.DMA,
        ],
        compiler_params=grant(48),
        name="sums",
    )(share, one_gate, other_gate, one_up, other_up)


def narrow_kernel(spans, fresh_g, fresh_u, total_ref, factor_g, factor_u, *outs):
    for side, fresh, factor in ((0, fresh_g, factor_g), (1, fresh_u, factor_u)):
        factor[...] = jnp.sqrt(total_ref[side:side + 1])
        scale = 1.0 / factor[...]
        for (lo, hi), out in zip(spans, outs[side * len(spans):]):
            for r in range(lo, hi, 16):
                out[r - lo:r - lo + 16] = (fresh[r:r + 16] * scale).astype(jnp.bfloat16)


def narrow(spans, fresh_gate, fresh_up, total):
    cols = fresh_gate.shape[1]
    factor = jax.ShapeDtypeStruct((1, cols), jnp.float32)
    shapes = [jax.ShapeDtypeStruct((hi - lo, cols), jnp.bfloat16) for lo, hi in spans]
    factor_gate, factor_up, *pieces = pl.pallas_call(
        functools.partial(narrow_kernel, spans),
        in_specs=[WHOLE] * 3,
        out_specs=[WHOLE] * (2 + 2 * len(spans)),
        out_shape=[factor] * 2 + shapes * 2,
        compiler_params=grant(16),
        name="narrow",
    )(fresh_gate, fresh_up, total)
    return factor_gate, factor_up, pieces[:len(spans)], pieces[len(spans):]


def run(copies):
    for copy in copies:
        copy.start()
    for copy in copies:
        copy.wait()


def start_kernel(spans, shard_ref, *refs):
    count = len(spans)
    outs, sems = refs[2 * count:2 * count + 2], refs[-1]
    first = pl.multiple_of(shard_ref[0] * spans[-1][1], 16)
    run([
        pltpu.make_async_copy(refs[side * count + c], outs[side].at[pl.ds(first + lo, hi - lo)], sems.at[side, c])
        for side in range(2)
        for c, (lo, hi) in enumerate(spans)
    ])


def start_outputs(shard, spans, gate, up, n):
    shape = jax.ShapeDtypeStruct((n * spans[-1][1], gate[0].shape[1]), jnp.bfloat16)
    return pl.pallas_call(
        functools.partial(start_kernel, spans),
        in_specs=[SCALARS] + [WHOLE] * (2 * len(spans)),
        out_specs=[OUTSIDE] * 2,
        out_shape=[shape, shape],
        scratch_shapes=[pltpu.SemaphoreType.DMA((2, len(spans)))],
        compiler_params=grant(4),
        name="start_outputs",
    )(shard, *gate, *up)


def put_kernel(step, lo, rows, n, shard_ref, gate, up, _, __, out_g, out_u, sems):
    copies = []
    for side, (part, out, back) in enumerate(((gate, out_g, -step), (up, out_u, step))):
        first = pl.multiple_of(ring_neighbour(shard_ref[0], back, n) * rows, 16)
        copies.append(pltpu.make_async_copy(part, out.at[pl.ds(first + lo, part.shape[0])], sems.at[side]))
    run(copies)


def put(shard, step, lo, rows, n, gate, up, outs):
    return pl.pallas_call(
        functools.partial(put_kernel, step, lo, rows, n),
        in_specs=[SCALARS, WHOLE, WHOLE, OUTSIDE, OUTSIDE],
        out_specs=[OUTSIDE] * 2,
        out_shape=[jax.ShapeDtypeStruct(out.shape, out.dtype) for out in outs],
        scratch_shapes=[pltpu.SemaphoreType.DMA((2,))],
        input_output_aliases={3: 0, 4: 1},
        compiler_params=grant(4),
        name="put",
    )(shard, gate, up, *outs)


def add_kernel(count, *refs):
    terms = [ref[...] for ref in refs[:count]]
    while len(terms) > 1:
        terms = [terms[i] + terms[i + 1] for i in range(0, len(terms), 2)]
    refs[-1][...] = terms[0].astype(refs[-1].dtype)


def tree_add(terms, after, kind=jnp.float32):
    return pl.pallas_call(
        functools.partial(add_kernel, len(terms)),
        in_specs=[WHOLE] * len(terms) + [OUTSIDE] * len(after),
        out_specs=WHOLE,
        out_shape=jax.ShapeDtypeStruct(terms[0].shape, kind),
        compiler_params=grant(2),
        name="tree_add",
    )(*terms, *after)


def slot_kernel(count, index_ref, train, step, out):
    value = (train[...] + step[...]).astype(jnp.bfloat16).astype(jnp.float32)
    width = value.shape[1]
    value = jnp.concatenate([value] * count, axis=1)
    slot = lax.broadcasted_iota(jnp.int32, value.shape, 1) // width
    out[...] = jnp.where(slot == index_ref[0], value, 0.0)


def slot_of(index, train, step, count):
    return pl.pallas_call(
        functools.partial(slot_kernel, count),
        in_specs=[SCALARS, WHOLE, WHOLE],
        out_specs=WHOLE,
        out_shape=jax.ShapeDtypeStruct((1, count * train.shape[1]), jnp.float32),
        compiler_params=grant(2),
        name="slot",
    )(index, train, step)


def stages_of(n, most):
    bits = [1 << b for b in range(n.bit_length() - 1)]
    stages, bits = [bits[:1]], bits[1:]
    while bits:
        stages.append(bits[:most])
        bits = bits[most:]
    spans = []
    for stage in stages:
        masks = [0]
        for bit in stage:
            masks += [mask + bit for mask in masks]
        spans.append(masks[1:])
    return spans


def exchange(value, axis, n, masks, after=(), kind=jnp.float32):
    others = [lax.ppermute(value, axis, [(i, i ^ m) for i in range(n)]) for m in masks]
    return tree_add([value] + others, after, kind)


def shards(mesh, one_gate, other_gate, one_up, other_up, mix_share, norm_train, norm_step):
    n, t = mesh.shape["shard"], mesh.shape["tp"]
    me = lax.axis_index("shard")
    shard = me[None].astype(jnp.int32)
    device = shard * t + lax.axis_index("tp").astype(jnp.int32)
    rows, _ = one_gate.shape
    order = ring_order(n)
    forward = [(order[i], order[(i + 1) % n]) for i in range(n)]
    backward = [(b, a) for a, b in forward]
    spans = cuts(rows)
    fresh_gate, fresh_up, total = sums_of(mix_share[None], one_gate, other_gate, one_up, other_up)
    for masks in stages_of(n, 2):
        total = exchange(total, "shard", n, masks)
    factor_gate, factor_up, gate, up = narrow(spans, fresh_gate, fresh_up, total)
    outs = start_outputs(shard, spans, gate, up, n)
    norm = slot_of(device, norm_train[None], norm_step[None], n * t)
    left = [("tp", t, masks) for masks in stages_of(t, 1)] + [("shard", n, masks) for masks in stages_of(n, 1)]
    stage = 0
    for step in range(1, n):
        for c, (lo, hi) in enumerate(spans):
            gate[c] = lax.ppermute(gate[c], "shard", forward)
            up[c] = lax.ppermute(up[c], "shard", backward)
            outs = put(shard, step, lo, rows, n, gate[c], up[c], outs)
        if step > 1 and stage < len(left):
            norm = exchange(norm, *left[stage], (gate[0],))
            stage += 1
    for axis, size, masks in left[stage:]:
        norm = exchange(norm, axis, size, masks)
    serve_norm = norm[0].astype(jnp.bfloat16)
    return (outs[0], outs[1], factor_gate[0], factor_up[0], serve_norm)


def solution(mesh):
    def layer(*args):
        return shards(mesh, *args)

    return jax.shard_map(
        layer,
        mesh=mesh,
        in_specs=(
            P("shard", "tp"),
            P("shard", "tp"),
            P("shard", "tp"),
            P("shard", "tp"),
            P("shard"),
            P(("shard", "tp")),
            P(("shard", "tp")),
        ),
        out_specs=(P(None, "tp"), P(None, "tp"), P("tp"), P("tp"), P()),
        check_vma=False,
    )
```

time: 329 us -> 215 us (0.65)
  waiting for transfers between devices: 207 us -> 120 us
  blocking collectives: 79.8 us -> 0 us
  starting transfers between devices: 0.08 us -> 40.5 us
  Pallas kernels: 0 us -> 24.3 us
  between operations: 14.1 us -> 0.91 us
  local copies, waits for them, and re-layouts: 17.2 us -> 27.4 us
  other arithmetic: 10.8 us -> 0.62 us
    all_gather x2 -> x0, waiting for transfers between devices: 206 us -> none  [the longest x1 125 us: shards(): lax.all_gather(narrow_up, 'shard', axis=0, tiled=True)]
    ppermute x0 -> x37, waiting for transfers between devices: none -> 120 us  [the longest x14 96.7 us: shards(): gate[c] = lax.ppermute(gate[c], 'shard', forward)]
    unnamed x1 -> x0, blocking collectives: 41 us -> none
    ppermute x0 -> x37, starting transfers between devices: none -> 40.5 us  [the longest x14 28.3 us: shards(): up[c] = lax.ppermute(up[c], 'shard', backward)]
    psum x1 -> x0, blocking collectives: 38.8 us -> none  [shards(): lax.psum((jnp.sum(fresh_gate * fresh_gate, axis=0), jnp.sum(fresh_up * fr...]
    pallas_call x0 -> x25, Pallas kernels: none -> 24.3 us  [the longest x14 18.3 us: put(): pl.pallas_call(functools.partial(put_kernel, step, lo, rows, n), in_specs...]
    unnamed x16 -> x86, local copies, waits for them, and re-layouts: 17.2 us -> 27.4 us
    reduce_sum x1 -> x0, other arithmetic: 4.76 us -> none  [shards(): jnp.sum(fresh_up * fresh_up, axis=0)]
  transfers between devices with their start and end apart: 2 -> 37, of which waited for: 2 -> 24; matrix products, arithmetic and copies ran while one was open for 0% -> 0% of each run, Pallas kernels for 0% -> 8%
where the time goes in v1:
time: 215 us; the launch traced here: 214 us
  waiting for transfers between devices  120 us (56%)
  starting transfers between devices  40.5 us (19%)
  local copies, waits for them, and re-layouts  27.4 us (13%)
  Pallas kernels  24.3 us (11%)
    ppermute x14, waiting for transfers between devices, shards(): gate[c] = lax.ppermute(gate[c], 'shard', forward)  96.7 us
    ppermute x14, starting transfers between devices, shards(): up[c] = lax.ppermute(up[c], 'shard', backward)  28.3 us
    unnamed x86, local copies, waits for them, and re-layouts  27.4 us
    ppermute x9, waiting for transfers between devices, exchange(): lax.ppermute(value, axis, [(i, i ^ m) for i in range(n)])  20.1 us
    pallas_call x14, Pallas kernels, put(): pl.pallas_call(functools.partial(put_kernel, step, lo, rows, n), in_specs...  18.3 us
    ppermute x9, starting transfers between devices, exchange(): lax.ppermute(value, axis, [(i, i ^ m) for i in range(n)])  12.1 us
  transfers between devices with their start and end apart: 37, of which 24 were waited for; matrix products, arithmetic and copies ran while one was open for 0% of the time, Pallas kernels for 8%

profile of v1, /device:TPU:0, one launch (start us, length us, event | category | flops | bytes accessed | tf_op | source)
XLA Modules:
  0.0 214.1 jit_solution(16948638370610790244)
XLA Ops:
  1.3 3.8 %sums.1 = (f32[256,2048]{1,0:T(8,128)S(1)}, f32[256,2048]{1,0:T(8,128)S(1)}, f32[2,2048]{1,0:T(2,128)S(1)}) custom-call(f32[1,256]{1,0:T(1,128)S(1)} %bitcast.7, f32[256,2048]{1,0:T(8,128)} %one_g.1, f32[256,2048]{1,0:T(8,128)} %other_g.1, f32[256,2048]{1,0:T(8,128)} %one_u.1, f32[256,2048]{1,0:T(8,128)} %other_u.1), custom_call_target="tpu_custom_call" | custom-call | tf_op jit(solution)/shard_map/sums/pallas_call | solution.py:72
  5.1 3.0 %collective-permute-start = (f32[2,2048]{1,0:T(2,128)S(1)}, f32[2,2048]{1,0:T(2,128)S(1)}, u32[]{:S(2)}, u32[]{:S(2)}) collective-permute-start(f32[2,2048]{1,0:T(2,128)S(1)} %get-tuple-element.46.refs_0_), channel_id=1, source_target_pairs={{0,4},{4,0},{8,12},{12,8},{16,20},{20,16},{24,28},{28,24},{1,5},{5... | collective-permute-start | bytes 49160 | tf_op jit(solution)/shard_map/ppermute | solution.py:217
  8.2 1.7 collective-permute-done.refs_1_
  9.9 2.1 collective-permute-start.1
  12.0 2.6 %collective-permute-start.2 = (f32[2,2048]{1,0:T(2,128)S(1)}, f32[2,2048]{1,0:T(2,128)S(1)}, u32[]{:S(2)}, u32[]{:S(2)}) collective-permute-start(f32[2,2048]{1,0:T(2,128)S(1)} %tree_add.7.refs_0_), channel_id=1, source_target_pairs={{0,16},{4,20},{8,24},{12,28},{16,0},{20,4},{24,8},{28,12},{1,17},{... | collective-permute-start | bytes 49160 | tf_op jit(solution)/shard_map/ppermute | solution.py:217
  14.6 2.0 collective-permute-done.2.refs_2_
  16.6 3.5 %collective-permute-done.3.refs_3_ = f32[2,2048]{1,0:T(2,128)S(1)} collective-permute-done((f32[2,2048]{1,0:T(2,128)S(1)}, f32[2,2048]{1,0:T(2,128)S(1)}, u32[]{:S(2)}, u32[]{:S(2)}) %collective-permute-start.3) | collective-permute-done | bytes 16416 | tf_op jit(solution)/shard_map/ppermute | solution.py:217
  21.7 2.0 collective-permute-start.25
  24.6 11.2 %collective-permute-done.18.gate = bf16[160,2048]{1,0:T(8,128)(2,1)S(1)} collective-permute-done((bf16[160,2048]{1,0:T(8,128)(2,1)S(1)}, bf16[160,2048]{1,0:T(8,128)(2,1)S(1)}, u32[]{:S(2)}, u32[]{:S(2)}) %collective-permute-start.18) | collective-permute-done | bytes 655392 | tf_op jit(solution)/shard_map/ppermute | solution.py:241
  36.6 2.0 collective-permute-start.26
  38.6 0.9 copy-done.10
  39.5 11.2 %collective-permute-done.19.gate.refs_2_ = bf16[160,2048]{1,0:T(8,128)(2,1)S(1)} collective-permute-done((bf16[160,2048]{1,0:T(8,128)(2,1)S(1)}, bf16[160,2048]{1,0:T(8,128)(2,1)S(1)}, u32[]{:S(2)}, u32[]{:S(2)}) %collective-permute-start.19) | collective-permute-done | bytes 655392 | tf_op jit(solution)/shard_map/ppermute | solution.py:241
  50.7 0.9 collective-permute-done.26.up
  51.5 2.0 collective-permute-start.27
  55.2 2.0 collective-permute-start.11
  58.0 10.3 %collective-permute-done.20.gate.refs_2_ = bf16[160,2048]{1,0:T(8,128)(2,1)S(1)} collective-permute-done((bf16[160,2048]{1,0:T(8,128)(2,1)S(1)}, bf16[160,2048]{1,0:T(8,128)(2,1)S(1)}, u32[]{:S(2)}, u32[]{:S(2)}) %collective-permute-start.20) | collective-permute-done | bytes 655392 | tf_op jit(solution)/shard_map/ppermute | solution.py:241
  68.3 0.9 collective-permute-done.27.up
  69.1 2.0 collective-permute-start.28
  72.0 4.7 %collective-permute-done.4.gate = bf16[96,2048]{1,0:T(8,128)(2,1)S(1)} collective-permute-done((bf16[96,2048]{1,0:T(8,128)(2,1)S(1)}, bf16[96,2048]{1,0:T(8,128)(2,1)S(1)}, u32[]{:S(2)}, u32[]{:S(2)}) %collective-permute-start.4) | collective-permute-done | bytes 393248 | tf_op jit(solution)/shard_map/ppermute | solution.py:241
  77.6 2.0 collective-permute-start.12
  80.3 10.4 %collective-permute-done.21.gate.refs_2_ = bf16[160,2048]{1,0:T(8,128)(2,1)S(1)} collective-permute-done((bf16[160,2048]{1,0:T(8,128)(2,1)S(1)}, bf16[160,2048]{1,0:T(8,128)(2,1)S(1)}, u32[]{:S(2)}, u32[]{:S(2)}) %collective-permute-start.21) | collective-permute-done | bytes 655392 | tf_op jit(solution)/shard_map/ppermute | solution.py:241
  90.7 0.9 collective-permute-done.28.up
  91.6 2.0 collective-permute-start.29
  94.5 4.7 %collective-permute-done.5.gate = bf16[96,2048]{1,0:T(8,128)(2,1)S(1)} collective-permute-done((bf16[96,2048]{1,0:T(8,128)(2,1)S(1)}, bf16[96,2048]{1,0:T(8,128)(2,1)S(1)}, u32[]{:S(2)}, u32[]{:S(2)}) %collective-permute-start.5) | collective-permute-done | bytes 393248 | tf_op jit(solution)/shard_map/ppermute | solution.py:241
  100.0 2.0 collective-permute-start.13
  102.8 16.1 %collective-permute-done.6.gate = bf16[96,2048]{1,0:T(8,128)(2,1)S(1)} collective-permute-done((bf16[96,2048]{1,0:T(8,128)(2,1)S(1)}, bf16[96,2048]{1,0:T(8,128)(2,1)S(1)}, u32[]{:S(2)}, u32[]{:S(2)}) %collective-permute-start.6) | collective-permute-done | bytes 393248 | tf_op jit(solution)/shard_map/ppermute | solution.py:241
  119.7 2.0 collective-permute-start.14
  122.5 2.0 collective-permute-start.30
  124.5 0.9 copy-done.14
  125.4 5.5 %collective-permute-done.7.gate = bf16[96,2048]{1,0:T(8,128)(2,1)S(1)} collective-permute-done((bf16[96,2048]{1,0:T(8,128)(2,1)S(1)}, bf16[96,2048]{1,0:T(8,128)(2,1)S(1)}, u32[]{:S(2)}, u32[]{:S(2)}) %collective-permute-start.7) | collective-permute-done | bytes 393248 | tf_op jit(solution)/shard_map/ppermute | solution.py:241
  131.7 2.0 collective-permute-start.15
  134.5 16.1 %collective-permute-done.8.gate = bf16[96,2048]{1,0:T(8,128)(2,1)S(1)} collective-permute-done((bf16[96,2048]{1,0:T(8,128)(2,1)S(1)}, bf16[96,2048]{1,0:T(8,128)(2,1)S(1)}, u32[]{:S(2)}, u32[]{:S(2)}) %collective-permute-start.8) | collective-permute-done | bytes 393248 | tf_op jit(solution)/shard_map/ppermute | solution.py:241
  151.3 2.0 collective-permute-start.16
  154.1 2.0 collective-permute-start.31
  156.2 6.5 %collective-permute-done.9.gate = bf16[96,2048]{1,0:T(8,128)(2,1)} collective-permute-done((bf16[96,2048]{1,0:T(8,128)(2,1)S(1)}, bf16[96,2048]{1,0:T(8,128)(2,1)}, u32[]{:S(2)}, u32[]{:S(2)}) %collective-permute-start.9) | collective-permute-done | bytes 393248 | tf_op jit(solution)/shard_map/ppermute | solution.py:241
  163.4 2.0 collective-permute-start.17
  165.6 1.2 collective-permute-done.32.refs_1_
  166.8 1.5 collective-permute-start.33
  168.3 2.1 collective-permute-done.33.refs_1_
  170.4 1.7 collective-permute-start.34
  172.1 5.9 %collective-permute-done.34.refs_1_ = f32[1,2048]{1,0:T(1,128)S(1)} collective-permute-done((f32[1,2048]{1,0:T(1,128)S(1)}, f32[1,2048]{1,0:T(1,128)S(1)}, u32[]{:S(2)}, u32[]{:S(2)}) %collective-permute-start.34) | collective-permute-done | bytes 8224 | tf_op jit(solution)/shard_map/ppermute | solution.py:217
  178.0 3.6 %collective-permute-done.35.refs_1_ = f32[1,2048]{1,0:T(1,128)S(1)} collective-permute-done((f32[1,2048]{1,0:T(1,128)S(1)}, f32[1,2048]{1,0:T(1,128)S(1)}, u32[]{:S(2)}, u32[]{:S(2)}) %collective-permute-start.35) | collective-permute-done | bytes 8224 | tf_op jit(solution)/shard_map/ppermute | solution.py:217
  181.7 1.1 collective-permute-start.36
  182.8 1.1 copy-done.1
  183.9 1.1 copy-done.3
  185.0 1.0 copy-done.17
  186.0 1.0 copy-done.19
  187.0 1.3 start_outputs.1
  188.4 1.1 copy-done.7
  189.4 1.1 copy-done.11
  190.5 1.1 put.14
  192.1 0.9 put.15
  193.5 1.1 put.16
  195.1 0.9 put.17
  196.4 1.1 put.18
  198.0 0.9 put.19
  199.4 1.1 put.20
  201.0 0.9 put.21
  202.4 1.1 put.22
  203.9 0.9 put.23
  204.9 2.2 %put.24 = (bf16[2048,2048]{1,0:T(8,128)(2,1)}, bf16[2048,2048]{1,0:T(8,128)(2,1)}) custom-call(s32[1]{0:T(128)} %bitcast.shard_ref, bf16[160,2048]{1,0:T(8,128)(2,1)S(1)} %collective-permute-done.23.gate.refs_2_, bf16[160,2048]{1,0:T(8,128)(2,1)} %collective-permute-done.30.up, ...), custom_call_target="tpu_custom_call", output_to_operand_aliasing={{0}: (3, {}), {1}: (4, {})} | custom-call | tf_op jit(solution)/shard_map/put/pallas_call | solution.py:152
  207.0 2.0 put.25
  209.7 2.4 %put.26 = (bf16[2048,2048]{1,0:T(8,128)(2,1)}, bf16[2048,2048]{1,0:T(8,128)(2,1)}) custom-call(s32[1]{0:T(128)} %bitcast.shard_ref, bf16[160,2048]{1,0:T(8,128)(2,1)} %collective-permute-done.24.gate, bf16[160,2048]{1,0:T(8,128)(2,1)} %collective-permute-done.31.up, ...), custom_call_target="tpu_custom_call", output_to_operand_aliasing={{0}: (3, {}), {1}: (4, {})} | custom-call | tf_op jit(solution)/shard_map/put/pallas_call | solution.py:152
  212.1 2.0 put.27
  (122 shorter events, 22.0 us)
Async XLA Ops:
  0.6 164.8 %copy-start.41 = (f32[64]{0:T(128)S(1)}, f32[64]{0:T(128)}, u32[]{:S(2)}) copy-start(f32[64]{0:T(128)} %param.12) | copy-start | bytes 772
  0.6 164.8 %copy-start.42 = (f32[64]{0:T(128)S(1)}, f32[64]{0:T(128)}, u32[]{:S(2)}) copy-start(f32[64]{0:T(128)} %param.13) | copy-start | bytes 772
  5.1 4.8 %collective-permute-start = (f32[2,2048]{1,0:T(2,128)S(1)}, f32[2,2048]{1,0:T(2,128)S(1)}, u32[]{:S(2)}, u32[]{:S(2)}) collective-permute-start(f32[2,2048]{1,0:T(2,128)S(1)} %get-tuple-element.46.refs_0_), channel_id=1, source_target_pairs={{0,4},{4,0},{8,12},{12,8},{16,20},{20,16},{24,28},{28,24},{1,5},{5... | collective-permute-start | bytes 49160 | tf_op jit(solution)/shard_map/ppermute | solution.py:217
  9.9 4.7 %collective-permute-start.1 = (f32[2,2048]{1,0:T(2,128)S(1)}, f32[2,2048]{1,0:T(2,128)S(1)}, u32[]{:S(2)}, u32[]{:S(2)}) collective-permute-start(f32[2,2048]{1,0:T(2,128)S(1)} %tree_add.7.refs_0_), channel_id=1, source_target_pairs={{0,8},{4,12},{8,0},{12,4},{16,24},{20,28},{24,16},{28,20},{1,9},{5... | collective-permute-start | bytes 49160 | tf_op jit(solution)/shard_map/ppermute | solution.py:217
  12.0 4.6 %collective-permute-start.2 = (f32[2,2048]{1,0:T(2,128)S(1)}, f32[2,2048]{1,0:T(2,128)S(1)}, u32[]{:S(2)}, u32[]{:S(2)}) collective-permute-start(f32[2,2048]{1,0:T(2,128)S(1)} %tree_add.7.refs_0_), channel_id=1, source_target_pairs={{0,16},{4,20},{8,24},{12,28},{16,0},{20,4},{24,8},{28,12},{1,17},{... | collective-permute-start | bytes 49160 | tf_op jit(solution)/shard_map/ppermute | solution.py:217
  14.6 5.5 %collective-permute-start.3 = (f32[2,2048]{1,0:T(2,128)S(1)}, f32[2,2048]{1,0:T(2,128)S(1)}, u32[]{:S(2)}, u32[]{:S(2)}) collective-permute-start(f32[2,2048]{1,0:T(2,128)S(1)} %tree_add.7.refs_0_), channel_id=1, source_target_pairs={{0,24},{4,28},{8,16},{12,20},{16,8},{20,12},{24,0},{28,4},{1,25},{... | collective-permute-start | bytes 49160 | tf_op jit(solution)/shard_map/ppermute | solution.py:217
  20.9 14.9 %collective-permute-start.18 = (bf16[160,2048]{1,0:T(8,128)(2,1)S(1)}, bf16[160,2048]{1,0:T(8,128)(2,1)S(1)}, u32[]{:S(2)}, u32[]{:S(2)}) collective-permute-start(bf16[160,2048]{1,0:T(8,128)(2,1)S(1)} %get-tuple-element.49.refs_0_), channel_id=1, source_target_pairs={{0,8},{8,16},{16,24},{24,28},{28,20},{20,12},{12,4},{4,0},{1,9},{9... | collective-permute-start | bytes 1966088 | tf_op jit(solution)/shard_map/ppermute | solution.py:241
  21.7 14.9 %collective-permute-start.25 = (bf16[160,2048]{1,0:T(8,128)(2,1)S(1)}, bf16[160,2048]{1,0:T(8,128)(2,1)S(1)}, u32[]{:S(2)}, u32[]{:S(2)}) collective-permute-start(bf16[160,2048]{1,0:T(8,128)(2,1)S(1)} %get-tuple-element.50.refs_2_), channel_id=1, source_target_pairs={{8,0},{16,8},{24,16},{28,24},{20,28},{12,20},{4,12},{0,4},{9,1},{1... | collective-permute-start | bytes 1966088 | tf_op jit(solution)/shard_map/ppermute | solution.py:242
  35.8 14.9 %collective-permute-start.19 = (bf16[160,2048]{1,0:T(8,128)(2,1)S(1)}, bf16[160,2048]{1,0:T(8,128)(2,1)S(1)}, u32[]{:S(2)}, u32[]{:S(2)}) collective-permute-start(bf16[160,2048]{1,0:T(8,128)(2,1)S(1)} %collective-permute-done.18.gate), channel_id=1, source_target_pairs={{0,8},{8,16},{16,24},{24,28},{28,20},{20,12},{12,4},{4,0},{1,9},{9... | collective-permute-start | bytes 1966088 | tf_op jit(solution)/shard_map/ppermute | solution.py:241
  36.6 14.9 %collective-permute-start.26 = (bf16[160,2048]{1,0:T(8,128)(2,1)S(1)}, bf16[160,2048]{1,0:T(8,128)(2,1)S(1)}, u32[]{:S(2)}, u32[]{:S(2)}) collective-permute-start(bf16[160,2048]{1,0:T(8,128)(2,1)S(1)} %collective-permute-done.25.up), channel_id=1, source_target_pairs={{8,0},{16,8},{24,16},{28,24},{20,28},{12,20},{4,12},{0,4},{9,1},{1... | collective-permute-start | bytes 1966088 | tf_op jit(solution)/shard_map/ppermute | solution.py:242
  38.6 0.9 copy-start.10
  50.7 17.6 %collective-permute-start.20 = (bf16[160,2048]{1,0:T(8,128)(2,1)S(1)}, bf16[160,2048]{1,0:T(8,128)(2,1)S(1)}, u32[]{:S(2)}, u32[]{:S(2)}) collective-permute-start(bf16[160,2048]{1,0:T(8,128)(2,1)S(1)} %collective-permute-done.19.gate.refs_2_), channel_id=1, source_target_pairs={{0,8},{8,16},{16,24},{24,28},{28,20},{20,12},{12,4},{4,0},{1,9},{9... | collective-permute-start | bytes 1966088 | tf_op jit(solution)/shard_map/ppermute | solution.py:241
  51.5 17.6 %collective-permute-start.27 = (bf16[160,2048]{1,0:T(8,128)(2,1)S(1)}, bf16[160,2048]{1,0:T(8,128)(2,1)S(1)}, u32[]{:S(2)}, u32[]{:S(2)}) collective-permute-start(bf16[160,2048]{1,0:T(8,128)(2,1)S(1)} %collective-permute-done.26.up), channel_id=1, source_target_pairs={{8,0},{16,8},{24,16},{28,24},{20,28},{12,20},{4,12},{0,4},{9,1},{1... | collective-permute-start | bytes 1966088 | tf_op jit(solution)/shard_map/ppermute | solution.py:242
  53.5 0.9 copy-start.8
  54.4 22.3 %collective-permute-start.4 = (bf16[96,2048]{1,0:T(8,128)(2,1)S(1)}, bf16[96,2048]{1,0:T(8,128)(2,1)S(1)}, u32[]{:S(2)}, u32[]{:S(2)}) collective-permute-start(bf16[96,2048]{1,0:T(8,128)(2,1)S(1)} %get-tuple-element.47.refs_1_), channel_id=1, source_target_pairs={{0,8},{8,16},{16,24},{24,28},{28,20},{20,12},{12,4},{4,0},{1,9},{9... | collective-permute-start | bytes 1179656 | tf_op jit(solution)/shard_map/ppermute | solution.py:241
  55.2 22.4 %collective-permute-start.11 = (bf16[96,2048]{1,0:T(8,128)(2,1)S(1)}, bf16[96,2048]{1,0:T(8,128)(2,1)S(1)}, u32[]{:S(2)}, u32[]{:S(2)}) collective-permute-start(bf16[96,2048]{1,0:T(8,128)(2,1)S(1)} %get-tuple-element.48.refs_3_), channel_id=1, source_target_pairs={{8,0},{16,8},{24,16},{28,24},{20,28},{12,20},{4,12},{0,4},{9,1},{1... | collective-permute-start | bytes 1179656 | tf_op jit(solution)/shard_map/ppermute | solution.py:242
  68.3 22.5 %collective-permute-start.21 = (bf16[160,2048]{1,0:T(8,128)(2,1)S(1)}, bf16[160,2048]{1,0:T(8,128)(2,1)S(1)}, u32[]{:S(2)}, u32[]{:S(2)}) collective-permute-start(bf16[160,2048]{1,0:T(8,128)(2,1)S(1)} %collective-permute-done.20.gate.refs_2_), channel_id=1, source_target_pairs={{0,8},{8,16},{16,24},{24,28},{28,20},{20,12},{12,4},{4,0},{1,9},{9... | collective-permute-start | bytes 1966088 | tf_op jit(solution)/shard_map/ppermute | solution.py:241
  69.1 22.5 %collective-permute-start.28 = (bf16[160,2048]{1,0:T(8,128)(2,1)S(1)}, bf16[160,2048]{1,0:T(8,128)(2,1)S(1)}, u32[]{:S(2)}, u32[]{:S(2)}) collective-permute-start(bf16[160,2048]{1,0:T(8,128)(2,1)S(1)} %collective-permute-done.27.up), channel_id=1, source_target_pairs={{8,0},{16,8},{24,16},{28,24},{20,28},{12,20},{4,12},{0,4},{9,1},{1... | collective-permute-start | bytes 1966088 | tf_op jit(solution)/shard_map/ppermute | solution.py:242
  71.1 0.8 copy-start.4
  76.7 22.5 %collective-permute-start.5 = (bf16[96,2048]{1,0:T(8,128)(2,1)S(1)}, bf16[96,2048]{1,0:T(8,128)(2,1)S(1)}, u32[]{:S(2)}, u32[]{:S(2)}) collective-permute-start(bf16[96,2048]{1,0:T(8,128)(2,1)S(1)} %collective-permute-done.4.gate), channel_id=1, source_target_pairs={{0,8},{8,16},{16,24},{24,28},{28,20},{20,12},{12,4},{4,0},{1,9},{9... | collective-permute-start | bytes 1179656 | tf_op jit(solution)/shard_map/ppermute | solution.py:241
  77.6 22.5 %collective-permute-start.12 = (bf16[96,2048]{1,0:T(8,128)(2,1)S(1)}, bf16[96,2048]{1,0:T(8,128)(2,1)S(1)}, u32[]{:S(2)}, u32[]{:S(2)}) collective-permute-start(bf16[96,2048]{1,0:T(8,128)(2,1)S(1)} %collective-permute-done.11.up), channel_id=1, source_target_pairs={{8,0},{16,8},{24,16},{28,24},{20,28},{12,20},{4,12},{0,4},{9,1},{1... | collective-permute-start | bytes 1179656 | tf_op jit(solution)/shard_map/ppermute | solution.py:242
  90.7 31.8 %collective-permute-start.22 = (bf16[160,2048]{1,0:T(8,128)(2,1)S(1)}, bf16[160,2048]{1,0:T(8,128)(2,1)S(1)}, u32[]{:S(2)}, u32[]{:S(2)}) collective-permute-start(bf16[160,2048]{1,0:T(8,128)(2,1)S(1)} %collective-permute-done.21.gate.refs_2_), channel_id=1, source_target_pairs={{0,8},{8,16},{16,24},{24,28},{28,20},{20,12},{12,4},{4,0},{1,9},{9... | collective-permute-start | bytes 1966088 | tf_op jit(solution)/shard_map/ppermute | solution.py:241
  91.6 30.9 %collective-permute-start.29 = (bf16[160,2048]{1,0:T(8,128)(2,1)S(1)}, bf16[160,2048]{1,0:T(8,128)(2,1)S(1)}, u32[]{:S(2)}, u32[]{:S(2)}) collective-permute-start(bf16[160,2048]{1,0:T(8,128)(2,1)S(1)} %collective-permute-done.28.up), channel_id=1, source_target_pairs={{8,0},{16,8},{24,16},{28,24},{20,28},{12,20},{4,12},{0,4},{9,1},{1... | collective-permute-start | bytes 1966088 | tf_op jit(solution)/shard_map/ppermute | solution.py:242
  93.6 0.8 copy-start.12
  99.2 19.8 %collective-permute-start.6 = (bf16[96,2048]{1,0:T(8,128)(2,1)S(1)}, bf16[96,2048]{1,0:T(8,128)(2,1)S(1)}, u32[]{:S(2)}, u32[]{:S(2)}) collective-permute-start(bf16[96,2048]{1,0:T(8,128)(2,1)S(1)} %collective-permute-done.5.gate), channel_id=1, source_target_pairs={{0,8},{8,16},{16,24},{24,28},{28,20},{20,12},{12,4},{4,0},{1,9},{9... | collective-permute-start | bytes 1179656 | tf_op jit(solution)/shard_map/ppermute | solution.py:241
  100.0 19.7 %collective-permute-start.13 = (bf16[96,2048]{1,0:T(8,128)(2,1)S(1)}, bf16[96,2048]{1,0:T(8,128)(2,1)S(1)}, u32[]{:S(2)}, u32[]{:S(2)}) collective-permute-start(bf16[96,2048]{1,0:T(8,128)(2,1)S(1)} %collective-permute-done.12.up), channel_id=1, source_target_pairs={{8,0},{16,8},{24,16},{28,24},{20,28},{12,20},{4,12},{0,4},{9,1},{1... | collective-permute-start | bytes 1179656 | tf_op jit(solution)/shard_map/ppermute | solution.py:242
  118.9 12.0 %collective-permute-start.7 = (bf16[96,2048]{1,0:T(8,128)(2,1)S(1)}, bf16[96,2048]{1,0:T(8,128)(2,1)S(1)}, u32[]{:S(2)}, u32[]{:S(2)}) collective-permute-start(bf16[96,2048]{1,0:T(8,128)(2,1)S(1)} %collective-permute-done.6.gate), channel_id=1, source_target_pairs={{0,8},{8,16},{16,24},{24,28},{28,20},{20,12},{12,4},{4,0},{1,9},{9... | collective-permute-start | bytes 1179656 | tf_op jit(solution)/shard_map/ppermute | solution.py:241
  119.7 12.0 %collective-permute-start.14 = (bf16[96,2048]{1,0:T(8,128)(2,1)S(1)}, bf16[96,2048]{1,0:T(8,128)(2,1)S(1)}, u32[]{:S(2)}, u32[]{:S(2)}) collective-permute-start(bf16[96,2048]{1,0:T(8,128)(2,1)S(1)} %collective-permute-done.13.up), channel_id=1, source_target_pairs={{8,0},{16,8},{24,16},{28,24},{20,28},{12,20},{4,12},{0,4},{9,1},{1... | collective-permute-start | bytes 1179656 | tf_op jit(solution)/shard_map/ppermute | solution.py:242
  122.5 31.6 %collective-permute-start.23 = (bf16[160,2048]{1,0:T(8,128)(2,1)S(1)}, bf16[160,2048]{1,0:T(8,128)(2,1)S(1)}, u32[]{:S(2)}, u32[]{:S(2)}) collective-permute-start(bf16[160,2048]{1,0:T(8,128)(2,1)S(1)} %collective-permute-done.22.gate.refs_2_), channel_id=1, source_target_pairs={{0,8},{8,16},{16,24},{24,28},{28,20},{20,12},{12,4},{4,0},{1,9},{9... | collective-permute-start | bytes 1966088 | tf_op jit(solution)/shard_map/ppermute | solution.py:241
  122.5 31.6 %collective-permute-start.30 = (bf16[160,2048]{1,0:T(8,128)(2,1)S(1)}, bf16[160,2048]{1,0:T(8,128)(2,1)}, u32[]{:S(2)}, u32[]{:S(2)}) collective-permute-start(bf16[160,2048]{1,0:T(8,128)(2,1)S(1)} %collective-permute-done.29.up), channel_id=1, source_target_pairs={{8,0},{16,8},{24,16},{28,24},{20,28},{12,20},{4,12},{0,4},{9,1},{1... | collective-permute-start | bytes 1966088 | tf_op jit(solution)/shard_map/ppermute | solution.py:242
  124.5 0.9 copy-start.14
  130.9 19.7 %collective-permute-start.8 = (bf16[96,2048]{1,0:T(8,128)(2,1)S(1)}, bf16[96,2048]{1,0:T(8,128)(2,1)S(1)}, u32[]{:S(2)}, u32[]{:S(2)}) collective-permute-start(bf16[96,2048]{1,0:T(8,128)(2,1)S(1)} %collective-permute-done.7.gate), channel_id=1, source_target_pairs={{0,8},{8,16},{16,24},{24,28},{28,20},{20,12},{12,4},{4,0},{1,9},{9... | collective-permute-start | bytes 1179656 | tf_op jit(solution)/shard_map/ppermute | solution.py:241
  131.7 19.6 %collective-permute-start.15 = (bf16[96,2048]{1,0:T(8,128)(2,1)S(1)}, bf16[96,2048]{1,0:T(8,128)(2,1)S(1)}, u32[]{:S(2)}, u32[]{:S(2)}) collective-permute-start(bf16[96,2048]{1,0:T(8,128)(2,1)S(1)} %collective-permute-done.14.up), channel_id=1, source_target_pairs={{8,0},{16,8},{24,16},{28,24},{20,28},{12,20},{4,12},{0,4},{9,1},{1... | collective-permute-start | bytes 1179656 | tf_op jit(solution)/shard_map/ppermute | solution.py:242
  150.6 12.1 %collective-permute-start.9 = (bf16[96,2048]{1,0:T(8,128)(2,1)S(1)}, bf16[96,2048]{1,0:T(8,128)(2,1)}, u32[]{:S(2)}, u32[]{:S(2)}) collective-permute-start(bf16[96,2048]{1,0:T(8,128)(2,1)S(1)} %collective-permute-done.8.gate), channel_id=1, source_target_pairs={{0,8},{8,16},{16,24},{24,28},{28,20},{20,12},{12,4},{4,0},{1,9},{9... | collective-permute-start | bytes 1179656 | tf_op jit(solution)/shard_map/ppermute | solution.py:241
  151.3 12.1 %collective-permute-start.16 = (bf16[96,2048]{1,0:T(8,128)(2,1)S(1)}, bf16[96,2048]{1,0:T(8,128)(2,1)}, u32[]{:S(2)}, u32[]{:S(2)}) collective-permute-start(bf16[96,2048]{1,0:T(8,128)(2,1)S(1)} %collective-permute-done.15.up), channel_id=1, source_target_pairs={{8,0},{16,8},{24,16},{28,24},{20,28},{12,20},{4,12},{0,4},{9,1},{1... | collective-permute-start | bytes 1179656 | tf_op jit(solution)/shard_map/ppermute | solution.py:242
  154.1 55.5 %collective-permute-start.24 = (bf16[160,2048]{1,0:T(8,128)(2,1)S(1)}, bf16[160,2048]{1,0:T(8,128)(2,1)}, u32[]{:S(2)}, u32[]{:S(2)}) collective-permute-start(bf16[160,2048]{1,0:T(8,128)(2,1)S(1)} %collective-permute-done.23.gate.refs_2_), channel_id=1, source_target_pairs={{0,8},{8,16},{16,24},{24,28},{28,20},{20,12},{12,4},{4,0},{1,9},{9... | collective-permute-start | bytes 1966088 | tf_op jit(solution)/shard_map/ppermute | solution.py:241
  154.1 55.5 %collective-permute-start.31 = (bf16[160,2048]{1,0:T(8,128)(2,1)}, bf16[160,2048]{1,0:T(8,128)(2,1)}, u32[]{:S(2)}, u32[]{:S(2)}) collective-permute-start(bf16[160,2048]{1,0:T(8,128)(2,1)} %collective-permute-done.30.up), channel_id=1, source_target_pairs={{8,0},{16,8},{24,16},{28,24},{20,28},{12,20},{4,12},{0,4},{9,1},{1... | collective-permute-start | bytes 1966088 | tf_op jit(solution)/shard_map/ppermute | solution.py:242
  162.7 49.4 %collective-permute-start.10 = (bf16[96,2048]{1,0:T(8,128)(2,1)}, bf16[96,2048]{1,0:T(8,128)(2,1)}, u32[]{:S(2)}, u32[]{:S(2)}) collective-permute-start(bf16[96,2048]{1,0:T(8,128)(2,1)} %collective-permute-done.9.gate), channel_id=1, source_target_pairs={{0,8},{8,16},{16,24},{24,28},{28,20},{20,12},{12,4},{4,0},{1,9},{9... | collective-permute-start | bytes 1179656 | tf_op jit(solution)/shard_map/ppermute | solution.py:241
  163.4 48.6 %collective-permute-start.17 = (bf16[96,2048]{1,0:T(8,128)(2,1)}, bf16[96,2048]{1,0:T(8,128)(2,1)}, u32[]{:S(2)}, u32[]{:S(2)}) collective-permute-start(bf16[96,2048]{1,0:T(8,128)(2,1)} %collective-permute-done.16.up), channel_id=1, source_target_pairs={{8,0},{16,8},{24,16},{28,24},{20,28},{12,20},{4,12},{0,4},{9,1},{1... | collective-permute-start | bytes 1179656 | tf_op jit(solution)/shard_map/ppermute | solution.py:242
  165.5 1.2 collective-permute-start.32
  166.8 3.7 %collective-permute-start.33 = (f32[1,2048]{1,0:T(1,128)S(1)}, f32[1,2048]{1,0:T(1,128)S(1)}, u32[]{:S(2)}, u32[]{:S(2)}) collective-permute-start(f32[1,2048]{1,0:T(1,128)S(1)} %tree_add.9.refs_0_), channel_id=1, source_target_pairs={{0,2},{1,3},{2,0},{3,1},{4,6},{5,7},{6,4},{7,5},{8,10},{9,11},{10,... | collective-permute-start | bytes 24584 | tf_op jit(solution)/shard_map/ppermute | solution.py:217
  170.4 7.6 %collective-permute-start.34 = (f32[1,2048]{1,0:T(1,128)S(1)}, f32[1,2048]{1,0:T(1,128)S(1)}, u32[]{:S(2)}, u32[]{:S(2)}) collective-permute-start(f32[1,2048]{1,0:T(1,128)S(1)} %tree_add.10.refs_0_), channel_id=1, source_target_pairs={{0,4},{4,0},{8,12},{12,8},{16,20},{20,16},{24,28},{28,24},{1,5},{5... | collective-permute-start | bytes 24584 | tf_op jit(solution)/shard_map/ppermute | solution.py:217
  178.0 3.7 %collective-permute-start.35 = (f32[1,2048]{1,0:T(1,128)S(1)}, f32[1,2048]{1,0:T(1,128)S(1)}, u32[]{:S(2)}, u32[]{:S(2)}) collective-permute-start(f32[1,2048]{1,0:T(1,128)S(1)} %tree_add.11.refs_0_), channel_id=1, source_target_pairs={{0,8},{4,12},{8,0},{12,4},{16,24},{20,28},{24,16},{28,20},{1,9},{5... | collective-permute-start | bytes 24584 | tf_op jit(solution)/shard_map/ppermute | solution.py:217
  181.7 23.2 %collective-permute-start.36 = (f32[1,2048]{1,0:T(1,128)S(1)}, f32[1,2048]{1,0:T(1,128)S(1)}, u32[]{:S(2)}, u32[]{:S(2)}) collective-permute-start(f32[1,2048]{1,0:T(1,128)S(1)} %tree_add.12.refs_0_), channel_id=1, source_target_pairs={{0,16},{4,20},{8,24},{12,28},{16,0},{20,4},{24,8},{28,12},{1,17},{... | collective-permute-start | bytes 24584 | tf_op jit(solution)/shard_map/ppermute | solution.py:217
  182.8 1.1 copy-start.1
  183.9 1.1 copy-start.3
  185.0 1.0 copy-start.17
  186.0 1.0 copy-start.19
  188.3 1.1 copy-start.7
  189.4 1.1 copy-start.11
  190.5 1.2 copy-start.21
  190.5 1.6 copy-start.23
  192.1 1.4 copy-start.9
  193.5 1.2 copy-start.25
  193.5 1.6 copy-start.27
  195.1 1.4 copy-start.5
  196.4 1.2 copy-start.31
  196.4 1.6 copy-start.35
  198.0 1.4 copy-start.13
  199.4 1.2 copy-start.29
  199.4 1.6 copy-start.33
  201.0 1.4 copy-start.15
  202.4 1.2 copy-start.37
  202.4 1.6 copy-start.39
  (16 other events, 12.3 us)

commit v2 on v1

--- a/solution.py
+++ b/solution.py
@@ -9,11 +9,12 @@
 
 WHOLE = pl.BlockSpec(memory_space=pltpu.VMEM)
 OUTSIDE = pl.BlockSpec(memory_space=pl.ANY)
-SCALARS = pl.BlockSpec(memory_space=pltpu.SMEM)
+GRANT = 48
+MOST = 1
 
 
 def grant(mib):
-    return pltpu.CompilerParams(vmem_limit_bytes=mib << 20)
+    return pltpu.CompilerParams(vmem_limit_bytes=int(mib * 2**20))
 
 
 def ring_order(n):
@@ -80,15 +81,14 @@
             pltpu.SemaphoreType.DMA((4, pieces)),
             pltpu.SemaphoreType.DMA,
         ],
-        compiler_params=grant(48),
+        compiler_params=grant(GRANT),
         name="sums",
-    )(share, one_gate, other_gate, one_up, other_up)
-
-
-def narrow_kernel(spans, fresh_g, fresh_u, total_ref, factor_g, factor_u, *outs):
-    for side, fresh, factor in ((0, fresh_g, factor_g), (1, fresh_u, factor_u)):
-        factor[...] = jnp.sqrt(total_ref[side:side + 1])
-        scale = 1.0 / factor[...]
+    )(*[pltpu.with_memory_space_constraint(part, pltpu.HBM) for part in (share, one_gate, other_gate, one_up, other_up)])
+
+
+def narrow_kernel(spans, fresh_g, fresh_u, total_ref, *outs):
+    for side, fresh in ((0, fresh_g), (1, fresh_u)):
+        scale = 1.0 / jnp.sqrt(total_ref[side:side + 1])
         for (lo, hi), out in zip(spans, outs[side * len(spans):]):
             for r in range(lo, hi, 16):
                 out[r - lo:r - lo + 16] = (fresh[r:r + 16] * scale).astype(jnp.bfloat16)
@@ -96,17 +96,33 @@
 
 def narrow(spans, fresh_gate, fresh_up, total):
     cols = fresh_gate.shape[1]
-    factor = jax.ShapeDtypeStruct((1, cols), jnp.float32)
     shapes = [jax.ShapeDtypeStruct((hi - lo, cols), jnp.bfloat16) for lo, hi in spans]
-    factor_gate, factor_up, *pieces = pl.pallas_call(
+    pieces = pl.pallas_call(
         functools.partial(narrow_kernel, spans),
         in_specs=[WHOLE] * 3,
-        out_specs=[WHOLE] * (2 + 2 * len(spans)),
-        out_shape=[factor] * 2 + shapes * 2,
+        out_specs=[WHOLE] * (2 * len(spans)),
+        out_shape=shapes * 2,
         compiler_params=grant(16),
         name="narrow",
     )(fresh_gate, fresh_up, total)
-    return factor_gate, factor_up, pieces[:len(spans)], pieces[len(spans):]
+    return list(pieces[:len(spans)]), list(pieces[len(spans):])
+
+
+def root_kernel(total_ref, factor_g, factor_u):
+    factor_g[...] = jnp.sqrt(total_ref[0:1])
+    factor_u[...] = jnp.sqrt(total_ref[1:2])
+
+
+def roots(total):
+    shape = jax.ShapeDtypeStruct((1, total.shape[1]), jnp.float32)
+    return pl.pallas_call(
+        root_kernel,
+        in_specs=[WHOLE],
+        out_specs=[WHOLE] * 2,
+        out_shape=[shape, shape],
+        compiler_params=grant(2),
+        name="roots",
+    )(total)
 
 
 def run(copies):
@@ -116,10 +132,10 @@
         copy.wait()
 
 
-def start_kernel(spans, shard_ref, *refs):
+def start_kernel(spans, *refs):
     count = len(spans)
     outs, sems = refs[2 * count:2 * count + 2], refs[-1]
-    first = pl.multiple_of(shard_ref[0] * spans[-1][1], 16)
+    first = pl.multiple_of(lax.axis_index("shard") * spans[-1][1], 16)
     run([
         pltpu.make_async_copy(refs[side * count + c], outs[side].at[pl.ds(first + lo, hi - lo)], sems.at[side, c])
         for side in range(2)
@@ -127,38 +143,38 @@
     ])
 
 
-def start_outputs(shard, spans, gate, up, n):
+def start_outputs(spans, gate, up, n):
     shape = jax.ShapeDtypeStruct((n * spans[-1][1], gate[0].shape[1]), jnp.bfloat16)
     return pl.pallas_call(
         functools.partial(start_kernel, spans),
-        in_specs=[SCALARS] + [WHOLE] * (2 * len(spans)),
+        in_specs=[WHOLE] * (2 * len(spans)),
         out_specs=[OUTSIDE] * 2,
         out_shape=[shape, shape],
         scratch_shapes=[pltpu.SemaphoreType.DMA((2, len(spans)))],
         compiler_params=grant(4),
         name="start_outputs",
-    )(shard, *gate, *up)
-
-
-def put_kernel(step, lo, rows, n, shard_ref, gate, up, _, __, out_g, out_u, sems):
+    )(*gate, *up)
+
+
+def put_kernel(step, lo, rows, n, gate, up, _, __, out_g, out_u, sems):
     copies = []
     for side, (part, out, back) in enumerate(((gate, out_g, -step), (up, out_u, step))):
-        first = pl.multiple_of(ring_neighbour(shard_ref[0], back, n) * rows, 16)
+        first = pl.multiple_of(ring_neighbour(lax.axis_index("shard"), back, n) * rows, 16)
         copies.append(pltpu.make_async_copy(part, out.at[pl.ds(first + lo, part.shape[0])], sems.at[side]))
     run(copies)
 
 
-def put(shard, step, lo, rows, n, gate, up, outs):
+def put(step, lo, rows, n, gate, up, outs):
     return pl.pallas_call(
         functools.partial(put_kernel, step, lo, rows, n),
-        in_specs=[SCALARS, WHOLE, WHOLE, OUTSIDE, OUTSIDE],
+        in_specs=[WHOLE, WHOLE, OUTSIDE, OUTSIDE],
         out_specs=[OUTSIDE] * 2,
         out_shape=[jax.ShapeDtypeStruct(out.shape, out.dtype) for out in outs],
         scratch_shapes=[pltpu.SemaphoreType.DMA((2,))],
-        input_output_aliases={3: 0, 4: 1},
+        input_output_aliases={2: 0, 3: 1},
         compiler_params=grant(4),
         name="put",
-    )(shard, gate, up, *outs)
+    )(gate, up, *outs)
 
 
 def add_kernel(count, *refs):
@@ -179,23 +195,23 @@
     )(*terms, *after)
 
 
-def slot_kernel(count, index_ref, train, step, out):
+def slot_kernel(count, t, train, step, out):
     value = (train[...] + step[...]).astype(jnp.bfloat16).astype(jnp.float32)
     width = value.shape[1]
     value = jnp.concatenate([value] * count, axis=1)
     slot = lax.broadcasted_iota(jnp.int32, value.shape, 1) // width
-    out[...] = jnp.where(slot == index_ref[0], value, 0.0)
-
-
-def slot_of(index, train, step, count):
-    return pl.pallas_call(
-        functools.partial(slot_kernel, count),
-        in_specs=[SCALARS, WHOLE, WHOLE],
+    out[...] = jnp.where(slot == lax.axis_index("shard") * t + lax.axis_index("tp"), value, 0.0)
+
+
+def slot_of(train, step, count, t):
+    return pl.pallas_call(
+        functools.partial(slot_kernel, count, t),
+        in_specs=[WHOLE, WHOLE],
         out_specs=WHOLE,
         out_shape=jax.ShapeDtypeStruct((1, count * train.shape[1]), jnp.float32),
         compiler_params=grant(2),
         name="slot",
-    )(index, train, step)
+    )(train, step)
 
 
 def stages_of(n, most):
@@ -220,27 +236,25 @@
 
 def shards(mesh, one_gate, other_gate, one_up, other_up, mix_share, norm_train, norm_step):
     n, t = mesh.shape["shard"], mesh.shape["tp"]
-    me = lax.axis_index("shard")
-    shard = me[None].astype(jnp.int32)
-    device = shard * t + lax.axis_index("tp").astype(jnp.int32)
     rows, _ = one_gate.shape
     order = ring_order(n)
     forward = [(order[i], order[(i + 1) % n]) for i in range(n)]
     backward = [(b, a) for a, b in forward]
     spans = cuts(rows)
     fresh_gate, fresh_up, total = sums_of(mix_share[None], one_gate, other_gate, one_up, other_up)
-    for masks in stages_of(n, 2):
+    for masks in stages_of(n, MOST):
         total = exchange(total, "shard", n, masks)
-    factor_gate, factor_up, gate, up = narrow(spans, fresh_gate, fresh_up, total)
-    outs = start_outputs(shard, spans, gate, up, n)
-    norm = slot_of(device, norm_train[None], norm_step[None], n * t)
+    gate, up = narrow(spans, fresh_gate, fresh_up, total)
+    factor_gate, factor_up = roots(total)
+    outs = start_outputs(spans, gate, up, n)
+    norm = slot_of(norm_train[None], norm_step[None], n * t, t)
     left = [("tp", t, masks) for masks in stages_of(t, 1)] + [("shard", n, masks) for masks in stages_of(n, 1)]
     stage = 0
     for step in range(1, n):
         for c, (lo, hi) in enumerate(spans):
             gate[c] = lax.ppermute(gate[c], "shard", forward)
             up[c] = lax.ppermute(up[c], "shard", backward)
-            outs = put(shard, step, lo, rows, n, gate[c], up[c], outs)
+            outs = put(step, lo, rows, n, gate[c], up[c], outs)
         if step > 1 and stage < len(left):
             norm = exchange(norm, *left[stage], (gate[0],))
             stage += 1

time: 215 us -> 199 us (0.926)
  local copies, waits for them, and re-layouts: 27.4 us -> 0.01 us
  waiting for transfers between devices: 120 us -> 135 us
  Pallas kernels: 24.3 us -> 20.6 us
    ppermute x14, waiting for transfers between devices: 3.6 us -> 68 us  [shards(): up[c] = lax.ppermute(up[c], 'shard', backward)]
    ppermute x14, waiting for transfers between devices: 96.7 us -> 49.4 us  [shards(): gate[c] = lax.ppermute(gate[c], 'shard', forward)]
    unnamed x86 -> x4, local copies, waits for them, and re-layouts: 27.4 us -> 0.01 us
    ppermute x14, starting transfers between devices: 0.04 us -> 24.7 us  [shards(): gate[c] = lax.ppermute(gate[c], 'shard', forward)]
    ppermute x14, starting transfers between devices: 28.3 us -> 3.76 us  [shards(): up[c] = lax.ppermute(up[c], 'shard', backward)]
    pallas_call x14, Pallas kernels: 18.3 us -> 14.1 us  [put(): pl.pallas_call(functools.partial(put_kernel, step, lo, rows, n), in_specs...]
    ppermute x9 -> x8, waiting for transfers between devices: 20.1 us -> 18 us  [exchange(): lax.ppermute(value, axis, [(i, i ^ m) for i in range(n)])]
    ppermute x9 -> x8, starting transfers between devices: 12.1 us -> 13.3 us  [exchange(): lax.ppermute(value, axis, [(i, i ^ m) for i in range(n)])]
  transfers between devices with their start and end apart: 37 -> 36, of which waited for: 24 -> 17; matrix products, arithmetic and copies ran while one was open for 0% -> 0% of each run, Pallas kernels for 8% -> 8%
where the time goes in v2:
time: 199 us
  waiting for transfers between devices  135 us (68%)
  starting transfers between devices  41.8 us (21%)
  Pallas kernels  20.6 us (10%)
    ppermute x14, waiting for transfers between devices, shards(): up[c] = lax.ppermute(up[c], 'shard', backward)  68 us
    ppermute x14, waiting for transfers between devices, shards(): gate[c] = lax.ppermute(gate[c], 'shard', forward)  49.4 us
    ppermute x14, starting transfers between devices, shards(): gate[c] = lax.ppermute(gate[c], 'shard', forward)  24.7 us
    ppermute x8, waiting for transfers between devices, exchange(): lax.ppermute(value, axis, [(i, i ^ m) for i in range(n)])  18 us
    pallas_call x14, Pallas kernels, put(): pl.pallas_call(functools.partial(put_kernel, step, lo, rows, n), in_specs...  14.1 us
    ppermute x8, starting transfers between devices, exchange(): lax.ppermute(value, axis, [(i, i ^ m) for i in range(n)])  13.3 us
    pallas_call x1, Pallas kernels, sums_of(): pl.pallas_call(functools.partial(sums_kernel, pieces), in_specs=[OUTSIDE]...  4.27 us
  transfers between devices with their start and end apart: 36, of which 17 were waited for; matrix products, arithmetic and copies ran while one was open for 0% of the time, Pallas kernels for 8%

profile of v2, /device:TPU:0, one launch (start us, length us, event | category | flops | bytes accessed | tf_op | source)
XLA Modules:
  0.0 199.2 jit_solution(2210555801599790454)
XLA Ops:
  0.7 4.3 %sums.1 = (f32[256,2048]{1,0:T(8,128)S(1)}, f32[256,2048]{1,0:T(8,128)S(1)}, f32[2,2048]{1,0:T(2,128)S(1)}) custom-call(f32[1,256]{1,0:T(1,128)} %bitcast.7, f32[256,2048]{1,0:T(8,128)} %one_g.1, f32[256,2048]{1,0:T(8,128)} %other_g.1, f32[256,2048]{1,0:T(8,128)} %one_u.1, f32[256,2048]{1,0:T(8,128)} %other_u.1), custom_call_target="tpu_custom_call" | custom-call | tf_op jit(solution)/shard_map/sums/pallas_call | solution.py:73
  4.9 3.0 %collective-permute-start = (f32[2,2048]{1,0:T(2,128)S(1)}, f32[2,2048]{1,0:T(2,128)S(1)}, u32[]{:S(2)}, u32[]{:S(2)}) collective-permute-start(f32[2,2048]{1,0:T(2,128)S(1)} %get-tuple-element.46.refs_0_), channel_id=1, source_target_pairs={{0,4},{4,0},{8,12},{12,8},{16,20},{20,16},{24,28},{28,24},{1,5},{5... | collective-permute-start | bytes 49160 | tf_op jit(solution)/shard_map/ppermute | solution.py:233
  8.0 1.7 collective-permute-done.refs_1_
  9.7 2.1 %collective-permute-start.1 = (f32[2,2048]{1,0:T(2,128)S(1)}, f32[2,2048]{1,0:T(2,128)S(1)}, u32[]{:S(2)}, u32[]{:S(2)}) collective-permute-start(f32[2,2048]{1,0:T(2,128)S(1)} %tree_add.8.refs_0_), channel_id=1, source_target_pairs={{0,8},{4,12},{8,0},{12,4},{16,24},{20,28},{24,16},{28,20},{1,9},{5... | collective-permute-start | bytes 49160 | tf_op jit(solution)/shard_map/ppermute | solution.py:233
  11.8 1.7 collective-permute-done.1.refs_1_
  13.5 3.0 %collective-permute-start.2 = (f32[2,2048]{1,0:T(2,128)S(1)}, f32[2,2048]{1,0:T(2,128)S(1)}, u32[]{:S(2)}, u32[]{:S(2)}) collective-permute-start(f32[2,2048]{1,0:T(2,128)S(1)} %tree_add.9.refs_0_), channel_id=1, source_target_pairs={{0,16},{4,20},{8,24},{12,28},{16,0},{20,4},{24,8},{28,12},{1,17},{... | collective-permute-start | bytes 49160 | tf_op jit(solution)/shard_map/ppermute | solution.py:233
  16.5 1.7 collective-permute-done.2.refs_1_
  18.3 0.2 narrow.1
  18.5 2.0 collective-permute-start.17
  20.6 12.9 %collective-permute-done.17.gate = bf16[160,2048]{1,0:T(8,128)(2,1)S(1)} collective-permute-done((bf16[160,2048]{1,0:T(8,128)(2,1)S(1)}, bf16[160,2048]{1,0:T(8,128)(2,1)S(1)}, u32[]{:S(2)}, u32[]{:S(2)}) %collective-permute-start.17) | collective-permute-done | bytes 655392 | tf_op jit(solution)/shard_map/ppermute | solution.py:255
  33.5 1.9 collective-permute-start.18
  35.4 0.1 collective-permute-start.25
  35.5 12.9 %collective-permute-done.18.gate.refs_2_ = bf16[160,2048]{1,0:T(8,128)(2,1)S(1)} collective-permute-done((bf16[160,2048]{1,0:T(8,128)(2,1)S(1)}, bf16[160,2048]{1,0:T(8,128)(2,1)S(1)}, u32[]{:S(2)}, u32[]{:S(2)}) %collective-permute-start.18) | collective-permute-done | bytes 655392 | tf_op jit(solution)/shard_map/ppermute | solution.py:255
  48.4 1.9 collective-permute-start.19
  50.3 0.1 collective-permute-start.26
  50.4 1.9 collective-permute-start.10
  52.4 13.5 %collective-permute-done.19.gate.refs_2_ = bf16[160,2048]{1,0:T(8,128)(2,1)S(1)} collective-permute-done((bf16[160,2048]{1,0:T(8,128)(2,1)S(1)}, bf16[160,2048]{1,0:T(8,128)(2,1)S(1)}, u32[]{:S(2)}, u32[]{:S(2)}) %collective-permute-start.19) | collective-permute-done | bytes 655392 | tf_op jit(solution)/shard_map/ppermute | solution.py:255
  66.0 1.9 collective-permute-start.20
  67.9 0.1 collective-permute-start.27
  68.0 8.3 %collective-permute-done.10.up = bf16[96,2048]{1,0:T(8,128)(2,1)S(1)} collective-permute-done((bf16[96,2048]{1,0:T(8,128)(2,1)S(1)}, bf16[96,2048]{1,0:T(8,128)(2,1)S(1)}, u32[]{:S(2)}, u32[]{:S(2)}) %collective-permute-start.10) | collective-permute-done | bytes 393248 | tf_op jit(solution)/shard_map/ppermute | solution.py:256
  76.4 1.9 collective-permute-start.4
  78.4 10.1 %collective-permute-done.20.gate.refs_2_ = bf16[160,2048]{1,0:T(8,128)(2,1)S(1)} collective-permute-done((bf16[160,2048]{1,0:T(8,128)(2,1)S(1)}, bf16[160,2048]{1,0:T(8,128)(2,1)S(1)}, u32[]{:S(2)}, u32[]{:S(2)}) %collective-permute-start.20) | collective-permute-done | bytes 655392 | tf_op jit(solution)/shard_map/ppermute | solution.py:255
  88.5 1.9 collective-permute-start.21
  90.5 8.3 %collective-permute-done.11.up = bf16[96,2048]{1,0:T(8,128)(2,1)S(1)} collective-permute-done((bf16[96,2048]{1,0:T(8,128)(2,1)S(1)}, bf16[96,2048]{1,0:T(8,128)(2,1)S(1)}, u32[]{:S(2)}, u32[]{:S(2)}) %collective-permute-start.11) | collective-permute-done | bytes 393248 | tf_op jit(solution)/shard_map/ppermute | solution.py:256
  98.8 0.1 collective-permute-start.12
  98.9 1.9 collective-permute-start.5
  100.8 17.7 %collective-permute-done.12.up = bf16[96,2048]{1,0:T(8,128)(2,1)S(1)} collective-permute-done((bf16[96,2048]{1,0:T(8,128)(2,1)S(1)}, bf16[96,2048]{1,0:T(8,128)(2,1)S(1)}, u32[]{:S(2)}, u32[]{:S(2)}) %collective-permute-start.12) | collective-permute-done | bytes 393248 | tf_op jit(solution)/shard_map/ppermute | solution.py:256
  118.7 1.9 collective-permute-start.6
  120.6 1.8 collective-permute-start.22
  122.3 0.3 collective-permute-start.29
  122.6 7.9 %collective-permute-done.13.up = bf16[96,2048]{1,0:T(8,128)(2,1)S(1)} collective-permute-done((bf16[96,2048]{1,0:T(8,128)(2,1)S(1)}, bf16[96,2048]{1,0:T(8,128)(2,1)S(1)}, u32[]{:S(2)}, u32[]{:S(2)}) %collective-permute-start.13) | collective-permute-done | bytes 393248 | tf_op jit(solution)/shard_map/ppermute | solution.py:256
  130.5 0.1 collective-permute-start.14
  130.7 1.9 collective-permute-start.7
  132.6 17.7 %collective-permute-done.14.up = bf16[96,2048]{1,0:T(8,128)(2,1)S(1)} collective-permute-done((bf16[96,2048]{1,0:T(8,128)(2,1)S(1)}, bf16[96,2048]{1,0:T(8,128)(2,1)S(1)}, u32[]{:S(2)}, u32[]{:S(2)}) %collective-permute-start.14) | collective-permute-done | bytes 393248 | tf_op jit(solution)/shard_map/ppermute | solution.py:256
  150.4 1.9 collective-permute-start.8
  152.3 1.8 collective-permute-start.23
  154.1 0.3 collective-permute-start.30
  154.4 7.9 %collective-permute-done.15.up = bf16[96,2048]{1,0:T(8,128)(2,1)S(1)} collective-permute-done((bf16[96,2048]{1,0:T(8,128)(2,1)S(1)}, bf16[96,2048]{1,0:T(8,128)(2,1)S(1)}, u32[]{:S(2)}, u32[]{:S(2)}) %collective-permute-start.15) | collective-permute-done | bytes 393248 | tf_op jit(solution)/shard_map/ppermute | solution.py:256
  162.3 0.1 collective-permute-start.16
  162.4 1.9 collective-permute-start.9
  164.5 1.2 collective-permute-done.31.refs_1_
  165.7 1.5 collective-permute-start.32
  167.2 2.1 %collective-permute-done.32.refs_1_ = f32[1,2048]{1,0:T(1,128)S(1)} collective-permute-done((f32[1,2048]{1,0:T(1,128)S(1)}, f32[1,2048]{1,0:T(1,128)S(1)}, u32[]{:S(2)}, u32[]{:S(2)}) %collective-permute-start.32) | collective-permute-done | bytes 8224 | tf_op jit(solution)/shard_map/ppermute | solution.py:233
  169.3 0.1 collective-permute-start.33
  169.4 5.9 %collective-permute-done.33.refs_1_ = f32[1,2048]{1,0:T(1,128)S(1)} collective-permute-done((f32[1,2048]{1,0:T(1,128)S(1)}, f32[1,2048]{1,0:T(1,128)S(1)}, u32[]{:S(2)}, u32[]{:S(2)}) %collective-permute-start.33) | collective-permute-done | bytes 8224 | tf_op jit(solution)/shard_map/ppermute | solution.py:233
  175.3 3.6 %collective-permute-done.34.refs_1_ = f32[1,2048]{1,0:T(1,128)S(1)} collective-permute-done((f32[1,2048]{1,0:T(1,128)S(1)}, f32[1,2048]{1,0:T(1,128)S(1)}, u32[]{:S(2)}, u32[]{:S(2)}) %collective-permute-start.34) | collective-permute-done | bytes 8224 | tf_op jit(solution)/shard_map/ppermute | solution.py:233
  179.0 3.5 %collective-permute-start.35 = (f32[1,2048]{1,0:T(1,128)S(1)}, f32[1,2048]{1,0:T(1,128)S(1)}, u32[]{:S(2)}, u32[]{:S(2)}) collective-permute-start(f32[1,2048]{1,0:T(1,128)S(1)} %tree_add.14.refs_0_), channel_id=1, source_target_pairs={{0,16},{4,20},{8,24},{12,28},{16,0},{20,4},{24,8},{28,12},{1,17},{... | collective-permute-start | bytes 24584 | tf_op jit(solution)/shard_map/ppermute | solution.py:233
  182.4 1.3 start_outputs.1
  183.8 0.6 roots.1
  184.4 1.1 put.14
  185.5 0.9 put.15
  186.4 1.1 put.16
  187.5 0.9 put.17
  188.4 1.1 put.18
  189.5 0.9 put.19
  190.5 1.1 put.20
  191.6 0.9 put.21
  192.5 1.1 put.22
  193.6 0.9 put.23
  194.6 1.1 put.24
  195.7 0.9 put.25
  196.6 0.6 convert_reduce_fusion
  197.2 1.1 put.26
  198.3 0.9 put.27
  (40 shorter events, 0.9 us)
Async XLA Ops:
  0.6 163.7 %copy-start = (f32[64]{0:T(128)S(1)}, f32[64]{0:T(128)}, u32[]{:S(2)}) copy-start(f32[64]{0:T(128)} %param.12) | copy-start | bytes 772
  0.6 163.7 %copy-start.1 = (f32[64]{0:T(128)S(1)}, f32[64]{0:T(128)}, u32[]{:S(2)}) copy-start(f32[64]{0:T(128)} %param.13) | copy-start | bytes 772
  4.9 4.8 %collective-permute-start = (f32[2,2048]{1,0:T(2,128)S(1)}, f32[2,2048]{1,0:T(2,128)S(1)}, u32[]{:S(2)}, u32[]{:S(2)}) collective-permute-start(f32[2,2048]{1,0:T(2,128)S(1)} %get-tuple-element.46.refs_0_), channel_id=1, source_target_pairs={{0,4},{4,0},{8,12},{12,8},{16,20},{20,16},{24,28},{28,24},{1,5},{5... | collective-permute-start | bytes 49160 | tf_op jit(solution)/shard_map/ppermute | solution.py:233
  9.7 3.8 %collective-permute-start.1 = (f32[2,2048]{1,0:T(2,128)S(1)}, f32[2,2048]{1,0:T(2,128)S(1)}, u32[]{:S(2)}, u32[]{:S(2)}) collective-permute-start(f32[2,2048]{1,0:T(2,128)S(1)} %tree_add.8.refs_0_), channel_id=1, source_target_pairs={{0,8},{4,12},{8,0},{12,4},{16,24},{20,28},{24,16},{28,20},{1,9},{5... | collective-permute-start | bytes 49160 | tf_op jit(solution)/shard_map/ppermute | solution.py:233
  13.5 4.8 %collective-permute-start.2 = (f32[2,2048]{1,0:T(2,128)S(1)}, f32[2,2048]{1,0:T(2,128)S(1)}, u32[]{:S(2)}, u32[]{:S(2)}) collective-permute-start(f32[2,2048]{1,0:T(2,128)S(1)} %tree_add.9.refs_0_), channel_id=1, source_target_pairs={{0,16},{4,20},{8,24},{12,28},{16,0},{20,4},{24,8},{28,12},{1,17},{... | collective-permute-start | bytes 49160 | tf_op jit(solution)/shard_map/ppermute | solution.py:233
  18.5 15.0 %collective-permute-start.17 = (bf16[160,2048]{1,0:T(8,128)(2,1)S(1)}, bf16[160,2048]{1,0:T(8,128)(2,1)S(1)}, u32[]{:S(2)}, u32[]{:S(2)}) collective-permute-start(bf16[160,2048]{1,0:T(8,128)(2,1)S(1)} %get-tuple-element.49.refs_0_), channel_id=1, source_target_pairs={{0,8},{8,16},{16,24},{24,28},{28,20},{20,12},{12,4},{4,0},{1,9},{9... | collective-permute-start | bytes 1966088 | tf_op jit(solution)/shard_map/ppermute | solution.py:255
  20.5 14.9 %collective-permute-start.24 = (bf16[160,2048]{1,0:T(8,128)(2,1)S(1)}, bf16[160,2048]{1,0:T(8,128)(2,1)S(1)}, u32[]{:S(2)}, u32[]{:S(2)}) collective-permute-start(bf16[160,2048]{1,0:T(8,128)(2,1)S(1)} %get-tuple-element.50.refs_2_), channel_id=1, source_target_pairs={{8,0},{16,8},{24,16},{28,24},{20,28},{12,20},{4,12},{0,4},{9,1},{1... | collective-permute-start | bytes 1966088 | tf_op jit(solution)/shard_map/ppermute | solution.py:256
  33.5 14.9 %collective-permute-start.18 = (bf16[160,2048]{1,0:T(8,128)(2,1)S(1)}, bf16[160,2048]{1,0:T(8,128)(2,1)S(1)}, u32[]{:S(2)}, u32[]{:S(2)}) collective-permute-start(bf16[160,2048]{1,0:T(8,128)(2,1)S(1)} %collective-permute-done.17.gate), channel_id=1, source_target_pairs={{0,8},{8,16},{16,24},{24,28},{28,20},{20,12},{12,4},{4,0},{1,9},{9... | collective-permute-start | bytes 1966088 | tf_op jit(solution)/shard_map/ppermute | solution.py:255
  35.4 14.9 %collective-permute-start.25 = (bf16[160,2048]{1,0:T(8,128)(2,1)S(1)}, bf16[160,2048]{1,0:T(8,128)(2,1)S(1)}, u32[]{:S(2)}, u32[]{:S(2)}) collective-permute-start(bf16[160,2048]{1,0:T(8,128)(2,1)S(1)} %collective-permute-done.24.up), channel_id=1, source_target_pairs={{8,0},{16,8},{24,16},{28,24},{20,28},{12,20},{4,12},{0,4},{9,1},{1... | collective-permute-start | bytes 1966088 | tf_op jit(solution)/shard_map/ppermute | solution.py:256
  48.4 17.6 %collective-permute-start.19 = (bf16[160,2048]{1,0:T(8,128)(2,1)S(1)}, bf16[160,2048]{1,0:T(8,128)(2,1)S(1)}, u32[]{:S(2)}, u32[]{:S(2)}) collective-permute-start(bf16[160,2048]{1,0:T(8,128)(2,1)S(1)} %collective-permute-done.18.gate.refs_2_), channel_id=1, source_target_pairs={{0,8},{8,16},{16,24},{24,28},{28,20},{20,12},{12,4},{4,0},{1,9},{9... | collective-permute-start | bytes 1966088 | tf_op jit(solution)/shard_map/ppermute | solution.py:255
  50.3 17.6 %collective-permute-start.26 = (bf16[160,2048]{1,0:T(8,128)(2,1)S(1)}, bf16[160,2048]{1,0:T(8,128)(2,1)S(1)}, u32[]{:S(2)}, u32[]{:S(2)}) collective-permute-start(bf16[160,2048]{1,0:T(8,128)(2,1)S(1)} %collective-permute-done.25.up), channel_id=1, source_target_pairs={{8,0},{16,8},{24,16},{28,24},{20,28},{12,20},{4,12},{0,4},{9,1},{1... | collective-permute-start | bytes 1966088 | tf_op jit(solution)/shard_map/ppermute | solution.py:256
  50.4 25.9 %collective-permute-start.10 = (bf16[96,2048]{1,0:T(8,128)(2,1)S(1)}, bf16[96,2048]{1,0:T(8,128)(2,1)S(1)}, u32[]{:S(2)}, u32[]{:S(2)}) collective-permute-start(bf16[96,2048]{1,0:T(8,128)(2,1)S(1)} %get-tuple-element.48.refs_3_), channel_id=1, source_target_pairs={{8,0},{16,8},{24,16},{28,24},{20,28},{12,20},{4,12},{0,4},{9,1},{1... | collective-permute-start | bytes 1179656 | tf_op jit(solution)/shard_map/ppermute | solution.py:256
  52.3 24.1 %collective-permute-start.3 = (bf16[96,2048]{1,0:T(8,128)(2,1)S(1)}, bf16[96,2048]{1,0:T(8,128)(2,1)S(1)}, u32[]{:S(2)}, u32[]{:S(2)}) collective-permute-start(bf16[96,2048]{1,0:T(8,128)(2,1)S(1)} %get-tuple-element.47.refs_1_), channel_id=1, source_target_pairs={{0,8},{8,16},{16,24},{24,28},{28,20},{20,12},{12,4},{4,0},{1,9},{9... | collective-permute-start | bytes 1179656 | tf_op jit(solution)/shard_map/ppermute | solution.py:255
  66.0 22.5 %collective-permute-start.20 = (bf16[160,2048]{1,0:T(8,128)(2,1)S(1)}, bf16[160,2048]{1,0:T(8,128)(2,1)S(1)}, u32[]{:S(2)}, u32[]{:S(2)}) collective-permute-start(bf16[160,2048]{1,0:T(8,128)(2,1)S(1)} %collective-permute-done.19.gate.refs_2_), channel_id=1, source_target_pairs={{0,8},{8,16},{16,24},{24,28},{28,20},{20,12},{12,4},{4,0},{1,9},{9... | collective-permute-start | bytes 1966088 | tf_op jit(solution)/shard_map/ppermute | solution.py:255
  67.9 22.5 %collective-permute-start.27 = (bf16[160,2048]{1,0:T(8,128)(2,1)S(1)}, bf16[160,2048]{1,0:T(8,128)(2,1)S(1)}, u32[]{:S(2)}, u32[]{:S(2)}) collective-permute-start(bf16[160,2048]{1,0:T(8,128)(2,1)S(1)} %collective-permute-done.26.up), channel_id=1, source_target_pairs={{8,0},{16,8},{24,16},{28,24},{20,28},{12,20},{4,12},{0,4},{9,1},{1... | collective-permute-start | bytes 1966088 | tf_op jit(solution)/shard_map/ppermute | solution.py:256
  76.3 22.5 %collective-permute-start.11 = (bf16[96,2048]{1,0:T(8,128)(2,1)S(1)}, bf16[96,2048]{1,0:T(8,128)(2,1)S(1)}, u32[]{:S(2)}, u32[]{:S(2)}) collective-permute-start(bf16[96,2048]{1,0:T(8,128)(2,1)S(1)} %collective-permute-done.10.up), channel_id=1, source_target_pairs={{8,0},{16,8},{24,16},{28,24},{20,28},{12,20},{4,12},{0,4},{9,1},{1... | collective-permute-start | bytes 1179656 | tf_op jit(solution)/shard_map/ppermute | solution.py:256
  76.4 22.5 %collective-permute-start.4 = (bf16[96,2048]{1,0:T(8,128)(2,1)S(1)}, bf16[96,2048]{1,0:T(8,128)(2,1)S(1)}, u32[]{:S(2)}, u32[]{:S(2)}) collective-permute-start(bf16[96,2048]{1,0:T(8,128)(2,1)S(1)} %collective-permute-done.3.gate), channel_id=1, source_target_pairs={{0,8},{8,16},{16,24},{24,28},{28,20},{20,12},{12,4},{4,0},{1,9},{9... | collective-permute-start | bytes 1179656 | tf_op jit(solution)/shard_map/ppermute | solution.py:255
  88.5 32.1 %collective-permute-start.21 = (bf16[160,2048]{1,0:T(8,128)(2,1)S(1)}, bf16[160,2048]{1,0:T(8,128)(2,1)S(1)}, u32[]{:S(2)}, u32[]{:S(2)}) collective-permute-start(bf16[160,2048]{1,0:T(8,128)(2,1)S(1)} %collective-permute-done.20.gate.refs_2_), channel_id=1, source_target_pairs={{0,8},{8,16},{16,24},{24,28},{28,20},{20,12},{12,4},{4,0},{1,9},{9... | collective-permute-start | bytes 1966088 | tf_op jit(solution)/shard_map/ppermute | solution.py:255
  90.4 32.0 %collective-permute-start.28 = (bf16[160,2048]{1,0:T(8,128)(2,1)S(1)}, bf16[160,2048]{1,0:T(8,128)(2,1)S(1)}, u32[]{:S(2)}, u32[]{:S(2)}) collective-permute-start(bf16[160,2048]{1,0:T(8,128)(2,1)S(1)} %collective-permute-done.27.up), channel_id=1, source_target_pairs={{8,0},{16,8},{24,16},{28,24},{20,28},{12,20},{4,12},{0,4},{9,1},{1... | collective-permute-start | bytes 1966088 | tf_op jit(solution)/shard_map/ppermute | solution.py:256
  98.8 19.8 %collective-permute-start.12 = (bf16[96,2048]{1,0:T(8,128)(2,1)S(1)}, bf16[96,2048]{1,0:T(8,128)(2,1)S(1)}, u32[]{:S(2)}, u32[]{:S(2)}) collective-permute-start(bf16[96,2048]{1,0:T(8,128)(2,1)S(1)} %collective-permute-done.11.up), channel_id=1, source_target_pairs={{8,0},{16,8},{24,16},{28,24},{20,28},{12,20},{4,12},{0,4},{9,1},{1... | collective-permute-start | bytes 1179656 | tf_op jit(solution)/shard_map/ppermute | solution.py:256
  98.9 19.8 %collective-permute-start.5 = (bf16[96,2048]{1,0:T(8,128)(2,1)S(1)}, bf16[96,2048]{1,0:T(8,128)(2,1)S(1)}, u32[]{:S(2)}, u32[]{:S(2)}) collective-permute-start(bf16[96,2048]{1,0:T(8,128)(2,1)S(1)} %collective-permute-done.4.gate), channel_id=1, source_target_pairs={{0,8},{8,16},{16,24},{24,28},{28,20},{20,12},{12,4},{4,0},{1,9},{9... | collective-permute-start | bytes 1179656 | tf_op jit(solution)/shard_map/ppermute | solution.py:255
  118.6 12.0 %collective-permute-start.13 = (bf16[96,2048]{1,0:T(8,128)(2,1)S(1)}, bf16[96,2048]{1,0:T(8,128)(2,1)S(1)}, u32[]{:S(2)}, u32[]{:S(2)}) collective-permute-start(bf16[96,2048]{1,0:T(8,128)(2,1)S(1)} %collective-permute-done.12.up), channel_id=1, source_target_pairs={{8,0},{16,8},{24,16},{28,24},{20,28},{12,20},{4,12},{0,4},{9,1},{1... | collective-permute-start | bytes 1179656 | tf_op jit(solution)/shard_map/ppermute | solution.py:256
  118.7 12.0 %collective-permute-start.6 = (bf16[96,2048]{1,0:T(8,128)(2,1)S(1)}, bf16[96,2048]{1,0:T(8,128)(2,1)S(1)}, u32[]{:S(2)}, u32[]{:S(2)}) collective-permute-start(bf16[96,2048]{1,0:T(8,128)(2,1)S(1)} %collective-permute-done.5.gate), channel_id=1, source_target_pairs={{0,8},{8,16},{16,24},{24,28},{28,20},{20,12},{12,4},{4,0},{1,9},{9... | collective-permute-start | bytes 1179656 | tf_op jit(solution)/shard_map/ppermute | solution.py:255
  120.6 31.8 %collective-permute-start.22 = (bf16[160,2048]{1,0:T(8,128)(2,1)S(1)}, bf16[160,2048]{1,0:T(8,128)(2,1)S(1)}, u32[]{:S(2)}, u32[]{:S(2)}) collective-permute-start(bf16[160,2048]{1,0:T(8,128)(2,1)S(1)} %collective-permute-done.21.gate.refs_2_), channel_id=1, source_target_pairs={{0,8},{8,16},{16,24},{24,28},{28,20},{20,12},{12,4},{4,0},{1,9},{9... | collective-permute-start | bytes 1966088 | tf_op jit(solution)/shard_map/ppermute | solution.py:255
  122.3 31.8 %collective-permute-start.29 = (bf16[160,2048]{1,0:T(8,128)(2,1)S(1)}, bf16[160,2048]{1,0:T(8,128)(2,1)S(1)}, u32[]{:S(2)}, u32[]{:S(2)}) collective-permute-start(bf16[160,2048]{1,0:T(8,128)(2,1)S(1)} %collective-permute-done.28.up), channel_id=1, source_target_pairs={{8,0},{16,8},{24,16},{28,24},{20,28},{12,20},{4,12},{0,4},{9,1},{1... | collective-permute-start | bytes 1966088 | tf_op jit(solution)/shard_map/ppermute | solution.py:256
  130.5 19.8 %collective-permute-start.14 = (bf16[96,2048]{1,0:T(8,128)(2,1)S(1)}, bf16[96,2048]{1,0:T(8,128)(2,1)S(1)}, u32[]{:S(2)}, u32[]{:S(2)}) collective-permute-start(bf16[96,2048]{1,0:T(8,128)(2,1)S(1)} %collective-permute-done.13.up), channel_id=1, source_target_pairs={{8,0},{16,8},{24,16},{28,24},{20,28},{12,20},{4,12},{0,4},{9,1},{1... | collective-permute-start | bytes 1179656 | tf_op jit(solution)/shard_map/ppermute | solution.py:256
  130.7 19.8 %collective-permute-start.7 = (bf16[96,2048]{1,0:T(8,128)(2,1)S(1)}, bf16[96,2048]{1,0:T(8,128)(2,1)S(1)}, u32[]{:S(2)}, u32[]{:S(2)}) collective-permute-start(bf16[96,2048]{1,0:T(8,128)(2,1)S(1)} %collective-permute-done.6.gate), channel_id=1, source_target_pairs={{0,8},{8,16},{16,24},{24,28},{28,20},{20,12},{12,4},{4,0},{1,9},{9... | collective-permute-start | bytes 1179656 | tf_op jit(solution)/shard_map/ppermute | solution.py:255
  150.3 12.0 %collective-permute-start.15 = (bf16[96,2048]{1,0:T(8,128)(2,1)S(1)}, bf16[96,2048]{1,0:T(8,128)(2,1)S(1)}, u32[]{:S(2)}, u32[]{:S(2)}) collective-permute-start(bf16[96,2048]{1,0:T(8,128)(2,1)S(1)} %collective-permute-done.14.up), channel_id=1, source_target_pairs={{8,0},{16,8},{24,16},{28,24},{20,28},{12,20},{4,12},{0,4},{9,1},{1... | collective-permute-start | bytes 1179656 | tf_op jit(solution)/shard_map/ppermute | solution.py:256
  150.4 12.0 %collective-permute-start.8 = (bf16[96,2048]{1,0:T(8,128)(2,1)S(1)}, bf16[96,2048]{1,0:T(8,128)(2,1)S(1)}, u32[]{:S(2)}, u32[]{:S(2)}) collective-permute-start(bf16[96,2048]{1,0:T(8,128)(2,1)S(1)} %collective-permute-done.7.gate), channel_id=1, source_target_pairs={{0,8},{8,16},{16,24},{24,28},{28,20},{20,12},{12,4},{4,0},{1,9},{9... | collective-permute-start | bytes 1179656 | tf_op jit(solution)/shard_map/ppermute | solution.py:255
  152.3 44.9 %collective-permute-start.23 = (bf16[160,2048]{1,0:T(8,128)(2,1)S(1)}, bf16[160,2048]{1,0:T(8,128)(2,1)S(1)}, u32[]{:S(2)}, u32[]{:S(2)}) collective-permute-start(bf16[160,2048]{1,0:T(8,128)(2,1)S(1)} %collective-permute-done.22.gate.refs_2_), channel_id=1, source_target_pairs={{0,8},{8,16},{16,24},{24,28},{28,20},{20,12},{12,4},{4,0},{1,9},{9... | collective-permute-start | bytes 1966088 | tf_op jit(solution)/shard_map/ppermute | solution.py:255
  154.1 43.1 %collective-permute-start.30 = (bf16[160,2048]{1,0:T(8,128)(2,1)S(1)}, bf16[160,2048]{1,0:T(8,128)(2,1)S(1)}, u32[]{:S(2)}, u32[]{:S(2)}) collective-permute-start(bf16[160,2048]{1,0:T(8,128)(2,1)S(1)} %collective-permute-done.29.up), channel_id=1, source_target_pairs={{8,0},{16,8},{24,16},{28,24},{20,28},{12,20},{4,12},{0,4},{9,1},{1... | collective-permute-start | bytes 1966088 | tf_op jit(solution)/shard_map/ppermute | solution.py:256
  162.3 36.0 %collective-permute-start.16 = (bf16[96,2048]{1,0:T(8,128)(2,1)S(1)}, bf16[96,2048]{1,0:T(8,128)(2,1)S(1)}, u32[]{:S(2)}, u32[]{:S(2)}) collective-permute-start(bf16[96,2048]{1,0:T(8,128)(2,1)S(1)} %collective-permute-done.15.up), channel_id=1, source_target_pairs={{8,0},{16,8},{24,16},{28,24},{20,28},{12,20},{4,12},{0,4},{9,1},{1... | collective-permute-start | bytes 1179656 | tf_op jit(solution)/shard_map/ppermute | solution.py:256
  162.4 35.9 %collective-permute-start.9 = (bf16[96,2048]{1,0:T(8,128)(2,1)S(1)}, bf16[96,2048]{1,0:T(8,128)(2,1)S(1)}, u32[]{:S(2)}, u32[]{:S(2)}) collective-permute-start(bf16[96,2048]{1,0:T(8,128)(2,1)S(1)} %collective-permute-done.8.gate), channel_id=1, source_target_pairs={{0,8},{8,16},{16,24},{24,28},{28,20},{20,12},{12,4},{4,0},{1,9},{9... | collective-permute-start | bytes 1179656 | tf_op jit(solution)/shard_map/ppermute | solution.py:255
  164.4 1.2 collective-permute-start.31
  165.7 3.7 %collective-permute-start.32 = (f32[1,2048]{1,0:T(1,128)S(1)}, f32[1,2048]{1,0:T(1,128)S(1)}, u32[]{:S(2)}, u32[]{:S(2)}) collective-permute-start(f32[1,2048]{1,0:T(1,128)S(1)} %tree_add.11.refs_0_), channel_id=1, source_target_pairs={{0,2},{1,3},{2,0},{3,1},{4,6},{5,7},{6,4},{7,5},{8,10},{9,11},{10,... | collective-permute-start | bytes 24584 | tf_op jit(solution)/shard_map/ppermute | solution.py:233
  169.3 6.0 %collective-permute-start.33 = (f32[1,2048]{1,0:T(1,128)S(1)}, f32[1,2048]{1,0:T(1,128)S(1)}, u32[]{:S(2)}, u32[]{:S(2)}) collective-permute-start(f32[1,2048]{1,0:T(1,128)S(1)} %tree_add.12.refs_0_), channel_id=1, source_target_pairs={{0,4},{4,0},{8,12},{12,8},{16,20},{20,16},{24,28},{28,24},{1,5},{5... | collective-permute-start | bytes 24584 | tf_op jit(solution)/shard_map/ppermute | solution.py:233
  175.3 3.7 %collective-permute-start.34 = (f32[1,2048]{1,0:T(1,128)S(1)}, f32[1,2048]{1,0:T(1,128)S(1)}, u32[]{:S(2)}, u32[]{:S(2)}) collective-permute-start(f32[1,2048]{1,0:T(1,128)S(1)} %tree_add.13.refs_0_), channel_id=1, source_target_pairs={{0,8},{4,12},{8,0},{12,4},{16,24},{20,28},{24,16},{28,20},{1,9},{5... | collective-permute-start | bytes 24584 | tf_op jit(solution)/shard_map/ppermute | solution.py:233
  179.0 15.6 %collective-permute-start.35 = (f32[1,2048]{1,0:T(1,128)S(1)}, f32[1,2048]{1,0:T(1,128)S(1)}, u32[]{:S(2)}, u32[]{:S(2)}) collective-permute-start(f32[1,2048]{1,0:T(1,128)S(1)} %tree_add.14.refs_0_), channel_id=1, source_target_pairs={{0,16},{4,20},{8,24},{12,28},{16,0},{20,4},{24,8},{28,12},{1,17},{... | collective-permute-start | bytes 24584 | tf_op jit(solution)/shard_map/ppermute | solution.py:233

commit v3 on v2

--- a/solution.py
+++ b/solution.py
@@ -10,7 +10,7 @@
 WHOLE = pl.BlockSpec(memory_space=pltpu.VMEM)
 OUTSIDE = pl.BlockSpec(memory_space=pl.ANY)
 GRANT = 48
-MOST = 1
+MOST = 2
 
 
 def grant(mib):
@@ -29,34 +29,28 @@
 def cuts(rows):
     if rows < 256:
         return [(0, rows)]
-    edges = [0, 5 * rows // 8, rows]
+    edges = [0, rows // 2, 3 * rows // 4, rows]
     return list(zip(edges[:-1], edges[1:]))
 
 
-def sums_kernel(pieces, share, one_g, other_g, one_u, other_u, fresh_g, fresh_u, sums, held, shares, sems, share_sem):
+def sums_kernel(edges, share, one_g, other_g, one_u, other_u, fresh_g, fresh_u, sums, held, shares, sems, share_sem):
     rows, cols = fresh_g.shape
-    tall = rows // pieces
-    sources = (one_g, other_g, one_u, other_u)
-
-    def copy(k, p):
-        span = pl.ds(p * tall, tall)
-        return pltpu.make_async_copy(sources[k].at[span], held.at[k, span], sems.at[k, p])
-
+    spans = list(zip(edges[:-1], edges[1:]))
     first = pltpu.make_async_copy(share, shares, share_sem)
     first.start()
-    for p in range(pieces):
-        for k in range(4):
-            copy(k, p).start()
+    for p, (lo, hi) in enumerate(spans):
+        for k, source in enumerate((one_g, other_g, one_u, other_u)):
+            pltpu.make_async_copy(source.at[pl.ds(lo, hi - lo)], held.at[k, pl.ds(lo, hi - lo)], sems.at[p]).start()
     first.wait()
     row = lax.broadcasted_iota(jnp.int32, (rows, rows), 0)
     lane = lax.broadcasted_iota(jnp.int32, (rows, rows), 1)
     mix = jnp.sum(jnp.where(row == lane, shares[...], 0.0), axis=1, keepdims=True)
     rest = 1.0 - mix
     total = [jnp.zeros((8, cols), jnp.float32) for _ in range(2)]
-    for p in range(pieces):
-        for k in range(4):
-            copy(k, p).wait()
-        for r in range(p * tall, (p + 1) * tall, 8):
+    for p, (lo, hi) in enumerate(spans):
+        piece = held.at[:, pl.ds(lo, hi - lo)]
+        pltpu.make_async_copy(piece, piece, sems.at[p]).wait()
+        for r in range(lo, hi, 8):
             m, w = mix[r:r + 8], rest[r:r + 8]
             for side, fresh in ((0, fresh_g), (1, fresh_u)):
                 value = m * held[2 * side, r:r + 8] + w * held[2 * side + 1, r:r + 8]
@@ -68,17 +62,17 @@
 
 def sums_of(share, one_gate, other_gate, one_up, other_up):
     rows, cols = one_gate.shape
-    pieces = max(1, rows // 32)
+    edges = [0, rows] if rows < 256 else [0, rows // 4, rows // 2, 3 * rows // 4, rows]
     wide = jax.ShapeDtypeStruct((rows, cols), jnp.float32)
     return pl.pallas_call(
-        functools.partial(sums_kernel, pieces),
+        functools.partial(sums_kernel, edges),
         in_specs=[OUTSIDE] * 5,
         out_specs=[WHOLE] * 3,
         out_shape=[wide, wide, jax.ShapeDtypeStruct((2, cols), jnp.float32)],
         scratch_shapes=[
             pltpu.VMEM((4, rows, cols), jnp.float32),
             pltpu.VMEM(share.shape, jnp.float32),
-            pltpu.SemaphoreType.DMA((4, pieces)),
+            pltpu.SemaphoreType.DMA((len(edges) - 1,)),
             pltpu.SemaphoreType.DMA,
         ],
         compiler_params=grant(GRANT),
@@ -229,9 +223,11 @@
     return spans
 
 
-def exchange(value, axis, n, masks, after=(), kind=jnp.float32):
-    others = [lax.ppermute(value, axis, [(i, i ^ m) for i in range(n)]) for m in masks]
-    return tree_add([value] + others, after, kind)
+def exchange(value, axis, n, masks, after=()):
+    others = []
+    for mask in masks:
+        others.append(lax.ppermute(value, axis, [(i, i ^ mask) for i in range(n)]))
+    return tree_add([value] + others, after)
 
 
 def shards(mesh, one_gate, other_gate, one_up, other_up, mix_share, norm_train, norm_step):
@@ -242,20 +238,21 @@
     backward = [(b, a) for a, b in forward]
     spans = cuts(rows)
     fresh_gate, fresh_up, total = sums_of(mix_share[None], one_gate, other_gate, one_up, other_up)
+    norm = slot_of(norm_train[None], norm_step[None], n * t, t)
     for masks in stages_of(n, MOST):
         total = exchange(total, "shard", n, masks)
     gate, up = narrow(spans, fresh_gate, fresh_up, total)
     factor_gate, factor_up = roots(total)
     outs = start_outputs(spans, gate, up, n)
-    norm = slot_of(norm_train[None], norm_step[None], n * t, t)
     left = [("tp", t, masks) for masks in stages_of(t, 1)] + [("shard", n, masks) for masks in stages_of(n, 1)]
-    stage = 0
+    norm = exchange(norm, *left[0])
+    stage = 1
     for step in range(1, n):
         for c, (lo, hi) in enumerate(spans):
             gate[c] = lax.ppermute(gate[c], "shard", forward)
             up[c] = lax.ppermute(up[c], "shard", backward)
             outs = put(step, lo, rows, n, gate[c], up[c], outs)
-        if step > 1 and stage < len(left):
+        if stage < len(left):
             norm = exchange(norm, *left[stage], (gate[0],))
             stage += 1
     for axis, size, masks in left[stage:]:

time: 199 us -> 201 us (1.010)
  waiting for transfers between devices: 135 us -> 127 us
  starting transfers between devices: 41.8 us -> 47.8 us
  Pallas kernels: 20.6 us -> 24.9 us
    ppermute x14 -> x21, waiting for transfers between devices: 68 us -> 44 us  [shards(): up[c] = lax.ppermute(up[c], 'shard', backward)]
    ppermute x14 -> x21, starting transfers between devices: 3.76 us -> 22.5 us  [shards(): up[c] = lax.ppermute(up[c], 'shard', backward)]
    ppermute x14 -> x21, starting transfers between devices: 24.7 us -> 12.3 us  [shards(): gate[c] = lax.ppermute(gate[c], 'shard', forward)]
    ppermute x8 -> x9, waiting for transfers between devices: 18 us -> 28.8 us  [exchange(): others.append(lax.ppermute(value, axis, [(i, i ^ mask) for i in range(n)]))]
    pallas_call x14 -> x21, Pallas kernels: 14.1 us -> 18.7 us  [put(): pl.pallas_call(functools.partial(put_kernel, step, lo, rows, n), in_specs...]
    ppermute x14 -> x21, waiting for transfers between devices: 49.4 us -> 54 us  [shards(): gate[c] = lax.ppermute(gate[c], 'shard', forward)]
    ppermute x8 -> x9, starting transfers between devices: 13.3 us -> 13 us  [exchange(): others.append(lax.ppermute(value, axis, [(i, i ^ mask) for i in range(n)]))]
  transfers between devices with their start and end apart: 36 -> 51, of which waited for: 17 -> 28; matrix products, arithmetic and copies ran while one was open for 0% -> 0% of each run, Pallas kernels for 8% -> 10%
where the time goes in v3:
time: 201 us
  waiting for transfers between devices  127 us (63%)
  starting transfers between devices  47.8 us (24%)
  Pallas kernels  24.9 us (12%)
    ppermute x21, waiting for transfers between devices, shards(): gate[c] = lax.ppermute(gate[c], 'shard', forward)  54 us
    ppermute x21, waiting for transfers between devices, shards(): up[c] = lax.ppermute(up[c], 'shard', backward)  44 us
    ppermute x9, waiting for transfers between devices, exchange(): others.append(lax.ppermute(value, axis, [(i, i ^ mask) for i in range(n)]))  28.8 us
    ppermute x21, starting transfers between devices, shards(): up[c] = lax.ppermute(up[c], 'shard', backward)  22.5 us
    pallas_call x21, Pallas kernels, put(): pl.pallas_call(functools.partial(put_kernel, step, lo, rows, n), in_specs...  18.7 us
    ppermute x9, starting transfers between devices, exchange(): others.append(lax.ppermute(value, axis, [(i, i ^ mask) for i in range(n)]))  13 us
    ppermute x21, starting transfers between devices, shards(): gate[c] = lax.ppermute(gate[c], 'shard', forward)  12.3 us
  transfers between devices with their start and end apart: 51, of which 28 were waited for; matrix products, arithmetic and copies ran while one was open for 0% of the time, Pallas kernels for 10%

profile of v3, /device:TPU:0, one launch (start us, length us, event | category | flops | bytes accessed | tf_op | source)
XLA Modules:
  0.0 201.1 jit_solution(4211878174813775666)
XLA Ops:
  0.7 3.9 %sums.1 = (f32[256,2048]{1,0:T(8,128)S(1)}, f32[256,2048]{1,0:T(8,128)S(1)}, f32[2,2048]{1,0:T(2,128)S(1)}) custom-call(f32[1,256]{1,0:T(1,128)} %bitcast.7, f32[256,2048]{1,0:T(8,128)} %one_g.1, f32[256,2048]{1,0:T(8,128)} %other_g.1, f32[256,2048]{1,0:T(8,128)} %one_u.1, f32[256,2048]{1,0:T(8,128)} %other_u.1), custom_call_target="tpu_custom_call" | custom-call | tf_op jit(solution)/shard_map/sums/pallas_call | solution.py:67
  4.6 3.0 %collective-permute-start = (f32[2,2048]{1,0:T(2,128)S(1)}, f32[2,2048]{1,0:T(2,128)S(1)}, u32[]{:S(2)}, u32[]{:S(2)}) collective-permute-start(f32[2,2048]{1,0:T(2,128)S(1)} %get-tuple-element.62.refs_0_), channel_id=1, source_target_pairs={{0,4},{4,0},{8,12},{12,8},{16,20},{20,16},{24,28},{28,24},{1,5},{5... | collective-permute-start | bytes 49160 | tf_op jit(solution)/shard_map/ppermute | solution.py:229
  7.6 1.7 collective-permute-done.refs_1_
  9.3 2.1 %collective-permute-start.1 = (f32[2,2048]{1,0:T(2,128)S(1)}, f32[2,2048]{1,0:T(2,128)S(1)}, u32[]{:S(2)}, u32[]{:S(2)}) collective-permute-start(f32[2,2048]{1,0:T(2,128)S(1)} %tree_add.7.refs_0_), channel_id=1, source_target_pairs={{0,8},{4,12},{8,0},{12,4},{16,24},{20,28},{24,16},{28,20},{1,9},{5... | collective-permute-start | bytes 49160 | tf_op jit(solution)/shard_map/ppermute | solution.py:229
  11.4 2.6 %collective-permute-start.2 = (f32[2,2048]{1,0:T(2,128)S(1)}, f32[2,2048]{1,0:T(2,128)S(1)}, u32[]{:S(2)}, u32[]{:S(2)}) collective-permute-start(f32[2,2048]{1,0:T(2,128)S(1)} %tree_add.7.refs_0_), channel_id=1, source_target_pairs={{0,16},{4,20},{8,24},{12,28},{16,0},{20,4},{24,8},{28,12},{1,17},{... | collective-permute-start | bytes 49160 | tf_op jit(solution)/shard_map/ppermute | solution.py:229
  14.0 2.0 %collective-permute-done.2.refs_2_ = f32[2,2048]{1,0:T(2,128)S(1)} collective-permute-done((f32[2,2048]{1,0:T(2,128)S(1)}, f32[2,2048]{1,0:T(2,128)S(1)}, u32[]{:S(2)}, u32[]{:S(2)}) %collective-permute-start.2) | collective-permute-done | bytes 16416 | tf_op jit(solution)/shard_map/ppermute | solution.py:229
  16.1 3.6 %collective-permute-done.3.refs_3_ = f32[2,2048]{1,0:T(2,128)S(1)} collective-permute-done((f32[2,2048]{1,0:T(2,128)S(1)}, f32[2,2048]{1,0:T(2,128)S(1)}, u32[]{:S(2)}, u32[]{:S(2)}) %collective-permute-start.3) | collective-permute-done | bytes 16416 | tf_op jit(solution)/shard_map/ppermute | solution.py:229
  20.0 2.0 %collective-permute-start.39 = (bf16[128,2048]{1,0:T(8,128)(2,1)S(1)}, bf16[128,2048]{1,0:T(8,128)(2,1)S(1)}, u32[]{:S(2)}, u32[]{:S(2)}) collective-permute-start(bf16[128,2048]{1,0:T(8,128)(2,1)S(1)} %get-tuple-element.68.refs_3_), channel_id=1, source_target_pairs={{8,0},{16,8},{24,16},{28,24},{20,28},{12,20},{4,12},{0,4},{9,1},{1... | collective-permute-start | bytes 1572872 | tf_op jit(solution)/shard_map/ppermute | solution.py:253
  22.0 10.1 %collective-permute-done.32.gate.refs_2_ = bf16[128,2048]{1,0:T(8,128)(2,1)S(1)} collective-permute-done((bf16[128,2048]{1,0:T(8,128)(2,1)S(1)}, bf16[128,2048]{1,0:T(8,128)(2,1)S(1)}, u32[]{:S(2)}, u32[]{:S(2)}) %collective-permute-start.32) | collective-permute-done | bytes 524320 | tf_op jit(solution)/shard_map/ppermute | solution.py:252
  32.1 2.0 collective-permute-start.40
  34.1 10.1 %collective-permute-done.33.gate.refs_2_ = bf16[128,2048]{1,0:T(8,128)(2,1)S(1)} collective-permute-done((bf16[128,2048]{1,0:T(8,128)(2,1)S(1)}, bf16[128,2048]{1,0:T(8,128)(2,1)S(1)}, u32[]{:S(2)}, u32[]{:S(2)}) %collective-permute-start.33) | collective-permute-done | bytes 524320 | tf_op jit(solution)/shard_map/ppermute | solution.py:252
  44.2 2.0 collective-permute-start.41
  46.5 1.0 collective-permute-done.46.refs_1_
  47.5 1.6 collective-permute-start.25
  49.1 1.5 collective-permute-start.47
  50.6 2.1 %collective-permute-done.47.refs_1_ = f32[1,2048]{1,0:T(1,128)S(1)} collective-permute-done((f32[1,2048]{1,0:T(1,128)S(1)}, f32[1,2048]{1,0:T(1,128)S(1)}, u32[]{:S(2)}, u32[]{:S(2)}) %collective-permute-start.47) | collective-permute-done | bytes 8224 | tf_op jit(solution)/shard_map/ppermute | solution.py:229
  52.7 0.9 collective-permute-start.11
  53.6 3.6 %collective-permute-done.34.gate.refs_2_ = bf16[128,2048]{1,0:T(8,128)(2,1)S(1)} collective-permute-done((bf16[128,2048]{1,0:T(8,128)(2,1)S(1)}, bf16[128,2048]{1,0:T(8,128)(2,1)S(1)}, u32[]{:S(2)}, u32[]{:S(2)}) %collective-permute-start.34) | collective-permute-done | bytes 524320 | tf_op jit(solution)/shard_map/ppermute | solution.py:252
  57.2 5.6 %collective-permute-done.18.gate = bf16[64,2048]{1,0:T(8,128)(2,1)S(1)} collective-permute-done((bf16[64,2048]{1,0:T(8,128)(2,1)S(1)}, bf16[64,2048]{1,0:T(8,128)(2,1)S(1)}, u32[]{:S(2)}, u32[]{:S(2)}) %collective-permute-start.18) | collective-permute-done | bytes 262176 | tf_op jit(solution)/shard_map/ppermute | solution.py:252
  62.9 2.1 %collective-permute-start.42 = (bf16[128,2048]{1,0:T(8,128)(2,1)S(1)}, bf16[128,2048]{1,0:T(8,128)(2,1)S(1)}, u32[]{:S(2)}, u32[]{:S(2)}) collective-permute-start(bf16[128,2048]{1,0:T(8,128)(2,1)S(1)} %collective-permute-done.41.up), channel_id=1, source_target_pairs={{8,0},{16,8},{24,16},{28,24},{20,28},{12,20},{4,12},{0,4},{9,1},{1... | collective-permute-start | bytes 1572872 | tf_op jit(solution)/shard_map/ppermute | solution.py:253
  64.9 2.8 %collective-permute-done.11.up = bf16[64,2048]{1,0:T(8,128)(2,1)S(1)} collective-permute-done((bf16[64,2048]{1,0:T(8,128)(2,1)S(1)}, bf16[64,2048]{1,0:T(8,128)(2,1)S(1)}, u32[]{:S(2)}, u32[]{:S(2)}) %collective-permute-start.11) | collective-permute-done | bytes 262176 | tf_op jit(solution)/shard_map/ppermute | solution.py:253
  67.8 2.4 %collective-permute-start.26 = (bf16[64,2048]{1,0:T(8,128)(2,1)S(1)}, bf16[64,2048]{1,0:T(8,128)(2,1)S(1)}, u32[]{:S(2)}, u32[]{:S(2)}) collective-permute-start(bf16[64,2048]{1,0:T(8,128)(2,1)S(1)} %collective-permute-done.25.up), channel_id=1, source_target_pairs={{8,0},{16,8},{24,16},{28,24},{20,28},{12,20},{4,12},{0,4},{9,1},{1... | collective-permute-start | bytes 786440 | tf_op jit(solution)/shard_map/ppermute | solution.py:253
  70.1 8.5 %collective-permute-done.4.gate = bf16[64,2048]{1,0:T(8,128)(2,1)S(1)} collective-permute-done((bf16[64,2048]{1,0:T(8,128)(2,1)S(1)}, bf16[64,2048]{1,0:T(8,128)(2,1)S(1)}, u32[]{:S(2)}, u32[]{:S(2)}) %collective-permute-start.4) | collective-permute-done | bytes 262176 | tf_op jit(solution)/shard_map/ppermute | solution.py:252
  78.6 1.6 collective-permute-start.12
  80.2 2.4 %collective-permute-done.19.gate = bf16[64,2048]{1,0:T(8,128)(2,1)S(1)} collective-permute-done((bf16[64,2048]{1,0:T(8,128)(2,1)S(1)}, bf16[64,2048]{1,0:T(8,128)(2,1)S(1)}, u32[]{:S(2)}, u32[]{:S(2)}) %collective-permute-start.19) | collective-permute-done | bytes 262176 | tf_op jit(solution)/shard_map/ppermute | solution.py:252
  82.6 1.7 collective-permute-done.26.up
  84.3 1.2 collective-permute-start.36
  85.5 2.0 collective-permute-done.12.up
  87.5 2.4 %collective-permute-start.27 = (bf16[64,2048]{1,0:T(8,128)(2,1)S(1)}, bf16[64,2048]{1,0:T(8,128)(2,1)S(1)}, u32[]{:S(2)}, u32[]{:S(2)}) collective-permute-start(bf16[64,2048]{1,0:T(8,128)(2,1)S(1)} %collective-permute-done.26.up), channel_id=1, source_target_pairs={{8,0},{16,8},{24,16},{28,24},{20,28},{12,20},{4,12},{0,4},{9,1},{1... | collective-permute-start | bytes 786440 | tf_op jit(solution)/shard_map/ppermute | solution.py:253
  89.9 1.9 collective-permute-done.5.gate
  91.8 1.6 collective-permute-start.48
  93.8 12.3 %collective-permute-done.48.refs_1_ = f32[1,2048]{1,0:T(1,128)S(1)} collective-permute-done((f32[1,2048]{1,0:T(1,128)S(1)}, f32[1,2048]{1,0:T(1,128)S(1)}, u32[]{:S(2)}, u32[]{:S(2)}) %collective-permute-start.48) | collective-permute-done | bytes 8224 | tf_op jit(solution)/shard_map/ppermute | solution.py:229
  106.1 2.0 %collective-permute-start.6 = (bf16[64,2048]{1,0:T(8,128)(2,1)S(1)}, bf16[64,2048]{1,0:T(8,128)(2,1)S(1)}, u32[]{:S(2)}, u32[]{:S(2)}) collective-permute-start(bf16[64,2048]{1,0:T(8,128)(2,1)S(1)} %collective-permute-done.5.gate), channel_id=1, source_target_pairs={{0,8},{8,16},{16,24},{24,28},{28,20},{20,12},{12,4},{4,0},{1,9},{9... | collective-permute-start | bytes 786440 | tf_op jit(solution)/shard_map/ppermute | solution.py:252
  108.2 7.1 %collective-permute-done.13.up = bf16[64,2048]{1,0:T(8,128)(2,1)S(1)} collective-permute-done((bf16[64,2048]{1,0:T(8,128)(2,1)S(1)}, bf16[64,2048]{1,0:T(8,128)(2,1)S(1)}, u32[]{:S(2)}, u32[]{:S(2)}) %collective-permute-start.13) | collective-permute-done | bytes 262176 | tf_op jit(solution)/shard_map/ppermute | solution.py:253
  115.3 2.1 %collective-permute-start.37 = (bf16[128,2048]{1,0:T(8,128)(2,1)S(1)}, bf16[128,2048]{1,0:T(8,128)(2,1)S(1)}, u32[]{:S(2)}, u32[]{:S(2)}) collective-permute-start(bf16[128,2048]{1,0:T(8,128)(2,1)S(1)} %collective-permute-done.36.gate), channel_id=1, source_target_pairs={{0,8},{8,16},{16,24},{24,28},{28,20},{20,12},{12,4},{4,0},{1,9},{9... | collective-permute-start | bytes 1572872 | tf_op jit(solution)/shard_map/ppermute | solution.py:252
  117.4 2.8 %collective-permute-done.21.gate = bf16[64,2048]{1,0:T(8,128)(2,1)S(1)} collective-permute-done((bf16[64,2048]{1,0:T(8,128)(2,1)S(1)}, bf16[64,2048]{1,0:T(8,128)(2,1)S(1)}, u32[]{:S(2)}, u32[]{:S(2)}) %collective-permute-start.21) | collective-permute-done | bytes 262176 | tf_op jit(solution)/shard_map/ppermute | solution.py:252
  120.2 2.3 %collective-permute-start.7 = (bf16[64,2048]{1,0:T(8,128)(2,1)S(1)}, bf16[64,2048]{1,0:T(8,128)(2,1)S(1)}, u32[]{:S(2)}, u32[]{:S(2)}) collective-permute-start(bf16[64,2048]{1,0:T(8,128)(2,1)S(1)} %collective-permute-done.6.gate), channel_id=1, source_target_pairs={{0,8},{8,16},{16,24},{24,28},{28,20},{20,12},{12,4},{4,0},{1,9},{9... | collective-permute-start | bytes 786440 | tf_op jit(solution)/shard_map/ppermute | solution.py:252
  122.5 1.9 collective-permute-done.28.up
  124.6 5.5 %collective-permute-done.14.up = bf16[64,2048]{1,0:T(8,128)(2,1)S(1)} collective-permute-done((bf16[64,2048]{1,0:T(8,128)(2,1)S(1)}, bf16[64,2048]{1,0:T(8,128)(2,1)S(1)}, u32[]{:S(2)}, u32[]{:S(2)}) %collective-permute-start.14) | collective-permute-done | bytes 262176 | tf_op jit(solution)/shard_map/ppermute | solution.py:253
  130.1 4.9 %collective-permute-done.7.gate = bf16[64,2048]{1,0:T(8,128)(2,1)S(1)} collective-permute-done((bf16[64,2048]{1,0:T(8,128)(2,1)S(1)}, bf16[64,2048]{1,0:T(8,128)(2,1)S(1)}, u32[]{:S(2)}, u32[]{:S(2)}) %collective-permute-start.7) | collective-permute-done | bytes 262176 | tf_op jit(solution)/shard_map/ppermute | solution.py:252
  135.0 2.1 %collective-permute-start.49 = (f32[1,2048]{1,0:T(1,128)S(1)}, f32[1,2048]{1,0:T(1,128)S(1)}, u32[]{:S(2)}, u32[]{:S(2)}) collective-permute-start(f32[1,2048]{1,0:T(1,128)S(1)} %tree_add.11.refs_0_), channel_id=1, source_target_pairs={{0,8},{4,12},{8,0},{12,4},{16,24},{20,28},{24,16},{28,20},{1,9},{5... | collective-permute-start | bytes 24584 | tf_op jit(solution)/shard_map/ppermute | solution.py:229
  137.1 6.0 %collective-permute-done.49.refs_1_ = f32[1,2048]{1,0:T(1,128)S(1)} collective-permute-done((f32[1,2048]{1,0:T(1,128)S(1)}, f32[1,2048]{1,0:T(1,128)S(1)}, u32[]{:S(2)}, u32[]{:S(2)}) %collective-permute-start.49) | collective-permute-done | bytes 8224 | tf_op jit(solution)/shard_map/ppermute | solution.py:229
  143.1 2.0 %collective-permute-start.8 = (bf16[64,2048]{1,0:T(8,128)(2,1)S(1)}, bf16[64,2048]{1,0:T(8,128)(2,1)S(1)}, u32[]{:S(2)}, u32[]{:S(2)}) collective-permute-start(bf16[64,2048]{1,0:T(8,128)(2,1)S(1)} %collective-permute-done.7.gate), channel_id=1, source_target_pairs={{0,8},{8,16},{16,24},{24,28},{28,20},{20,12},{12,4},{4,0},{1,9},{9... | collective-permute-start | bytes 786440 | tf_op jit(solution)/shard_map/ppermute | solution.py:252
  145.2 7.0 %collective-permute-done.15.up = bf16[64,2048]{1,0:T(8,128)(2,1)S(1)} collective-permute-done((bf16[64,2048]{1,0:T(8,128)(2,1)S(1)}, bf16[64,2048]{1,0:T(8,128)(2,1)S(1)}, u32[]{:S(2)}, u32[]{:S(2)}) %collective-permute-start.15) | collective-permute-done | bytes 262176 | tf_op jit(solution)/shard_map/ppermute | solution.py:253
  152.3 1.1 collective-permute-start.45
  153.4 4.1 %collective-permute-done.23.gate = bf16[64,2048]{1,0:T(8,128)(2,1)S(1)} collective-permute-done((bf16[64,2048]{1,0:T(8,128)(2,1)S(1)}, bf16[64,2048]{1,0:T(8,128)(2,1)S(1)}, u32[]{:S(2)}, u32[]{:S(2)}) %collective-permute-start.23) | collective-permute-done | bytes 262176 | tf_op jit(solution)/shard_map/ppermute | solution.py:252
  157.5 2.2 %collective-permute-start.9 = (bf16[64,2048]{1,0:T(8,128)(2,1)S(1)}, bf16[64,2048]{1,0:T(8,128)(2,1)S(1)}, u32[]{:S(2)}, u32[]{:S(2)}) collective-permute-start(bf16[64,2048]{1,0:T(8,128)(2,1)S(1)} %collective-permute-done.8.gate), channel_id=1, source_target_pairs={{0,8},{8,16},{16,24},{24,28},{28,20},{20,12},{12,4},{4,0},{1,9},{9... | collective-permute-start | bytes 786440 | tf_op jit(solution)/shard_map/ppermute | solution.py:252
  159.7 1.7 collective-permute-done.30.up
  161.4 14.1 %collective-permute-done.16.up = bf16[64,2048]{1,0:T(8,128)(2,1)S(1)} collective-permute-done((bf16[64,2048]{1,0:T(8,128)(2,1)S(1)}, bf16[64,2048]{1,0:T(8,128)(2,1)S(1)}, u32[]{:S(2)}, u32[]{:S(2)}) %collective-permute-start.16) | collective-permute-done | bytes 262176 | tf_op jit(solution)/shard_map/ppermute | solution.py:253
  175.5 2.0 %collective-permute-start.31 = (bf16[64,2048]{1,0:T(8,128)(2,1)S(1)}, bf16[64,2048]{1,0:T(8,128)(2,1)S(1)}, u32[]{:S(2)}, u32[]{:S(2)}) collective-permute-start(bf16[64,2048]{1,0:T(8,128)(2,1)S(1)} %collective-permute-done.30.up), channel_id=1, source_target_pairs={{8,0},{16,8},{24,16},{28,24},{20,28},{12,20},{4,12},{0,4},{9,1},{1... | collective-permute-start | bytes 786440 | tf_op jit(solution)/shard_map/ppermute | solution.py:253
  177.6 2.0 %collective-permute-start.17 = (bf16[64,2048]{1,0:T(8,128)(2,1)S(1)}, bf16[64,2048]{1,0:T(8,128)(2,1)S(1)}, u32[]{:S(2)}, u32[]{:S(2)}) collective-permute-start(bf16[64,2048]{1,0:T(8,128)(2,1)S(1)} %collective-permute-done.16.up), channel_id=1, source_target_pairs={{8,0},{16,8},{24,16},{28,24},{20,28},{12,20},{4,12},{0,4},{9,1},{1... | collective-permute-start | bytes 786440 | tf_op jit(solution)/shard_map/ppermute | solution.py:253
  179.6 1.4 start_outputs.1
  181.6 1.0 put.21
  182.5 0.8 put.22
  183.4 0.8 put.23
  184.2 1.0 put.24
  186.9 1.0 put.27
  187.9 0.8 put.28
  189.6 1.0 put.30
  193.0 1.0 put.33
  195.6 1.0 put.36
  196.7 0.8 put.37
  198.3 1.0 put.39
  200.3 0.8 put.41
  (76 shorter events, 10.4 us)
Async XLA Ops:
  0.6 45.6 %copy-start = (f32[64]{0:T(128)S(1)}, f32[64]{0:T(128)}, u32[]{:S(2)}) copy-start(f32[64]{0:T(128)} %param.12) | copy-start | bytes 772
  0.6 45.5 %copy-start.1 = (f32[64]{0:T(128)S(1)}, f32[64]{0:T(128)}, u32[]{:S(2)}) copy-start(f32[64]{0:T(128)} %param.13) | copy-start | bytes 772
  4.6 4.8 %collective-permute-start = (f32[2,2048]{1,0:T(2,128)S(1)}, f32[2,2048]{1,0:T(2,128)S(1)}, u32[]{:S(2)}, u32[]{:S(2)}) collective-permute-start(f32[2,2048]{1,0:T(2,128)S(1)} %get-tuple-element.62.refs_0_), channel_id=1, source_target_pairs={{0,4},{4,0},{8,12},{12,8},{16,20},{20,16},{24,28},{28,24},{1,5},{5... | collective-permute-start | bytes 49160 | tf_op jit(solution)/shard_map/ppermute | solution.py:229
  9.3 4.7 %collective-permute-start.1 = (f32[2,2048]{1,0:T(2,128)S(1)}, f32[2,2048]{1,0:T(2,128)S(1)}, u32[]{:S(2)}, u32[]{:S(2)}) collective-permute-start(f32[2,2048]{1,0:T(2,128)S(1)} %tree_add.7.refs_0_), channel_id=1, source_target_pairs={{0,8},{4,12},{8,0},{12,4},{16,24},{20,28},{24,16},{28,20},{1,9},{5... | collective-permute-start | bytes 49160 | tf_op jit(solution)/shard_map/ppermute | solution.py:229
  11.4 4.6 %collective-permute-start.2 = (f32[2,2048]{1,0:T(2,128)S(1)}, f32[2,2048]{1,0:T(2,128)S(1)}, u32[]{:S(2)}, u32[]{:S(2)}) collective-permute-start(f32[2,2048]{1,0:T(2,128)S(1)} %tree_add.7.refs_0_), channel_id=1, source_target_pairs={{0,16},{4,20},{8,24},{12,28},{16,0},{20,4},{24,8},{28,12},{1,17},{... | collective-permute-start | bytes 49160 | tf_op jit(solution)/shard_map/ppermute | solution.py:229
  14.0 5.7 %collective-permute-start.3 = (f32[2,2048]{1,0:T(2,128)S(1)}, f32[2,2048]{1,0:T(2,128)S(1)}, u32[]{:S(2)}, u32[]{:S(2)}) collective-permute-start(f32[2,2048]{1,0:T(2,128)S(1)} %tree_add.7.refs_0_), channel_id=1, source_target_pairs={{0,24},{4,28},{8,16},{12,20},{16,8},{20,12},{24,0},{28,4},{1,25},{... | collective-permute-start | bytes 49160 | tf_op jit(solution)/shard_map/ppermute | solution.py:229
  19.9 12.1 %collective-permute-start.32 = (bf16[128,2048]{1,0:T(8,128)(2,1)S(1)}, bf16[128,2048]{1,0:T(8,128)(2,1)S(1)}, u32[]{:S(2)}, u32[]{:S(2)}) collective-permute-start(bf16[128,2048]{1,0:T(8,128)(2,1)S(1)} %get-tuple-element.67.refs_0_), channel_id=1, source_target_pairs={{0,8},{8,16},{16,24},{24,28},{28,20},{20,12},{12,4},{4,0},{1,9},{9... | collective-permute-start | bytes 1572872 | tf_op jit(solution)/shard_map/ppermute | solution.py:252
  20.0 12.1 %collective-permute-start.39 = (bf16[128,2048]{1,0:T(8,128)(2,1)S(1)}, bf16[128,2048]{1,0:T(8,128)(2,1)S(1)}, u32[]{:S(2)}, u32[]{:S(2)}) collective-permute-start(bf16[128,2048]{1,0:T(8,128)(2,1)S(1)} %get-tuple-element.68.refs_3_), channel_id=1, source_target_pairs={{8,0},{16,8},{24,16},{28,24},{20,28},{12,20},{4,12},{0,4},{9,1},{1... | collective-permute-start | bytes 1572872 | tf_op jit(solution)/shard_map/ppermute | solution.py:253
  32.1 12.1 %collective-permute-start.33 = (bf16[128,2048]{1,0:T(8,128)(2,1)S(1)}, bf16[128,2048]{1,0:T(8,128)(2,1)S(1)}, u32[]{:S(2)}, u32[]{:S(2)}) collective-permute-start(bf16[128,2048]{1,0:T(8,128)(2,1)S(1)} %collective-permute-done.32.gate.refs_2_), channel_id=1, source_target_pairs={{0,8},{8,16},{16,24},{24,28},{28,20},{20,12},{12,4},{4,0},{1,9},{9... | collective-permute-start | bytes 1572872 | tf_op jit(solution)/shard_map/ppermute | solution.py:252
  32.1 12.1 %collective-permute-start.40 = (bf16[128,2048]{1,0:T(8,128)(2,1)S(1)}, bf16[128,2048]{1,0:T(8,128)(2,1)S(1)}, u32[]{:S(2)}, u32[]{:S(2)}) collective-permute-start(bf16[128,2048]{1,0:T(8,128)(2,1)S(1)} %collective-permute-done.39.up), channel_id=1, source_target_pairs={{8,0},{16,8},{24,16},{28,24},{20,28},{12,20},{4,12},{0,4},{9,1},{1... | collective-permute-start | bytes 1572872 | tf_op jit(solution)/shard_map/ppermute | solution.py:253
  44.2 13.1 %collective-permute-start.34 = (bf16[128,2048]{1,0:T(8,128)(2,1)S(1)}, bf16[128,2048]{1,0:T(8,128)(2,1)S(1)}, u32[]{:S(2)}, u32[]{:S(2)}) collective-permute-start(bf16[128,2048]{1,0:T(8,128)(2,1)S(1)} %collective-permute-done.33.gate.refs_2_), channel_id=1, source_target_pairs={{0,8},{8,16},{16,24},{24,28},{28,20},{20,12},{12,4},{4,0},{1,9},{9... | collective-permute-start | bytes 1572872 | tf_op jit(solution)/shard_map/ppermute | solution.py:252
  44.2 18.6 %collective-permute-start.41 = (bf16[128,2048]{1,0:T(8,128)(2,1)S(1)}, bf16[128,2048]{1,0:T(8,128)(2,1)S(1)}, u32[]{:S(2)}, u32[]{:S(2)}) collective-permute-start(bf16[128,2048]{1,0:T(8,128)(2,1)S(1)} %collective-permute-done.40.up), channel_id=1, source_target_pairs={{8,0},{16,8},{24,16},{28,24},{20,28},{12,20},{4,12},{0,4},{9,1},{1... | collective-permute-start | bytes 1572872 | tf_op jit(solution)/shard_map/ppermute | solution.py:253
  46.3 1.2 collective-permute-start.46
  46.3 16.5 %collective-permute-start.18 = (bf16[64,2048]{1,0:T(8,128)(2,1)S(1)}, bf16[64,2048]{1,0:T(8,128)(2,1)S(1)}, u32[]{:S(2)}, u32[]{:S(2)}) collective-permute-start(bf16[64,2048]{1,0:T(8,128)(2,1)S(1)} %get-tuple-element.65.refs_1_), channel_id=1, source_target_pairs={{0,8},{8,16},{16,24},{24,28},{28,20},{20,12},{12,4},{4,0},{1,9},{9... | collective-permute-start | bytes 786440 | tf_op jit(solution)/shard_map/ppermute | solution.py:252
  47.5 15.3 %collective-permute-start.25 = (bf16[64,2048]{1,0:T(8,128)(2,1)S(1)}, bf16[64,2048]{1,0:T(8,128)(2,1)S(1)}, u32[]{:S(2)}, u32[]{:S(2)}) collective-permute-start(bf16[64,2048]{1,0:T(8,128)(2,1)S(1)} %get-tuple-element.66.refs_4_), channel_id=1, source_target_pairs={{8,0},{16,8},{24,16},{28,24},{20,28},{12,20},{4,12},{0,4},{9,1},{1... | collective-permute-start | bytes 786440 | tf_op jit(solution)/shard_map/ppermute | solution.py:253
  49.1 3.7 %collective-permute-start.47 = (f32[1,2048]{1,0:T(1,128)S(1)}, f32[1,2048]{1,0:T(1,128)S(1)}, u32[]{:S(2)}, u32[]{:S(2)}) collective-permute-start(f32[1,2048]{1,0:T(1,128)S(1)} %tree_add.9.refs_0_), channel_id=1, source_target_pairs={{0,2},{1,3},{2,0},{3,1},{4,6},{5,7},{6,4},{7,5},{8,10},{9,11},{10,... | collective-permute-start | bytes 24584 | tf_op jit(solution)/shard_map/ppermute | solution.py:229
  52.7 15.0 %collective-permute-start.11 = (bf16[64,2048]{1,0:T(8,128)(2,1)S(1)}, bf16[64,2048]{1,0:T(8,128)(2,1)S(1)}, u32[]{:S(2)}, u32[]{:S(2)}) collective-permute-start(bf16[64,2048]{1,0:T(8,128)(2,1)S(1)} %get-tuple-element.64.refs_5_), channel_id=1, source_target_pairs={{8,0},{16,8},{24,16},{28,24},{20,28},{12,20},{4,12},{0,4},{9,1},{1... | collective-permute-start | bytes 786440 | tf_op jit(solution)/shard_map/ppermute | solution.py:253
  57.2 27.1 %collective-permute-start.35 = (bf16[128,2048]{1,0:T(8,128)(2,1)S(1)}, bf16[128,2048]{1,0:T(8,128)(2,1)S(1)}, u32[]{:S(2)}, u32[]{:S(2)}) collective-permute-start(bf16[128,2048]{1,0:T(8,128)(2,1)S(1)} %collective-permute-done.34.gate.refs_2_), channel_id=1, source_target_pairs={{0,8},{8,16},{16,24},{24,28},{28,20},{20,12},{12,4},{4,0},{1,9},{9... | collective-permute-start | bytes 1572872 | tf_op jit(solution)/shard_map/ppermute | solution.py:252
  62.8 15.8 %collective-permute-start.4 = (bf16[64,2048]{1,0:T(8,128)(2,1)S(1)}, bf16[64,2048]{1,0:T(8,128)(2,1)S(1)}, u32[]{:S(2)}, u32[]{:S(2)}) collective-permute-start(bf16[64,2048]{1,0:T(8,128)(2,1)S(1)} %get-tuple-element.63.refs_2_), channel_id=1, source_target_pairs={{0,8},{8,16},{16,24},{24,28},{28,20},{20,12},{12,4},{4,0},{1,9},{9... | collective-permute-start | bytes 786440 | tf_op jit(solution)/shard_map/ppermute | solution.py:252
  62.9 19.8 %collective-permute-start.19 = (bf16[64,2048]{1,0:T(8,128)(2,1)S(1)}, bf16[64,2048]{1,0:T(8,128)(2,1)S(1)}, u32[]{:S(2)}, u32[]{:S(2)}) collective-permute-start(bf16[64,2048]{1,0:T(8,128)(2,1)S(1)} %collective-permute-done.18.gate), channel_id=1, source_target_pairs={{0,8},{8,16},{16,24},{24,28},{28,20},{20,12},{12,4},{4,0},{1,9},{9... | collective-permute-start | bytes 786440 | tf_op jit(solution)/shard_map/ppermute | solution.py:252
  62.9 30.5 %collective-permute-start.42 = (bf16[128,2048]{1,0:T(8,128)(2,1)S(1)}, bf16[128,2048]{1,0:T(8,128)(2,1)S(1)}, u32[]{:S(2)}, u32[]{:S(2)}) collective-permute-start(bf16[128,2048]{1,0:T(8,128)(2,1)S(1)} %collective-permute-done.41.up), channel_id=1, source_target_pairs={{8,0},{16,8},{24,16},{28,24},{20,28},{12,20},{4,12},{0,4},{9,1},{1... | collective-permute-start | bytes 1572872 | tf_op jit(solution)/shard_map/ppermute | solution.py:253
  67.8 16.5 %collective-permute-start.26 = (bf16[64,2048]{1,0:T(8,128)(2,1)S(1)}, bf16[64,2048]{1,0:T(8,128)(2,1)S(1)}, u32[]{:S(2)}, u32[]{:S(2)}) collective-permute-start(bf16[64,2048]{1,0:T(8,128)(2,1)S(1)} %collective-permute-done.25.up), channel_id=1, source_target_pairs={{8,0},{16,8},{24,16},{28,24},{20,28},{12,20},{4,12},{0,4},{9,1},{1... | collective-permute-start | bytes 786440 | tf_op jit(solution)/shard_map/ppermute | solution.py:253
  78.6 8.9 %collective-permute-start.12 = (bf16[64,2048]{1,0:T(8,128)(2,1)S(1)}, bf16[64,2048]{1,0:T(8,128)(2,1)S(1)}, u32[]{:S(2)}, u32[]{:S(2)}) collective-permute-start(bf16[64,2048]{1,0:T(8,128)(2,1)S(1)} %collective-permute-done.11.up), channel_id=1, source_target_pairs={{8,0},{16,8},{24,16},{28,24},{20,28},{12,20},{4,12},{0,4},{9,1},{1... | collective-permute-start | bytes 786440 | tf_op jit(solution)/shard_map/ppermute | solution.py:253
  82.6 9.2 %collective-permute-start.5 = (bf16[64,2048]{1,0:T(8,128)(2,1)S(1)}, bf16[64,2048]{1,0:T(8,128)(2,1)S(1)}, u32[]{:S(2)}, u32[]{:S(2)}) collective-permute-start(bf16[64,2048]{1,0:T(8,128)(2,1)S(1)} %collective-permute-done.4.gate), channel_id=1, source_target_pairs={{0,8},{8,16},{16,24},{24,28},{28,20},{20,12},{12,4},{4,0},{1,9},{9... | collective-permute-start | bytes 786440 | tf_op jit(solution)/shard_map/ppermute | solution.py:252
  84.3 21.8 %collective-permute-start.20 = (bf16[64,2048]{1,0:T(8,128)(2,1)S(1)}, bf16[64,2048]{1,0:T(8,128)(2,1)S(1)}, u32[]{:S(2)}, u32[]{:S(2)}) collective-permute-start(bf16[64,2048]{1,0:T(8,128)(2,1)S(1)} %collective-permute-done.19.gate), channel_id=1, source_target_pairs={{0,8},{8,16},{16,24},{24,28},{28,20},{20,12},{12,4},{4,0},{1,9},{9... | collective-permute-start | bytes 786440 | tf_op jit(solution)/shard_map/ppermute | solution.py:252
  84.3 31.0 %collective-permute-start.36 = (bf16[128,2048]{1,0:T(8,128)(2,1)S(1)}, bf16[128,2048]{1,0:T(8,128)(2,1)S(1)}, u32[]{:S(2)}, u32[]{:S(2)}) collective-permute-start(bf16[128,2048]{1,0:T(8,128)(2,1)S(1)} %collective-permute-done.35.gate.refs_2_), channel_id=1, source_target_pairs={{0,8},{8,16},{16,24},{24,28},{28,20},{20,12},{12,4},{4,0},{1,9},{9... | collective-permute-start | bytes 1572872 | tf_op jit(solution)/shard_map/ppermute | solution.py:252
  87.5 20.6 %collective-permute-start.27 = (bf16[64,2048]{1,0:T(8,128)(2,1)S(1)}, bf16[64,2048]{1,0:T(8,128)(2,1)S(1)}, u32[]{:S(2)}, u32[]{:S(2)}) collective-permute-start(bf16[64,2048]{1,0:T(8,128)(2,1)S(1)} %collective-permute-done.26.up), channel_id=1, source_target_pairs={{8,0},{16,8},{24,16},{28,24},{20,28},{12,20},{4,12},{0,4},{9,1},{1... | collective-permute-start | bytes 786440 | tf_op jit(solution)/shard_map/ppermute | solution.py:253
  91.8 14.3 %collective-permute-start.48 = (f32[1,2048]{1,0:T(1,128)S(1)}, f32[1,2048]{1,0:T(1,128)S(1)}, u32[]{:S(2)}, u32[]{:S(2)}) collective-permute-start(f32[1,2048]{1,0:T(1,128)S(1)} %tree_add.10.refs_0_), channel_id=1, source_target_pairs={{0,4},{4,0},{8,12},{12,8},{16,20},{20,16},{24,28},{28,24},{1,5},{5... | collective-permute-start | bytes 24584 | tf_op jit(solution)/shard_map/ppermute | solution.py:229
  93.4 29.2 %collective-permute-start.43 = (bf16[128,2048]{1,0:T(8,128)(2,1)S(1)}, bf16[128,2048]{1,0:T(8,128)(2,1)S(1)}, u32[]{:S(2)}, u32[]{:S(2)}) collective-permute-start(bf16[128,2048]{1,0:T(8,128)(2,1)S(1)} %collective-permute-done.42.up), channel_id=1, source_target_pairs={{8,0},{16,8},{24,16},{28,24},{20,28},{12,20},{4,12},{0,4},{9,1},{1... | collective-permute-start | bytes 1572872 | tf_op jit(solution)/shard_map/ppermute | solution.py:253
  106.1 9.2 %collective-permute-start.13 = (bf16[64,2048]{1,0:T(8,128)(2,1)S(1)}, bf16[64,2048]{1,0:T(8,128)(2,1)S(1)}, u32[]{:S(2)}, u32[]{:S(2)}) collective-permute-start(bf16[64,2048]{1,0:T(8,128)(2,1)S(1)} %collective-permute-done.12.up), channel_id=1, source_target_pairs={{8,0},{16,8},{24,16},{28,24},{20,28},{12,20},{4,12},{0,4},{9,1},{1... | collective-permute-start | bytes 786440 | tf_op jit(solution)/shard_map/ppermute | solution.py:253
  106.1 9.2 %collective-permute-start.6 = (bf16[64,2048]{1,0:T(8,128)(2,1)S(1)}, bf16[64,2048]{1,0:T(8,128)(2,1)S(1)}, u32[]{:S(2)}, u32[]{:S(2)}) collective-permute-start(bf16[64,2048]{1,0:T(8,128)(2,1)S(1)} %collective-permute-done.5.gate), channel_id=1, source_target_pairs={{0,8},{8,16},{16,24},{24,28},{28,20},{20,12},{12,4},{4,0},{1,9},{9... | collective-permute-start | bytes 786440 | tf_op jit(solution)/shard_map/ppermute | solution.py:252
  108.1 12.1 %collective-permute-start.21 = (bf16[64,2048]{1,0:T(8,128)(2,1)S(1)}, bf16[64,2048]{1,0:T(8,128)(2,1)S(1)}, u32[]{:S(2)}, u32[]{:S(2)}) collective-permute-start(bf16[64,2048]{1,0:T(8,128)(2,1)S(1)} %collective-permute-done.20.gate), channel_id=1, source_target_pairs={{0,8},{8,16},{16,24},{24,28},{28,20},{20,12},{12,4},{4,0},{1,9},{9... | collective-permute-start | bytes 786440 | tf_op jit(solution)/shard_map/ppermute | solution.py:252
  115.3 9.2 %collective-permute-start.28 = (bf16[64,2048]{1,0:T(8,128)(2,1)S(1)}, bf16[64,2048]{1,0:T(8,128)(2,1)S(1)}, u32[]{:S(2)}, u32[]{:S(2)}) collective-permute-start(bf16[64,2048]{1,0:T(8,128)(2,1)S(1)} %collective-permute-done.27.up), channel_id=1, source_target_pairs={{8,0},{16,8},{24,16},{28,24},{20,28},{12,20},{4,12},{0,4},{9,1},{1... | collective-permute-start | bytes 786440 | tf_op jit(solution)/shard_map/ppermute | solution.py:253
  115.3 14.8 %collective-permute-start.14 = (bf16[64,2048]{1,0:T(8,128)(2,1)S(1)}, bf16[64,2048]{1,0:T(8,128)(2,1)S(1)}, u32[]{:S(2)}, u32[]{:S(2)}) collective-permute-start(bf16[64,2048]{1,0:T(8,128)(2,1)S(1)} %collective-permute-done.13.up), channel_id=1, source_target_pairs={{8,0},{16,8},{24,16},{28,24},{20,28},{12,20},{4,12},{0,4},{9,1},{1... | collective-permute-start | bytes 786440 | tf_op jit(solution)/shard_map/ppermute | solution.py:253
  115.3 29.9 %collective-permute-start.37 = (bf16[128,2048]{1,0:T(8,128)(2,1)S(1)}, bf16[128,2048]{1,0:T(8,128)(2,1)S(1)}, u32[]{:S(2)}, u32[]{:S(2)}) collective-permute-start(bf16[128,2048]{1,0:T(8,128)(2,1)S(1)} %collective-permute-done.36.gate), channel_id=1, source_target_pairs={{0,8},{8,16},{16,24},{24,28},{28,20},{20,12},{12,4},{4,0},{1,9},{9... | collective-permute-start | bytes 1572872 | tf_op jit(solution)/shard_map/ppermute | solution.py:252
  120.2 14.8 %collective-permute-start.7 = (bf16[64,2048]{1,0:T(8,128)(2,1)S(1)}, bf16[64,2048]{1,0:T(8,128)(2,1)S(1)}, u32[]{:S(2)}, u32[]{:S(2)}) collective-permute-start(bf16[64,2048]{1,0:T(8,128)(2,1)S(1)} %collective-permute-done.6.gate), channel_id=1, source_target_pairs={{0,8},{8,16},{16,24},{24,28},{28,20},{20,12},{12,4},{4,0},{1,9},{9... | collective-permute-start | bytes 786440 | tf_op jit(solution)/shard_map/ppermute | solution.py:252
  122.5 29.7 %collective-permute-start.44 = (bf16[128,2048]{1,0:T(8,128)(2,1)S(1)}, bf16[128,2048]{1,0:T(8,128)(2,1)S(1)}, u32[]{:S(2)}, u32[]{:S(2)}) collective-permute-start(bf16[128,2048]{1,0:T(8,128)(2,1)S(1)} %collective-permute-done.43.up), channel_id=1, source_target_pairs={{8,0},{16,8},{24,16},{28,24},{20,28},{12,20},{4,12},{0,4},{9,1},{1... | collective-permute-start | bytes 1572872 | tf_op jit(solution)/shard_map/ppermute | solution.py:253
  124.5 18.6 %collective-permute-start.22 = (bf16[64,2048]{1,0:T(8,128)(2,1)S(1)}, bf16[64,2048]{1,0:T(8,128)(2,1)S(1)}, u32[]{:S(2)}, u32[]{:S(2)}) collective-permute-start(bf16[64,2048]{1,0:T(8,128)(2,1)S(1)} %collective-permute-done.21.gate), channel_id=1, source_target_pairs={{0,8},{8,16},{16,24},{24,28},{28,20},{20,12},{12,4},{4,0},{1,9},{9... | collective-permute-start | bytes 786440 | tf_op jit(solution)/shard_map/ppermute | solution.py:252
  130.1 15.0 %collective-permute-start.29 = (bf16[64,2048]{1,0:T(8,128)(2,1)S(1)}, bf16[64,2048]{1,0:T(8,128)(2,1)S(1)}, u32[]{:S(2)}, u32[]{:S(2)}) collective-permute-start(bf16[64,2048]{1,0:T(8,128)(2,1)S(1)} %collective-permute-done.28.up), channel_id=1, source_target_pairs={{8,0},{16,8},{24,16},{28,24},{20,28},{12,20},{4,12},{0,4},{9,1},{1... | collective-permute-start | bytes 786440 | tf_op jit(solution)/shard_map/ppermute | solution.py:253
  135.0 8.1 %collective-permute-start.49 = (f32[1,2048]{1,0:T(1,128)S(1)}, f32[1,2048]{1,0:T(1,128)S(1)}, u32[]{:S(2)}, u32[]{:S(2)}) collective-permute-start(f32[1,2048]{1,0:T(1,128)S(1)} %tree_add.11.refs_0_), channel_id=1, source_target_pairs={{0,8},{4,12},{8,0},{12,4},{16,24},{20,28},{24,16},{28,20},{1,9},{5... | collective-permute-start | bytes 24584 | tf_op jit(solution)/shard_map/ppermute | solution.py:229
  143.1 9.2 %collective-permute-start.15 = (bf16[64,2048]{1,0:T(8,128)(2,1)S(1)}, bf16[64,2048]{1,0:T(8,128)(2,1)S(1)}, u32[]{:S(2)}, u32[]{:S(2)}) collective-permute-start(bf16[64,2048]{1,0:T(8,128)(2,1)S(1)} %collective-permute-done.14.up), channel_id=1, source_target_pairs={{8,0},{16,8},{24,16},{28,24},{20,28},{12,20},{4,12},{0,4},{9,1},{1... | collective-permute-start | bytes 786440 | tf_op jit(solution)/shard_map/ppermute | solution.py:253
  143.1 10.3 %collective-permute-start.8 = (bf16[64,2048]{1,0:T(8,128)(2,1)S(1)}, bf16[64,2048]{1,0:T(8,128)(2,1)S(1)}, u32[]{:S(2)}, u32[]{:S(2)}) collective-permute-start(bf16[64,2048]{1,0:T(8,128)(2,1)S(1)} %collective-permute-done.7.gate), channel_id=1, source_target_pairs={{0,8},{8,16},{16,24},{24,28},{28,20},{20,12},{12,4},{4,0},{1,9},{9... | collective-permute-start | bytes 786440 | tf_op jit(solution)/shard_map/ppermute | solution.py:252
  145.1 12.4 %collective-permute-start.23 = (bf16[64,2048]{1,0:T(8,128)(2,1)S(1)}, bf16[64,2048]{1,0:T(8,128)(2,1)S(1)}, u32[]{:S(2)}, u32[]{:S(2)}) collective-permute-start(bf16[64,2048]{1,0:T(8,128)(2,1)S(1)} %collective-permute-done.22.gate), channel_id=1, source_target_pairs={{0,8},{8,16},{16,24},{24,28},{28,20},{20,12},{12,4},{4,0},{1,9},{9... | collective-permute-start | bytes 786440 | tf_op jit(solution)/shard_map/ppermute | solution.py:252
  145.2 32.4 %collective-permute-start.38 = (bf16[128,2048]{1,0:T(8,128)(2,1)S(1)}, bf16[128,2048]{1,0:T(8,128)(2,1)S(1)}, u32[]{:S(2)}, u32[]{:S(2)}) collective-permute-start(bf16[128,2048]{1,0:T(8,128)(2,1)S(1)} %collective-permute-done.37.gate), channel_id=1, source_target_pairs={{0,8},{8,16},{16,24},{24,28},{28,20},{20,12},{12,4},{4,0},{1,9},{9... | collective-permute-start | bytes 1572872 | tf_op jit(solution)/shard_map/ppermute | solution.py:252
  152.2 9.1 %collective-permute-start.30 = (bf16[64,2048]{1,0:T(8,128)(2,1)S(1)}, bf16[64,2048]{1,0:T(8,128)(2,1)S(1)}, u32[]{:S(2)}, u32[]{:S(2)}) collective-permute-start(bf16[64,2048]{1,0:T(8,128)(2,1)S(1)} %collective-permute-done.29.up), channel_id=1, source_target_pairs={{8,0},{16,8},{24,16},{28,24},{20,28},{12,20},{4,12},{0,4},{9,1},{1... | collective-permute-start | bytes 786440 | tf_op jit(solution)/shard_map/ppermute | solution.py:253
  152.3 46.1 %collective-permute-start.45 = (bf16[128,2048]{1,0:T(8,128)(2,1)S(1)}, bf16[128,2048]{1,0:T(8,128)(2,1)S(1)}, u32[]{:S(2)}, u32[]{:S(2)}) collective-permute-start(bf16[128,2048]{1,0:T(8,128)(2,1)S(1)} %collective-permute-done.44.up), channel_id=1, source_target_pairs={{8,0},{16,8},{24,16},{28,24},{20,28},{12,20},{4,12},{0,4},{9,1},{1... | collective-permute-start | bytes 1572872 | tf_op jit(solution)/shard_map/ppermute | solution.py:253
  153.4 22.1 %collective-permute-start.16 = (bf16[64,2048]{1,0:T(8,128)(2,1)S(1)}, bf16[64,2048]{1,0:T(8,128)(2,1)S(1)}, u32[]{:S(2)}, u32[]{:S(2)}) collective-permute-start(bf16[64,2048]{1,0:T(8,128)(2,1)S(1)} %collective-permute-done.15.up), channel_id=1, source_target_pairs={{8,0},{16,8},{24,16},{28,24},{20,28},{12,20},{4,12},{0,4},{9,1},{1... | collective-permute-start | bytes 786440 | tf_op jit(solution)/shard_map/ppermute | solution.py:253
  157.5 18.0 %collective-permute-start.9 = (bf16[64,2048]{1,0:T(8,128)(2,1)S(1)}, bf16[64,2048]{1,0:T(8,128)(2,1)S(1)}, u32[]{:S(2)}, u32[]{:S(2)}) collective-permute-start(bf16[64,2048]{1,0:T(8,128)(2,1)S(1)} %collective-permute-done.8.gate), channel_id=1, source_target_pairs={{0,8},{8,16},{16,24},{24,28},{28,20},{20,12},{12,4},{4,0},{1,9},{9... | collective-permute-start | bytes 786440 | tf_op jit(solution)/shard_map/ppermute | solution.py:252
  161.4 16.2 %collective-permute-start.50 = (f32[1,2048]{1,0:T(1,128)S(1)}, f32[1,2048]{1,0:T(1,128)S(1)}, u32[]{:S(2)}, u32[]{:S(2)}) collective-permute-start(f32[1,2048]{1,0:T(1,128)S(1)} %tree_add.12.refs_0_), channel_id=1, source_target_pairs={{0,16},{4,20},{8,24},{12,28},{16,0},{20,4},{24,8},{28,12},{1,17},{... | collective-permute-start | bytes 24584 | tf_op jit(solution)/shard_map/ppermute | solution.py:229
  175.5 23.9 %collective-permute-start.24 = (bf16[64,2048]{1,0:T(8,128)(2,1)S(1)}, bf16[64,2048]{1,0:T(8,128)(2,1)S(1)}, u32[]{:S(2)}, u32[]{:S(2)}) collective-permute-start(bf16[64,2048]{1,0:T(8,128)(2,1)S(1)} %collective-permute-done.23.gate), channel_id=1, source_target_pairs={{0,8},{8,16},{16,24},{24,28},{28,20},{20,12},{12,4},{4,0},{1,9},{9... | collective-permute-start | bytes 786440 | tf_op jit(solution)/shard_map/ppermute | solution.py:252
  175.5 23.9 %collective-permute-start.31 = (bf16[64,2048]{1,0:T(8,128)(2,1)S(1)}, bf16[64,2048]{1,0:T(8,128)(2,1)S(1)}, u32[]{:S(2)}, u32[]{:S(2)}) collective-permute-start(bf16[64,2048]{1,0:T(8,128)(2,1)S(1)} %collective-permute-done.30.up), channel_id=1, source_target_pairs={{8,0},{16,8},{24,16},{28,24},{20,28},{12,20},{4,12},{0,4},{9,1},{1... | collective-permute-start | bytes 786440 | tf_op jit(solution)/shard_map/ppermute | solution.py:253
  177.5 22.7 %collective-permute-start.10 = (bf16[64,2048]{1,0:T(8,128)(2,1)S(1)}, bf16[64,2048]{1,0:T(8,128)(2,1)S(1)}, u32[]{:S(2)}, u32[]{:S(2)}) collective-permute-start(bf16[64,2048]{1,0:T(8,128)(2,1)S(1)} %collective-permute-done.9.gate), channel_id=1, source_target_pairs={{0,8},{8,16},{16,24},{24,28},{28,20},{20,12},{12,4},{4,0},{1,9},{9... | collective-permute-start | bytes 786440 | tf_op jit(solution)/shard_map/ppermute | solution.py:252
  177.6 22.7 %collective-permute-start.17 = (bf16[64,2048]{1,0:T(8,128)(2,1)S(1)}, bf16[64,2048]{1,0:T(8,128)(2,1)S(1)}, u32[]{:S(2)}, u32[]{:S(2)}) collective-permute-start(bf16[64,2048]{1,0:T(8,128)(2,1)S(1)} %collective-permute-done.16.up), channel_id=1, source_target_pairs={{8,0},{16,8},{24,16},{28,24},{20,28},{12,20},{4,12},{0,4},{9,1},{1... | collective-permute-start | bytes 786440 | tf_op jit(solution)/shard_map/ppermute | solution.py:253

commit v4 on v3

--- a/solution.py
+++ b/solution.py
@@ -9,7 +9,8 @@
 
 WHOLE = pl.BlockSpec(memory_space=pltpu.VMEM)
 OUTSIDE = pl.BlockSpec(memory_space=pl.ANY)
-GRANT = 48
+GRANT = 47
+EARLY = 16
 MOST = 2
 
 
@@ -29,18 +30,19 @@
 def cuts(rows):
     if rows < 256:
         return [(0, rows)]
-    edges = [0, rows // 2, 3 * rows // 4, rows]
+    edges = [0, EARLY, EARLY + 16 * ((rows - EARLY) // 32), rows]
     return list(zip(edges[:-1], edges[1:]))
 
 
-def sums_kernel(edges, share, one_g, other_g, one_u, other_u, fresh_g, fresh_u, sums, held, shares, sems, share_sem):
+def sums_kernel(edges, share, one_g, other_g, one_u, other_u, fresh_g, fresh_u, sums, *refs):
+    early, (held, shares, sems, share_sem) = refs[:-4], refs[-4:]
     rows, cols = fresh_g.shape
     spans = list(zip(edges[:-1], edges[1:]))
     first = pltpu.make_async_copy(share, shares, share_sem)
     first.start()
     for p, (lo, hi) in enumerate(spans):
         for k, source in enumerate((one_g, other_g, one_u, other_u)):
-            pltpu.make_async_copy(source.at[pl.ds(lo, hi - lo)], held.at[k, pl.ds(lo, hi - lo)], sems.at[p]).start()
+            pltpu.make_async_copy(source.at[pl.ds(lo, hi - lo)], held.at[k, pl.ds(lo, hi - lo)], sems.at[p]).start(priority=k % 2)
     first.wait()
     row = lax.broadcasted_iota(jnp.int32, (rows, rows), 0)
     lane = lax.broadcasted_iota(jnp.int32, (rows, rows), 1)
@@ -55,6 +57,8 @@
             for side, fresh in ((0, fresh_g), (1, fresh_u)):
                 value = m * held[2 * side, r:r + 8] + w * held[2 * side + 1, r:r + 8]
                 fresh[r:r + 8] = value
+                if early and r < early[side].shape[0]:
+                    early[side][r:r + 8] = value
                 total[side] = total[side] + value * value
     sums[0:1] = jnp.sum(total[0], axis=0, keepdims=True)
     sums[1:2] = jnp.sum(total[1], axis=0, keepdims=True)
@@ -64,11 +68,12 @@
     rows, cols = one_gate.shape
     edges = [0, rows] if rows < 256 else [0, rows // 4, rows // 2, 3 * rows // 4, rows]
     wide = jax.ShapeDtypeStruct((rows, cols), jnp.float32)
+    early = [jax.ShapeDtypeStruct((EARLY, cols), jnp.float32)] * 2 if rows >= 256 else []
     return pl.pallas_call(
         functools.partial(sums_kernel, edges),
         in_specs=[OUTSIDE] * 5,
-        out_specs=[WHOLE] * 3,
-        out_shape=[wide, wide, jax.ShapeDtypeStruct((2, cols), jnp.float32)],
+        out_specs=[WHOLE] * (3 + len(early)),
+        out_shape=[wide, wide, jax.ShapeDtypeStruct((2, cols), jnp.float32)] + early,
         scratch_shapes=[
             pltpu.VMEM((4, rows, cols), jnp.float32),
             pltpu.VMEM(share.shape, jnp.float32),
@@ -100,6 +105,25 @@
         name="narrow",
     )(fresh_gate, fresh_up, total)
     return list(pieces[:len(spans)]), list(pieces[len(spans):])
+
+
+def late_kernel(early_g, early_u, total_ref, gate, up):
+    for side, early, out in ((0, early_g, gate), (1, early_u, up)):
+        scale = 1.0 / jnp.sqrt(total_ref[side:side + 1])
+        for r in range(0, out.shape[0], 16):
+            out[r:r + 16] = (early[r:r + 16] * scale).astype(jnp.bfloat16)
+
+
+def narrow_late(early_gate, early_up, total):
+    shape = jax.ShapeDtypeStruct(early_gate.shape, jnp.bfloat16)
+    return pl.pallas_call(
+        late_kernel,
+        in_specs=[WHOLE] * 3,
+        out_specs=[WHOLE] * 2,
+        out_shape=[shape, shape],
+        compiler_params=grant(4),
+        name="narrow_late",
+    )(early_gate, early_up, total)
 
 
 def root_kernel(total_ref, factor_g, factor_u):
@@ -237,22 +261,28 @@
     forward = [(order[i], order[(i + 1) % n]) for i in range(n)]
     backward = [(b, a) for a, b in forward]
     spans = cuts(rows)
-    fresh_gate, fresh_up, total = sums_of(mix_share[None], one_gate, other_gate, one_up, other_up)
+    fresh_gate, fresh_up, total, *early = sums_of(mix_share[None], one_gate, other_gate, one_up, other_up)
+    if early:
+        early[0] = lax.ppermute(early[0], "shard", forward)
+        early[1] = lax.ppermute(early[1], "shard", backward)
     norm = slot_of(norm_train[None], norm_step[None], n * t, t)
     for masks in stages_of(n, MOST):
         total = exchange(total, "shard", n, masks)
     gate, up = narrow(spans, fresh_gate, fresh_up, total)
     factor_gate, factor_up = roots(total)
     outs = start_outputs(spans, gate, up, n)
-    left = [("tp", t, masks) for masks in stages_of(t, 1)] + [("shard", n, masks) for masks in stages_of(n, 1)]
-    norm = exchange(norm, *left[0])
-    stage = 1
+    left = [("tp", t, masks) for masks in stages_of(t, 1)]
+    left = left[1:] + [("shard", n, masks) for masks in stages_of(n, 1)] + left[:1]
+    stage = 0
     for step in range(1, n):
         for c, (lo, hi) in enumerate(spans):
-            gate[c] = lax.ppermute(gate[c], "shard", forward)
-            up[c] = lax.ppermute(up[c], "shard", backward)
+            if early and (step, c) == (1, 0):
+                gate[c], up[c] = narrow_late(*early, total)
+            else:
+                gate[c] = lax.ppermute(gate[c], "shard", forward)
+                up[c] = lax.ppermute(up[c], "shard", backward)
             outs = put(step, lo, rows, n, gate[c], up[c], outs)
-        if stage < len(left):
+        if step > 1 and stage < len(left) - 1:
             norm = exchange(norm, *left[stage], (gate[0],))
             stage += 1
     for axis, size, masks in left[stage:]:

time: 201 us -> 232 us (1.15)
  waiting for transfers between devices: 127 us -> 147 us
  starting transfers between devices: 47.8 us -> 58.5 us
    ppermute x21 -> x20, waiting for transfers between devices: 54 us -> 98.2 us  [shards(): gate[c] = lax.ppermute(gate[c], 'shard', forward)]
    ppermute x21 -> x20, waiting for transfers between devices: 44 us -> 11.1 us  [shards(): up[c] = lax.ppermute(up[c], 'shard', backward)]
    ppermute x0 -> x2, waiting for transfers between devices: none -> 18.2 us  [the longest x1 10.6 us: shards(): early[0] = lax.ppermute(early[0], 'shard', forward)]
    ppermute x21 -> x20, starting transfers between devices: 22.5 us -> 37.1 us  [shards(): up[c] = lax.ppermute(up[c], 'shard', backward)]
    ppermute x9, waiting for transfers between devices: 28.8 us -> 19.7 us  [exchange(): others.append(lax.ppermute(value, axis, [(i, i ^ mask) for i in range(n)]))]
    ppermute x21 -> x20, starting transfers between devices: 12.3 us -> 6.7 us  [shards(): gate[c] = lax.ppermute(gate[c], 'shard', forward)]
  transfers between devices with their start and end apart: 51 -> 51, of which waited for: 28 -> 39; matrix products, arithmetic and copies ran while one was open for 0% -> 0% of each run, Pallas kernels for 10% -> 9%
where the time goes in v4:
time: 232 us
  waiting for transfers between devices  147 us (63%)
  starting transfers between devices  58.5 us (25%)
  Pallas kernels  24.7 us (11%)
    ppermute x20, waiting for transfers between devices, shards(): gate[c] = lax.ppermute(gate[c], 'shard', forward)  98.2 us
    ppermute x20, starting transfers between devices, shards(): up[c] = lax.ppermute(up[c], 'shard', backward)  37.1 us
    ppermute x9, waiting for transfers between devices, exchange(): others.append(lax.ppermute(value, axis, [(i, i ^ mask) for i in range(n)]))  19.7 us
    pallas_call x21, Pallas kernels, put(): pl.pallas_call(functools.partial(put_kernel, step, lo, rows, n), in_specs...  18.7 us
    ppermute x9, starting transfers between devices, exchange(): others.append(lax.ppermute(value, axis, [(i, i ^ mask) for i in range(n)]))  13 us
    ppermute x20, waiting for transfers between devices, shards(): up[c] = lax.ppermute(up[c], 'shard', backward)  11.1 us
    ppermute x1, waiting for transfers between devices, shards(): early[0] = lax.ppermute(early[0], 'shard', forward)  10.6 us
    ppermute x1, waiting for transfers between devices, shards(): early[1] = lax.ppermute(early[1], 'shard', backward)  7.62 us
  transfers between devices with their start and end apart: 51, of which 39 were waited for; matrix products, arithmetic and copies ran while one was open for 0% of the time, Pallas kernels for 9%

profile of v4, /device:TPU:0, one launch (start us, length us, event | category | flops | bytes accessed | tf_op | source)
XLA Modules:
  0.0 231.9 jit_solution(10933889856344861586)
XLA Ops:
  0.7 3.7 %sums.1 = (f32[256,2048]{1,0:T(8,128)S(1)}, f32[256,2048]{1,0:T(8,128)S(1)}, f32[2,2048]{1,0:T(2,128)S(1)}, f32[16,2048]{1,0:T(8,128)S(1)}, f32[16,2048]{1,0:T(8,128)S(1)}) custom-call(f32[1,256]{1,0:T(1,128)} %bitcast.7, f32[256,2048]{1,0:T(8,128)} %one_g.1, f32[256,2048]{1,0:T(8,128)} %other_g.1, f32[256,2048]{1,0:T(8,128)} %one_u.1, f32[256,2048]{1,0:T(8,128)} %other_u.1), custom_call_target="tpu_custom_call" | custom-call | tf_op jit(solution)/shard_map/sums/pallas_call | solution.py:72
  4.3 3.0 %collective-permute-start = (f32[2,2048]{1,0:T(2,128)S(1)}, f32[2,2048]{1,0:T(2,128)S(1)}, u32[]{:S(2)}, u32[]{:S(2)}) collective-permute-start(f32[2,2048]{1,0:T(2,128)S(1)} %get-tuple-element.66.refs_0_), channel_id=1, source_target_pairs={{0,4},{4,0},{8,12},{12,8},{16,20},{20,16},{24,28},{28,24},{1,5},{5... | collective-permute-start | bytes 49160 | tf_op jit(solution)/shard_map/ppermute | solution.py:253
  7.4 1.7 collective-permute-done.refs_1_
  9.1 2.1 collective-permute-start.1
  11.2 2.6 %collective-permute-start.2 = (f32[2,2048]{1,0:T(2,128)S(1)}, f32[2,2048]{1,0:T(2,128)S(1)}, u32[]{:S(2)}, u32[]{:S(2)}) collective-permute-start(f32[2,2048]{1,0:T(2,128)S(1)} %tree_add.7.refs_0_), channel_id=1, source_target_pairs={{0,16},{4,20},{8,24},{12,28},{16,0},{20,4},{24,8},{28,12},{1,17},{... | collective-permute-start | bytes 49160 | tf_op jit(solution)/shard_map/ppermute | solution.py:253
  13.8 2.0 collective-permute-done.2.refs_2_
  15.8 3.6 %collective-permute-done.3.refs_3_ = f32[2,2048]{1,0:T(2,128)S(1)} collective-permute-done((f32[2,2048]{1,0:T(2,128)S(1)}, f32[2,2048]{1,0:T(2,128)S(1)}, u32[]{:S(2)}, u32[]{:S(2)}) %collective-permute-start.3) | collective-permute-done | bytes 16416 | tf_op jit(solution)/shard_map/ppermute | solution.py:253
  19.8 2.0 collective-permute-start.11
  21.8 2.0 collective-permute-start.25
  23.8 10.7 %collective-permute-done.4.gate = bf16[128,2048]{1,0:T(8,128)(2,1)S(1)} collective-permute-done((bf16[128,2048]{1,0:T(8,128)(2,1)S(1)}, bf16[128,2048]{1,0:T(8,128)(2,1)S(1)}, u32[]{:S(2)}, u32[]{:S(2)}) %collective-permute-start.4) | collective-permute-done | bytes 524320 | tf_op jit(solution)/shard_map/ppermute | solution.py:282
  34.6 2.0 collective-permute-start.12
  36.6 7.8 %collective-permute-done.18.gate = bf16[112,2048]{1,0:T(8,128)(2,1)S(1)} collective-permute-done((bf16[112,2048]{1,0:T(8,128)(2,1)S(1)}, bf16[112,2048]{1,0:T(8,128)(2,1)S(1)}, u32[]{:S(2)}, u32[]{:S(2)}) %collective-permute-start.18) | collective-permute-done | bytes 458784 | tf_op jit(solution)/shard_map/ppermute | solution.py:282
  44.4 2.0 collective-permute-start.26
  46.4 9.2 %collective-permute-done.5.gate = bf16[128,2048]{1,0:T(8,128)(2,1)S(1)} collective-permute-done((bf16[128,2048]{1,0:T(8,128)(2,1)S(1)}, bf16[128,2048]{1,0:T(8,128)(2,1)S(1)}, u32[]{:S(2)}, u32[]{:S(2)}) %collective-permute-start.5) | collective-permute-done | bytes 524320 | tf_op jit(solution)/shard_map/ppermute | solution.py:282
  55.7 2.0 collective-permute-start.13
  57.6 7.8 %collective-permute-done.19.gate = bf16[112,2048]{1,0:T(8,128)(2,1)S(1)} collective-permute-done((bf16[112,2048]{1,0:T(8,128)(2,1)S(1)}, bf16[112,2048]{1,0:T(8,128)(2,1)S(1)}, u32[]{:S(2)}, u32[]{:S(2)}) %collective-permute-start.19) | collective-permute-done | bytes 458784 | tf_op jit(solution)/shard_map/ppermute | solution.py:282
  65.5 2.0 collective-permute-start.27
  67.5 9.2 %collective-permute-done.6.gate = bf16[128,2048]{1,0:T(8,128)(2,1)S(1)} collective-permute-done((bf16[128,2048]{1,0:T(8,128)(2,1)S(1)}, bf16[128,2048]{1,0:T(8,128)(2,1)S(1)}, u32[]{:S(2)}, u32[]{:S(2)}) %collective-permute-start.6) | collective-permute-done | bytes 524320 | tf_op jit(solution)/shard_map/ppermute | solution.py:282
  76.7 2.0 collective-permute-start.14
  78.7 7.8 %collective-permute-done.20.gate = bf16[112,2048]{1,0:T(8,128)(2,1)S(1)} collective-permute-done((bf16[112,2048]{1,0:T(8,128)(2,1)S(1)}, bf16[112,2048]{1,0:T(8,128)(2,1)S(1)}, u32[]{:S(2)}, u32[]{:S(2)}) %collective-permute-start.20) | collective-permute-done | bytes 458784 | tf_op jit(solution)/shard_map/ppermute | solution.py:282
  86.6 2.0 collective-permute-start.28
  88.5 9.2 %collective-permute-done.7.gate = bf16[128,2048]{1,0:T(8,128)(2,1)S(1)} collective-permute-done((bf16[128,2048]{1,0:T(8,128)(2,1)S(1)}, bf16[128,2048]{1,0:T(8,128)(2,1)S(1)}, u32[]{:S(2)}, u32[]{:S(2)}) %collective-permute-start.7) | collective-permute-done | bytes 524320 | tf_op jit(solution)/shard_map/ppermute | solution.py:282
  97.8 2.0 collective-permute-start.15
  99.8 7.8 %collective-permute-done.21.gate = bf16[112,2048]{1,0:T(8,128)(2,1)S(1)} collective-permute-done((bf16[112,2048]{1,0:T(8,128)(2,1)S(1)}, bf16[112,2048]{1,0:T(8,128)(2,1)S(1)}, u32[]{:S(2)}, u32[]{:S(2)}) %collective-permute-start.21) | collective-permute-done | bytes 458784 | tf_op jit(solution)/shard_map/ppermute | solution.py:282
  107.6 2.0 collective-permute-start.29
  109.7 9.1 %collective-permute-done.8.gate = bf16[128,2048]{1,0:T(8,128)(2,1)S(1)} collective-permute-done((bf16[128,2048]{1,0:T(8,128)(2,1)S(1)}, bf16[128,2048]{1,0:T(8,128)(2,1)S(1)}, u32[]{:S(2)}, u32[]{:S(2)}) %collective-permute-start.8) | collective-permute-done | bytes 524320 | tf_op jit(solution)/shard_map/ppermute | solution.py:282
  118.9 2.0 collective-permute-start.16
  120.8 10.6 %collective-permute-done.32.early_g = f32[16,2048]{1,0:T(8,128)S(1)} collective-permute-done((f32[16,2048]{1,0:T(8,128)S(1)}, f32[16,2048]{1,0:T(8,128)S(1)}, u32[]{:S(2)}, u32[]{:S(2)}) %collective-permute-start.32) | collective-permute-done | bytes 131104 | tf_op jit(solution)/shard_map/ppermute | solution.py:266
  131.4 1.6 collective-permute-start.33
  133.5 1.6 collective-permute-start.30
  135.1 7.6 %collective-permute-done.33.early_u = f32[16,2048]{1,0:T(8,128)S(1)} collective-permute-done((f32[16,2048]{1,0:T(8,128)S(1)}, f32[16,2048]{1,0:T(8,128)S(1)}, u32[]{:S(2)}, u32[]{:S(2)}) %collective-permute-start.33) | collective-permute-done | bytes 131104 | tf_op jit(solution)/shard_map/ppermute | solution.py:267
  142.8 1.5 collective-permute-start.46
  144.3 2.1 collective-permute-done.46.refs_1_
  146.4 4.3 %collective-permute-done.34.gate.refs_2_ = bf16[16,2048]{1,0:T(8,128)(2,1)S(1)} collective-permute-done((bf16[16,2048]{1,0:T(8,128)(2,1)S(1)}, bf16[16,2048]{1,0:T(8,128)(2,1)S(1)}, u32[]{:S(2)}, u32[]{:S(2)}) %collective-permute-start.34) | collective-permute-done | bytes 65568 | tf_op jit(solution)/shard_map/ppermute | solution.py:282
  150.7 2.0 collective-permute-start.40
  152.6 2.3 collective-permute-done.40.up
  154.9 2.0 collective-permute-start.47
  156.9 1.7 collective-permute-done.47.refs_1_
  158.6 1.5 collective-permute-start.35
  160.1 2.8 %collective-permute-done.35.gate.refs_2_ = bf16[16,2048]{1,0:T(8,128)(2,1)S(1)} collective-permute-done((bf16[16,2048]{1,0:T(8,128)(2,1)S(1)}, bf16[16,2048]{1,0:T(8,128)(2,1)S(1)}, u32[]{:S(2)}, u32[]{:S(2)}) %collective-permute-start.35) | collective-permute-done | bytes 65568 | tf_op jit(solution)/shard_map/ppermute | solution.py:282
  162.9 2.0 collective-permute-start.41
  164.8 3.0 %collective-permute-done.41.up = bf16[16,2048]{1,0:T(8,128)(2,1)S(1)} collective-permute-done((bf16[16,2048]{1,0:T(8,128)(2,1)S(1)}, bf16[16,2048]{1,0:T(8,128)(2,1)S(1)}, u32[]{:S(2)}, u32[]{:S(2)}) %collective-permute-start.41) | collective-permute-done | bytes 65568 | tf_op jit(solution)/shard_map/ppermute | solution.py:283
  167.8 1.2 collective-permute-start.48
  168.9 2.6 %collective-permute-done.48.refs_1_ = f32[1,2048]{1,0:T(1,128)S(1)} collective-permute-done((f32[1,2048]{1,0:T(1,128)S(1)}, f32[1,2048]{1,0:T(1,128)S(1)}, u32[]{:S(2)}, u32[]{:S(2)}) %collective-permute-start.48) | collective-permute-done | bytes 8224 | tf_op jit(solution)/shard_map/ppermute | solution.py:253
  171.5 1.2 collective-permute-start.36
  172.7 3.8 %collective-permute-done.36.gate.refs_2_ = bf16[16,2048]{1,0:T(8,128)(2,1)S(1)} collective-permute-done((bf16[16,2048]{1,0:T(8,128)(2,1)S(1)}, bf16[16,2048]{1,0:T(8,128)(2,1)S(1)}, u32[]{:S(2)}, u32[]{:S(2)}) %collective-permute-start.36) | collective-permute-done | bytes 65568 | tf_op jit(solution)/shard_map/ppermute | solution.py:282
  176.5 1.7 collective-permute-start.42
  178.5 1.7 collective-permute-start.17
  181.4 1.4 collective-permute-start.24
  183.8 4.8 %collective-permute-done.49.refs_1_ = f32[1,2048]{1,0:T(1,128)S(1)} collective-permute-done((f32[1,2048]{1,0:T(1,128)S(1)}, f32[1,2048]{1,0:T(1,128)S(1)}, u32[]{:S(2)}, u32[]{:S(2)}) %collective-permute-start.49) | collective-permute-done | bytes 8224 | tf_op jit(solution)/shard_map/ppermute | solution.py:253
  189.3 3.7 %collective-permute-done.37.gate.refs_2_ = bf16[16,2048]{1,0:T(8,128)(2,1)S(1)} collective-permute-done((bf16[16,2048]{1,0:T(8,128)(2,1)S(1)}, bf16[16,2048]{1,0:T(8,128)(2,1)S(1)}, u32[]{:S(2)}, u32[]{:S(2)}) %collective-permute-start.37) | collective-permute-done | bytes 65568 | tf_op jit(solution)/shard_map/ppermute | solution.py:282
  193.0 1.9 collective-permute-start.43
  194.9 2.4 %collective-permute-done.43.up = bf16[16,2048]{1,0:T(8,128)(2,1)S(1)} collective-permute-done((bf16[16,2048]{1,0:T(8,128)(2,1)S(1)}, bf16[16,2048]{1,0:T(8,128)(2,1)S(1)}, u32[]{:S(2)}, u32[]{:S(2)}) %collective-permute-start.43) | collective-permute-done | bytes 65568 | tf_op jit(solution)/shard_map/ppermute | solution.py:283
  197.3 1.2 collective-permute-done.50.refs_1_
  199.0 3.8 %collective-permute-done.38.gate = bf16[16,2048]{1,0:T(8,128)(2,1)S(1)} collective-permute-done((bf16[16,2048]{1,0:T(8,128)(2,1)S(1)}, bf16[16,2048]{1,0:T(8,128)(2,1)S(1)}, u32[]{:S(2)}, u32[]{:S(2)}) %collective-permute-start.38) | collective-permute-done | bytes 65568 | tf_op jit(solution)/shard_map/ppermute | solution.py:282
  202.8 1.8 collective-permute-start.44
  204.6 2.4 %collective-permute-done.44.up = bf16[16,2048]{1,0:T(8,128)(2,1)S(1)} collective-permute-done((bf16[16,2048]{1,0:T(8,128)(2,1)S(1)}, bf16[16,2048]{1,0:T(8,128)(2,1)S(1)}, u32[]{:S(2)}, u32[]{:S(2)}) %collective-permute-start.44) | collective-permute-done | bytes 65568 | tf_op jit(solution)/shard_map/ppermute | solution.py:283
  208.1 1.4 start_outputs.1
  210.2 1.1 collective-permute-done.39.gate
  211.3 1.8 collective-permute-start.45
  214.7 1.0 put.23
  217.4 1.0 put.26
  220.1 1.0 put.29
  222.8 1.0 put.32
  (77 shorter events, 21.6 us)
Async XLA Ops:
  0.6 134.4 %copy-start = (f32[64]{0:T(128)S(1)}, f32[64]{0:T(128)}, u32[]{:S(2)}) copy-start(f32[64]{0:T(128)} %param.12) | copy-start | bytes 772
  0.6 134.4 %copy-start.1 = (f32[64]{0:T(128)S(1)}, f32[64]{0:T(128)}, u32[]{:S(2)}) copy-start(f32[64]{0:T(128)} %param.13) | copy-start | bytes 772
  4.3 4.8 %collective-permute-start = (f32[2,2048]{1,0:T(2,128)S(1)}, f32[2,2048]{1,0:T(2,128)S(1)}, u32[]{:S(2)}, u32[]{:S(2)}) collective-permute-start(f32[2,2048]{1,0:T(2,128)S(1)} %get-tuple-element.66.refs_0_), channel_id=1, source_target_pairs={{0,4},{4,0},{8,12},{12,8},{16,20},{20,16},{24,28},{28,24},{1,5},{5... | collective-permute-start | bytes 49160 | tf_op jit(solution)/shard_map/ppermute | solution.py:253
  9.1 4.7 %collective-permute-start.1 = (f32[2,2048]{1,0:T(2,128)S(1)}, f32[2,2048]{1,0:T(2,128)S(1)}, u32[]{:S(2)}, u32[]{:S(2)}) collective-permute-start(f32[2,2048]{1,0:T(2,128)S(1)} %tree_add.7.refs_0_), channel_id=1, source_target_pairs={{0,8},{4,12},{8,0},{12,4},{16,24},{20,28},{24,16},{28,20},{1,9},{5... | collective-permute-start | bytes 49160 | tf_op jit(solution)/shard_map/ppermute | solution.py:253
  11.2 4.6 %collective-permute-start.2 = (f32[2,2048]{1,0:T(2,128)S(1)}, f32[2,2048]{1,0:T(2,128)S(1)}, u32[]{:S(2)}, u32[]{:S(2)}) collective-permute-start(f32[2,2048]{1,0:T(2,128)S(1)} %tree_add.7.refs_0_), channel_id=1, source_target_pairs={{0,16},{4,20},{8,24},{12,28},{16,0},{20,4},{24,8},{28,12},{1,17},{... | collective-permute-start | bytes 49160 | tf_op jit(solution)/shard_map/ppermute | solution.py:253
  13.8 5.7 %collective-permute-start.3 = (f32[2,2048]{1,0:T(2,128)S(1)}, f32[2,2048]{1,0:T(2,128)S(1)}, u32[]{:S(2)}, u32[]{:S(2)}) collective-permute-start(f32[2,2048]{1,0:T(2,128)S(1)} %tree_add.7.refs_0_), channel_id=1, source_target_pairs={{0,24},{4,28},{8,16},{12,20},{16,8},{20,12},{24,0},{28,4},{1,25},{... | collective-permute-start | bytes 49160 | tf_op jit(solution)/shard_map/ppermute | solution.py:253
  19.7 14.8 %collective-permute-start.4 = (bf16[128,2048]{1,0:T(8,128)(2,1)S(1)}, bf16[128,2048]{1,0:T(8,128)(2,1)S(1)}, u32[]{:S(2)}, u32[]{:S(2)}) collective-permute-start(bf16[128,2048]{1,0:T(8,128)(2,1)S(1)} %get-tuple-element.67.refs_2_), channel_id=1, source_target_pairs={{0,8},{8,16},{16,24},{24,28},{28,20},{20,12},{12,4},{4,0},{1,9},{9... | collective-permute-start | bytes 1572872 | tf_op jit(solution)/shard_map/ppermute | solution.py:282
  19.8 14.9 %collective-permute-start.11 = (bf16[128,2048]{1,0:T(8,128)(2,1)S(1)}, bf16[128,2048]{1,0:T(8,128)(2,1)S(1)}, u32[]{:S(2)}, u32[]{:S(2)}) collective-permute-start(bf16[128,2048]{1,0:T(8,128)(2,1)S(1)} %get-tuple-element.68.refs_5_), channel_id=1, source_target_pairs={{8,0},{16,8},{24,16},{28,24},{20,28},{12,20},{4,12},{0,4},{9,1},{1... | collective-permute-start | bytes 1572872 | tf_op jit(solution)/shard_map/ppermute | solution.py:283
  21.8 22.6 %collective-permute-start.18 = (bf16[112,2048]{1,0:T(8,128)(2,1)S(1)}, bf16[112,2048]{1,0:T(8,128)(2,1)S(1)}, u32[]{:S(2)}, u32[]{:S(2)}) collective-permute-start(bf16[112,2048]{1,0:T(8,128)(2,1)S(1)} %get-tuple-element.69.refs_1_), channel_id=1, source_target_pairs={{0,8},{8,16},{16,24},{24,28},{28,20},{20,12},{12,4},{4,0},{1,9},{9... | collective-permute-start | bytes 1376264 | tf_op jit(solution)/shard_map/ppermute | solution.py:282
  21.8 22.6 %collective-permute-start.25 = (bf16[112,2048]{1,0:T(8,128)(2,1)S(1)}, bf16[112,2048]{1,0:T(8,128)(2,1)S(1)}, u32[]{:S(2)}, u32[]{:S(2)}) collective-permute-start(bf16[112,2048]{1,0:T(8,128)(2,1)S(1)} %get-tuple-element.70.refs_4_), channel_id=1, source_target_pairs={{8,0},{16,8},{24,16},{28,24},{20,28},{12,20},{4,12},{0,4},{9,1},{1... | collective-permute-start | bytes 1376264 | tf_op jit(solution)/shard_map/ppermute | solution.py:283
  34.5 21.1 %collective-permute-start.5 = (bf16[128,2048]{1,0:T(8,128)(2,1)S(1)}, bf16[128,2048]{1,0:T(8,128)(2,1)S(1)}, u32[]{:S(2)}, u32[]{:S(2)}) collective-permute-start(bf16[128,2048]{1,0:T(8,128)(2,1)S(1)} %collective-permute-done.4.gate), channel_id=1, source_target_pairs={{0,8},{8,16},{16,24},{24,28},{28,20},{20,12},{12,4},{4,0},{1,9},{9... | collective-permute-start | bytes 1572872 | tf_op jit(solution)/shard_map/ppermute | solution.py:282
  34.6 21.1 %collective-permute-start.12 = (bf16[128,2048]{1,0:T(8,128)(2,1)S(1)}, bf16[128,2048]{1,0:T(8,128)(2,1)S(1)}, u32[]{:S(2)}, u32[]{:S(2)}) collective-permute-start(bf16[128,2048]{1,0:T(8,128)(2,1)S(1)} %collective-permute-done.11.up), channel_id=1, source_target_pairs={{8,0},{16,8},{24,16},{28,24},{20,28},{12,20},{4,12},{0,4},{9,1},{1... | collective-permute-start | bytes 1572872 | tf_op jit(solution)/shard_map/ppermute | solution.py:283
  44.4 21.1 %collective-permute-start.19 = (bf16[112,2048]{1,0:T(8,128)(2,1)S(1)}, bf16[112,2048]{1,0:T(8,128)(2,1)S(1)}, u32[]{:S(2)}, u32[]{:S(2)}) collective-permute-start(bf16[112,2048]{1,0:T(8,128)(2,1)S(1)} %collective-permute-done.18.gate), channel_id=1, source_target_pairs={{0,8},{8,16},{16,24},{24,28},{28,20},{20,12},{12,4},{4,0},{1,9},{9... | collective-permute-start | bytes 1376264 | tf_op jit(solution)/shard_map/ppermute | solution.py:282
  44.4 21.1 %collective-permute-start.26 = (bf16[112,2048]{1,0:T(8,128)(2,1)S(1)}, bf16[112,2048]{1,0:T(8,128)(2,1)S(1)}, u32[]{:S(2)}, u32[]{:S(2)}) collective-permute-start(bf16[112,2048]{1,0:T(8,128)(2,1)S(1)} %collective-permute-done.25.up), channel_id=1, source_target_pairs={{8,0},{16,8},{24,16},{28,24},{20,28},{12,20},{4,12},{0,4},{9,1},{1... | collective-permute-start | bytes 1376264 | tf_op jit(solution)/shard_map/ppermute | solution.py:283
  55.6 21.1 %collective-permute-start.6 = (bf16[128,2048]{1,0:T(8,128)(2,1)S(1)}, bf16[128,2048]{1,0:T(8,128)(2,1)S(1)}, u32[]{:S(2)}, u32[]{:S(2)}) collective-permute-start(bf16[128,2048]{1,0:T(8,128)(2,1)S(1)} %collective-permute-done.5.gate), channel_id=1, source_target_pairs={{0,8},{8,16},{16,24},{24,28},{28,20},{20,12},{12,4},{4,0},{1,9},{9... | collective-permute-start | bytes 1572872 | tf_op jit(solution)/shard_map/ppermute | solution.py:282
  55.7 21.1 %collective-permute-start.13 = (bf16[128,2048]{1,0:T(8,128)(2,1)S(1)}, bf16[128,2048]{1,0:T(8,128)(2,1)S(1)}, u32[]{:S(2)}, u32[]{:S(2)}) collective-permute-start(bf16[128,2048]{1,0:T(8,128)(2,1)S(1)} %collective-permute-done.12.up), channel_id=1, source_target_pairs={{8,0},{16,8},{24,16},{28,24},{20,28},{12,20},{4,12},{0,4},{9,1},{1... | collective-permute-start | bytes 1572872 | tf_op jit(solution)/shard_map/ppermute | solution.py:283
  65.4 21.1 %collective-permute-start.20 = (bf16[112,2048]{1,0:T(8,128)(2,1)S(1)}, bf16[112,2048]{1,0:T(8,128)(2,1)S(1)}, u32[]{:S(2)}, u32[]{:S(2)}) collective-permute-start(bf16[112,2048]{1,0:T(8,128)(2,1)S(1)} %collective-permute-done.19.gate), channel_id=1, source_target_pairs={{0,8},{8,16},{16,24},{24,28},{28,20},{20,12},{12,4},{4,0},{1,9},{9... | collective-permute-start | bytes 1376264 | tf_op jit(solution)/shard_map/ppermute | solution.py:282
  65.5 21.1 %collective-permute-start.27 = (bf16[112,2048]{1,0:T(8,128)(2,1)S(1)}, bf16[112,2048]{1,0:T(8,128)(2,1)S(1)}, u32[]{:S(2)}, u32[]{:S(2)}) collective-permute-start(bf16[112,2048]{1,0:T(8,128)(2,1)S(1)} %collective-permute-done.26.up), channel_id=1, source_target_pairs={{8,0},{16,8},{24,16},{28,24},{20,28},{12,20},{4,12},{0,4},{9,1},{1... | collective-permute-start | bytes 1376264 | tf_op jit(solution)/shard_map/ppermute | solution.py:283
  76.7 21.1 %collective-permute-start.7 = (bf16[128,2048]{1,0:T(8,128)(2,1)S(1)}, bf16[128,2048]{1,0:T(8,128)(2,1)S(1)}, u32[]{:S(2)}, u32[]{:S(2)}) collective-permute-start(bf16[128,2048]{1,0:T(8,128)(2,1)S(1)} %collective-permute-done.6.gate), channel_id=1, source_target_pairs={{0,8},{8,16},{16,24},{24,28},{28,20},{20,12},{12,4},{4,0},{1,9},{9... | collective-permute-start | bytes 1572872 | tf_op jit(solution)/shard_map/ppermute | solution.py:282
  76.7 21.1 %collective-permute-start.14 = (bf16[128,2048]{1,0:T(8,128)(2,1)S(1)}, bf16[128,2048]{1,0:T(8,128)(2,1)S(1)}, u32[]{:S(2)}, u32[]{:S(2)}) collective-permute-start(bf16[128,2048]{1,0:T(8,128)(2,1)S(1)} %collective-permute-done.13.up), channel_id=1, source_target_pairs={{8,0},{16,8},{24,16},{28,24},{20,28},{12,20},{4,12},{0,4},{9,1},{1... | collective-permute-start | bytes 1572872 | tf_op jit(solution)/shard_map/ppermute | solution.py:283
  86.5 21.1 %collective-permute-start.21 = (bf16[112,2048]{1,0:T(8,128)(2,1)S(1)}, bf16[112,2048]{1,0:T(8,128)(2,1)S(1)}, u32[]{:S(2)}, u32[]{:S(2)}) collective-permute-start(bf16[112,2048]{1,0:T(8,128)(2,1)S(1)} %collective-permute-done.20.gate), channel_id=1, source_target_pairs={{0,8},{8,16},{16,24},{24,28},{28,20},{20,12},{12,4},{4,0},{1,9},{9... | collective-permute-start | bytes 1376264 | tf_op jit(solution)/shard_map/ppermute | solution.py:282
  86.6 21.1 %collective-permute-start.28 = (bf16[112,2048]{1,0:T(8,128)(2,1)S(1)}, bf16[112,2048]{1,0:T(8,128)(2,1)S(1)}, u32[]{:S(2)}, u32[]{:S(2)}) collective-permute-start(bf16[112,2048]{1,0:T(8,128)(2,1)S(1)} %collective-permute-done.27.up), channel_id=1, source_target_pairs={{8,0},{16,8},{24,16},{28,24},{20,28},{12,20},{4,12},{0,4},{9,1},{1... | collective-permute-start | bytes 1376264 | tf_op jit(solution)/shard_map/ppermute | solution.py:283
  97.7 21.1 %collective-permute-start.8 = (bf16[128,2048]{1,0:T(8,128)(2,1)S(1)}, bf16[128,2048]{1,0:T(8,128)(2,1)S(1)}, u32[]{:S(2)}, u32[]{:S(2)}) collective-permute-start(bf16[128,2048]{1,0:T(8,128)(2,1)S(1)} %collective-permute-done.7.gate), channel_id=1, source_target_pairs={{0,8},{8,16},{16,24},{24,28},{28,20},{20,12},{12,4},{4,0},{1,9},{9... | collective-permute-start | bytes 1572872 | tf_op jit(solution)/shard_map/ppermute | solution.py:282
  97.8 21.1 %collective-permute-start.15 = (bf16[128,2048]{1,0:T(8,128)(2,1)S(1)}, bf16[128,2048]{1,0:T(8,128)(2,1)S(1)}, u32[]{:S(2)}, u32[]{:S(2)}) collective-permute-start(bf16[128,2048]{1,0:T(8,128)(2,1)S(1)} %collective-permute-done.14.up), channel_id=1, source_target_pairs={{8,0},{16,8},{24,16},{28,24},{20,28},{12,20},{4,12},{0,4},{9,1},{1... | collective-permute-start | bytes 1572872 | tf_op jit(solution)/shard_map/ppermute | solution.py:283
  107.6 25.4 %collective-permute-start.22 = (bf16[112,2048]{1,0:T(8,128)(2,1)S(1)}, bf16[112,2048]{1,0:T(8,128)(2,1)S(1)}, u32[]{:S(2)}, u32[]{:S(2)}) collective-permute-start(bf16[112,2048]{1,0:T(8,128)(2,1)S(1)} %collective-permute-done.21.gate), channel_id=1, source_target_pairs={{0,8},{8,16},{16,24},{24,28},{28,20},{20,12},{12,4},{4,0},{1,9},{9... | collective-permute-start | bytes 1376264 | tf_op jit(solution)/shard_map/ppermute | solution.py:282
  107.6 25.8 %collective-permute-start.29 = (bf16[112,2048]{1,0:T(8,128)(2,1)S(1)}, bf16[112,2048]{1,0:T(8,128)(2,1)S(1)}, u32[]{:S(2)}, u32[]{:S(2)}) collective-permute-start(bf16[112,2048]{1,0:T(8,128)(2,1)S(1)} %collective-permute-done.28.up), channel_id=1, source_target_pairs={{8,0},{16,8},{24,16},{28,24},{20,28},{12,20},{4,12},{0,4},{9,1},{1... | collective-permute-start | bytes 1376264 | tf_op jit(solution)/shard_map/ppermute | solution.py:283
  109.6 21.8 %collective-permute-start.32 = (f32[16,2048]{1,0:T(8,128)S(1)}, f32[16,2048]{1,0:T(8,128)S(1)}, u32[]{:S(2)}, u32[]{:S(2)}) collective-permute-start(f32[16,2048]{1,0:T(8,128)S(1)} %get-tuple-element.71), channel_id=1, source_target_pairs={{0,8},{8,16},{16,24},{24,28},{28,20},{20,12},{12,4},{4,0},{1,9},{9... | collective-permute-start | bytes 393224 | tf_op jit(solution)/shard_map/ppermute | solution.py:266
  118.8 59.4 %collective-permute-start.9 = (bf16[128,2048]{1,0:T(8,128)(2,1)S(1)}, bf16[128,2048]{1,0:T(8,128)(2,1)S(1)}, u32[]{:S(2)}, u32[]{:S(2)}) collective-permute-start(bf16[128,2048]{1,0:T(8,128)(2,1)S(1)} %collective-permute-done.8.gate), channel_id=1, source_target_pairs={{0,8},{8,16},{16,24},{24,28},{28,20},{20,12},{12,4},{4,0},{1,9},{9... | collective-permute-start | bytes 1572872 | tf_op jit(solution)/shard_map/ppermute | solution.py:282
  118.9 59.6 %collective-permute-start.16 = (bf16[128,2048]{1,0:T(8,128)(2,1)S(1)}, bf16[128,2048]{1,0:T(8,128)(2,1)S(1)}, u32[]{:S(2)}, u32[]{:S(2)}) collective-permute-start(bf16[128,2048]{1,0:T(8,128)(2,1)S(1)} %collective-permute-done.15.up), channel_id=1, source_target_pairs={{8,0},{16,8},{24,16},{28,24},{20,28},{12,20},{4,12},{0,4},{9,1},{1... | collective-permute-start | bytes 1572872 | tf_op jit(solution)/shard_map/ppermute | solution.py:283
  131.4 11.3 %collective-permute-start.33 = (f32[16,2048]{1,0:T(8,128)S(1)}, f32[16,2048]{1,0:T(8,128)S(1)}, u32[]{:S(2)}, u32[]{:S(2)}) collective-permute-start(f32[16,2048]{1,0:T(8,128)S(1)} %get-tuple-element.72), channel_id=1, source_target_pairs={{8,0},{16,8},{24,16},{28,24},{20,28},{12,20},{4,12},{0,4},{9,1},{1... | collective-permute-start | bytes 393224 | tf_op jit(solution)/shard_map/ppermute | solution.py:267
  133.0 48.4 %collective-permute-start.23 = (bf16[112,2048]{1,0:T(8,128)(2,1)S(1)}, bf16[112,2048]{1,0:T(8,128)(2,1)S(1)}, u32[]{:S(2)}, u32[]{:S(2)}) collective-permute-start(bf16[112,2048]{1,0:T(8,128)(2,1)S(1)} %collective-permute-done.22.gate), channel_id=1, source_target_pairs={{0,8},{8,16},{16,24},{24,28},{28,20},{20,12},{12,4},{4,0},{1,9},{9... | collective-permute-start | bytes 1376264 | tf_op jit(solution)/shard_map/ppermute | solution.py:282
  133.5 49.4 %collective-permute-start.30 = (bf16[112,2048]{1,0:T(8,128)(2,1)S(1)}, bf16[112,2048]{1,0:T(8,128)(2,1)S(1)}, u32[]{:S(2)}, u32[]{:S(2)}) collective-permute-start(bf16[112,2048]{1,0:T(8,128)(2,1)S(1)} %collective-permute-done.29.up), channel_id=1, source_target_pairs={{8,0},{16,8},{24,16},{28,24},{20,28},{12,20},{4,12},{0,4},{9,1},{1... | collective-permute-start | bytes 1376264 | tf_op jit(solution)/shard_map/ppermute | solution.py:283
  142.8 3.7 %collective-permute-start.46 = (f32[1,2048]{1,0:T(1,128)S(1)}, f32[1,2048]{1,0:T(1,128)S(1)}, u32[]{:S(2)}, u32[]{:S(2)}) collective-permute-start(f32[1,2048]{1,0:T(1,128)S(1)} %slot.1.refs_0_), channel_id=1, source_target_pairs={{0,2},{1,3},{2,0},{3,1},{4,6},{5,7},{6,4},{7,5},{8,10},{9,11},{10,... | collective-permute-start | bytes 24584 | tf_op jit(solution)/shard_map/ppermute | solution.py:253
  146.4 4.3 %collective-permute-start.34 = (bf16[16,2048]{1,0:T(8,128)(2,1)S(1)}, bf16[16,2048]{1,0:T(8,128)(2,1)S(1)}, u32[]{:S(2)}, u32[]{:S(2)}) collective-permute-start(bf16[16,2048]{1,0:T(8,128)(2,1)S(1)} %get-tuple-element.73.gate), channel_id=1, source_target_pairs={{0,8},{8,16},{16,24},{24,28},{28,20},{20,12},{12,4},{4,0},{1,9},{9... | collective-permute-start | bytes 196616 | tf_op jit(solution)/shard_map/ppermute | solution.py:282
  150.7 4.3 %collective-permute-start.40 = (bf16[16,2048]{1,0:T(8,128)(2,1)S(1)}, bf16[16,2048]{1,0:T(8,128)(2,1)S(1)}, u32[]{:S(2)}, u32[]{:S(2)}) collective-permute-start(bf16[16,2048]{1,0:T(8,128)(2,1)S(1)} %get-tuple-element.74.up), channel_id=1, source_target_pairs={{8,0},{16,8},{24,16},{28,24},{20,28},{12,20},{4,12},{0,4},{9,1},{1... | collective-permute-start | bytes 196616 | tf_op jit(solution)/shard_map/ppermute | solution.py:283
  154.9 3.7 %collective-permute-start.47 = (f32[1,2048]{1,0:T(1,128)S(1)}, f32[1,2048]{1,0:T(1,128)S(1)}, u32[]{:S(2)}, u32[]{:S(2)}) collective-permute-start(f32[1,2048]{1,0:T(1,128)S(1)} %tree_add.9.refs_0_), channel_id=1, source_target_pairs={{0,4},{4,0},{8,12},{12,8},{16,20},{20,16},{24,28},{28,24},{1,5},{5... | collective-permute-start | bytes 24584 | tf_op jit(solution)/shard_map/ppermute | solution.py:253
  158.6 4.3 %collective-permute-start.35 = (bf16[16,2048]{1,0:T(8,128)(2,1)S(1)}, bf16[16,2048]{1,0:T(8,128)(2,1)S(1)}, u32[]{:S(2)}, u32[]{:S(2)}) collective-permute-start(bf16[16,2048]{1,0:T(8,128)(2,1)S(1)} %collective-permute-done.34.gate.refs_2_), channel_id=1, source_target_pairs={{0,8},{8,16},{16,24},{24,28},{28,20},{20,12},{12,4},{4,0},{1,9},{9... | collective-permute-start | bytes 196616 | tf_op jit(solution)/shard_map/ppermute | solution.py:282
  162.9 4.9 %collective-permute-start.41 = (bf16[16,2048]{1,0:T(8,128)(2,1)S(1)}, bf16[16,2048]{1,0:T(8,128)(2,1)S(1)}, u32[]{:S(2)}, u32[]{:S(2)}) collective-permute-start(bf16[16,2048]{1,0:T(8,128)(2,1)S(1)} %collective-permute-done.40.up), channel_id=1, source_target_pairs={{8,0},{16,8},{24,16},{28,24},{20,28},{12,20},{4,12},{0,4},{9,1},{1... | collective-permute-start | bytes 196616 | tf_op jit(solution)/shard_map/ppermute | solution.py:283
  167.8 3.7 %collective-permute-start.48 = (f32[1,2048]{1,0:T(1,128)S(1)}, f32[1,2048]{1,0:T(1,128)S(1)}, u32[]{:S(2)}, u32[]{:S(2)}) collective-permute-start(f32[1,2048]{1,0:T(1,128)S(1)} %tree_add.10.refs_0_), channel_id=1, source_target_pairs={{0,8},{4,12},{8,0},{12,4},{16,24},{20,28},{24,16},{28,20},{1,9},{5... | collective-permute-start | bytes 24584 | tf_op jit(solution)/shard_map/ppermute | solution.py:253
  171.5 5.0 %collective-permute-start.36 = (bf16[16,2048]{1,0:T(8,128)(2,1)S(1)}, bf16[16,2048]{1,0:T(8,128)(2,1)S(1)}, u32[]{:S(2)}, u32[]{:S(2)}) collective-permute-start(bf16[16,2048]{1,0:T(8,128)(2,1)S(1)} %collective-permute-done.35.gate.refs_2_), channel_id=1, source_target_pairs={{0,8},{8,16},{16,24},{24,28},{28,20},{20,12},{12,4},{4,0},{1,9},{9... | collective-permute-start | bytes 196616 | tf_op jit(solution)/shard_map/ppermute | solution.py:282
  176.5 4.3 %collective-permute-start.42 = (bf16[16,2048]{1,0:T(8,128)(2,1)S(1)}, bf16[16,2048]{1,0:T(8,128)(2,1)S(1)}, u32[]{:S(2)}, u32[]{:S(2)}) collective-permute-start(bf16[16,2048]{1,0:T(8,128)(2,1)S(1)} %collective-permute-done.41.up), channel_id=1, source_target_pairs={{8,0},{16,8},{24,16},{28,24},{20,28},{12,20},{4,12},{0,4},{9,1},{1... | collective-permute-start | bytes 196616 | tf_op jit(solution)/shard_map/ppermute | solution.py:283
  178.2 52.7 %collective-permute-start.10 = (bf16[128,2048]{1,0:T(8,128)(2,1)S(1)}, bf16[128,2048]{1,0:T(8,128)(2,1)S(1)}, u32[]{:S(2)}, u32[]{:S(2)}) collective-permute-start(bf16[128,2048]{1,0:T(8,128)(2,1)S(1)} %collective-permute-done.9.gate), channel_id=1, source_target_pairs={{0,8},{8,16},{16,24},{24,28},{28,20},{20,12},{12,4},{4,0},{1,9},{9... | collective-permute-start | bytes 1572872 | tf_op jit(solution)/shard_map/ppermute | solution.py:282
  178.5 52.4 %collective-permute-start.17 = (bf16[128,2048]{1,0:T(8,128)(2,1)S(1)}, bf16[128,2048]{1,0:T(8,128)(2,1)S(1)}, u32[]{:S(2)}, u32[]{:S(2)}) collective-permute-start(bf16[128,2048]{1,0:T(8,128)(2,1)S(1)} %collective-permute-done.16.up), channel_id=1, source_target_pairs={{8,0},{16,8},{24,16},{28,24},{20,28},{12,20},{4,12},{0,4},{9,1},{1... | collective-permute-start | bytes 1572872 | tf_op jit(solution)/shard_map/ppermute | solution.py:283
  180.8 7.9 %collective-permute-start.49 = (f32[1,2048]{1,0:T(1,128)S(1)}, f32[1,2048]{1,0:T(1,128)S(1)}, u32[]{:S(2)}, u32[]{:S(2)}) collective-permute-start(f32[1,2048]{1,0:T(1,128)S(1)} %tree_add.11.refs_0_), channel_id=1, source_target_pairs={{0,16},{4,20},{8,24},{12,28},{16,0},{20,4},{24,8},{28,12},{1,17},{... | collective-permute-start | bytes 24584 | tf_op jit(solution)/shard_map/ppermute | solution.py:253
  181.4 48.5 %collective-permute-start.24 = (bf16[112,2048]{1,0:T(8,128)(2,1)S(1)}, bf16[112,2048]{1,0:T(8,128)(2,1)S(1)}, u32[]{:S(2)}, u32[]{:S(2)}) collective-permute-start(bf16[112,2048]{1,0:T(8,128)(2,1)S(1)} %collective-permute-done.23.gate), channel_id=1, source_target_pairs={{0,8},{8,16},{16,24},{24,28},{28,20},{20,12},{12,4},{4,0},{1,9},{9... | collective-permute-start | bytes 1376264 | tf_op jit(solution)/shard_map/ppermute | solution.py:282
  182.9 47.0 %collective-permute-start.31 = (bf16[112,2048]{1,0:T(8,128)(2,1)S(1)}, bf16[112,2048]{1,0:T(8,128)(2,1)S(1)}, u32[]{:S(2)}, u32[]{:S(2)}) collective-permute-start(bf16[112,2048]{1,0:T(8,128)(2,1)S(1)} %collective-permute-done.30.up), channel_id=1, source_target_pairs={{8,0},{16,8},{24,16},{28,24},{20,28},{12,20},{4,12},{0,4},{9,1},{1... | collective-permute-start | bytes 1376264 | tf_op jit(solution)/shard_map/ppermute | solution.py:283
  188.6 4.4 %collective-permute-start.37 = (bf16[16,2048]{1,0:T(8,128)(2,1)S(1)}, bf16[16,2048]{1,0:T(8,128)(2,1)S(1)}, u32[]{:S(2)}, u32[]{:S(2)}) collective-permute-start(bf16[16,2048]{1,0:T(8,128)(2,1)S(1)} %collective-permute-done.36.gate.refs_2_), channel_id=1, source_target_pairs={{0,8},{8,16},{16,24},{24,28},{28,20},{20,12},{12,4},{4,0},{1,9},{9... | collective-permute-start | bytes 196616 | tf_op jit(solution)/shard_map/ppermute | solution.py:282
  193.0 4.3 %collective-permute-start.43 = (bf16[16,2048]{1,0:T(8,128)(2,1)S(1)}, bf16[16,2048]{1,0:T(8,128)(2,1)S(1)}, u32[]{:S(2)}, u32[]{:S(2)}) collective-permute-start(bf16[16,2048]{1,0:T(8,128)(2,1)S(1)} %collective-permute-done.42.up), channel_id=1, source_target_pairs={{8,0},{16,8},{24,16},{28,24},{20,28},{12,20},{4,12},{0,4},{9,1},{1... | collective-permute-start | bytes 196616 | tf_op jit(solution)/shard_map/ppermute | solution.py:283
  197.3 1.2 collective-permute-start.50
  198.5 4.3 %collective-permute-start.38 = (bf16[16,2048]{1,0:T(8,128)(2,1)S(1)}, bf16[16,2048]{1,0:T(8,128)(2,1)S(1)}, u32[]{:S(2)}, u32[]{:S(2)}) collective-permute-start(bf16[16,2048]{1,0:T(8,128)(2,1)S(1)} %collective-permute-done.37.gate.refs_2_), channel_id=1, source_target_pairs={{0,8},{8,16},{16,24},{24,28},{28,20},{20,12},{12,4},{4,0},{1,9},{9... | collective-permute-start | bytes 196616 | tf_op jit(solution)/shard_map/ppermute | solution.py:282
  202.8 4.3 %collective-permute-start.44 = (bf16[16,2048]{1,0:T(8,128)(2,1)S(1)}, bf16[16,2048]{1,0:T(8,128)(2,1)S(1)}, u32[]{:S(2)}, u32[]{:S(2)}) collective-permute-start(bf16[16,2048]{1,0:T(8,128)(2,1)S(1)} %collective-permute-done.43.up), channel_id=1, source_target_pairs={{8,0},{16,8},{24,16},{28,24},{20,28},{12,20},{4,12},{0,4},{9,1},{1... | collective-permute-start | bytes 196616 | tf_op jit(solution)/shard_map/ppermute | solution.py:283
  207.0 4.3 %collective-permute-start.39 = (bf16[16,2048]{1,0:T(8,128)(2,1)S(1)}, bf16[16,2048]{1,0:T(8,128)(2,1)S(1)}, u32[]{:S(2)}, u32[]{:S(2)}) collective-permute-start(bf16[16,2048]{1,0:T(8,128)(2,1)S(1)} %collective-permute-done.38.gate), channel_id=1, source_target_pairs={{0,8},{8,16},{16,24},{24,28},{28,20},{20,12},{12,4},{4,0},{1,9},{9... | collective-permute-start | bytes 196616 | tf_op jit(solution)/shard_map/ppermute | solution.py:282
  211.3 17.9 %collective-permute-start.45 = (bf16[16,2048]{1,0:T(8,128)(2,1)S(1)}, bf16[16,2048]{1,0:T(8,128)(2,1)S(1)}, u32[]{:S(2)}, u32[]{:S(2)}) collective-permute-start(bf16[16,2048]{1,0:T(8,128)(2,1)S(1)} %collective-permute-done.44.up), channel_id=1, source_target_pairs={{8,0},{16,8},{24,16},{28,24},{20,28},{12,20},{4,12},{0,4},{9,1},{1... | collective-permute-start | bytes 196616 | tf_op jit(solution)/shard_map/ppermute | solution.py:283

commit v5 on v4

--- a/solution.py
+++ b/solution.py
@@ -10,7 +10,7 @@
 WHOLE = pl.BlockSpec(memory_space=pltpu.VMEM)
 OUTSIDE = pl.BlockSpec(memory_space=pl.ANY)
 GRANT = 47
-EARLY = 16
+EARLY = 32
 MOST = 2
 
 
@@ -57,8 +57,8 @@
             for side, fresh in ((0, fresh_g), (1, fresh_u)):
                 value = m * held[2 * side, r:r + 8] + w * held[2 * side + 1, r:r + 8]
                 fresh[r:r + 8] = value
-                if early and r < early[side].shape[0]:
-                    early[side][r:r + 8] = value
+                if early and r < EARLY:
+                    early[2 * (r // (EARLY // 2)) + side][r % (EARLY // 2):r % (EARLY // 2) + 8] = value
                 total[side] = total[side] + value * value
     sums[0:1] = jnp.sum(total[0], axis=0, keepdims=True)
     sums[1:2] = jnp.sum(total[1], axis=0, keepdims=True)
@@ -68,7 +68,7 @@
     rows, cols = one_gate.shape
     edges = [0, rows] if rows < 256 else [0, rows // 4, rows // 2, 3 * rows // 4, rows]
     wide = jax.ShapeDtypeStruct((rows, cols), jnp.float32)
-    early = [jax.ShapeDtypeStruct((EARLY, cols), jnp.float32)] * 2 if rows >= 256 else []
+    early = [jax.ShapeDtypeStruct((EARLY // 2, cols), jnp.float32)] * 4 if rows >= 256 else []
     return pl.pallas_call(
         functools.partial(sums_kernel, edges),
         in_specs=[OUTSIDE] * 5,
@@ -107,23 +107,27 @@
     return list(pieces[:len(spans)]), list(pieces[len(spans):])
 
 
-def late_kernel(early_g, early_u, total_ref, gate, up):
-    for side, early, out in ((0, early_g, gate), (1, early_u, up)):
+def late_kernel(*refs):
+    early, total_ref, outs = refs[:-3], refs[-3], refs[-2:]
+    for side, out in enumerate(outs):
         scale = 1.0 / jnp.sqrt(total_ref[side:side + 1])
-        for r in range(0, out.shape[0], 16):
-            out[r:r + 16] = (early[r:r + 16] * scale).astype(jnp.bfloat16)
-
-
-def narrow_late(early_gate, early_up, total):
-    shape = jax.ShapeDtypeStruct(early_gate.shape, jnp.bfloat16)
+        low = 0
+        for part in early[side::2]:
+            tall = part.shape[0]
+            out[low:low + tall] = (part[...] * scale).astype(jnp.bfloat16)
+            low += tall
+
+
+def narrow_late(early, total):
+    shape = jax.ShapeDtypeStruct((EARLY, total.shape[1]), jnp.bfloat16)
     return pl.pallas_call(
         late_kernel,
-        in_specs=[WHOLE] * 3,
+        in_specs=[WHOLE] * (len(early) + 1),
         out_specs=[WHOLE] * 2,
         out_shape=[shape, shape],
         compiler_params=grant(4),
         name="narrow_late",
-    )(early_gate, early_up, total)
+    )(*early, total)
 
 
 def root_kernel(total_ref, factor_g, factor_u):
@@ -262,9 +266,8 @@
     backward = [(b, a) for a, b in forward]
     spans = cuts(rows)
     fresh_gate, fresh_up, total, *early = sums_of(mix_share[None], one_gate, other_gate, one_up, other_up)
-    if early:
-        early[0] = lax.ppermute(early[0], "shard", forward)
-        early[1] = lax.ppermute(early[1], "shard", backward)
+    for k in range(len(early)):
+        early[k] = lax.ppermute(early[k], "shard", backward if k % 2 else forward)
     norm = slot_of(norm_train[None], norm_step[None], n * t, t)
     for masks in stages_of(n, MOST):
         total = exchange(total, "shard", n, masks)
@@ -277,7 +280,7 @@
     for step in range(1, n):
         for c, (lo, hi) in enumerate(spans):
             if early and (step, c) == (1, 0):
-                gate[c], up[c] = narrow_late(*early, total)
+                gate[c], up[c] = narrow_late(early, total)
             else:
                 gate[c] = lax.ppermute(gate[c], "shard", forward)
                 up[c] = lax.ppermute(up[c], "shard", backward)

time: 232 us -> 238 us (1.026)
  waiting for transfers between devices: 147 us -> 160 us
  starting transfers between devices: 58.5 us -> 52.1 us
    ppermute x20, waiting for transfers between devices: 98.2 us -> 60.3 us  [shards(): gate[c] = lax.ppermute(gate[c], 'shard', forward)]
    ppermute x20, waiting for transfers between devices: 11.1 us -> 29 us  [shards(): up[c] = lax.ppermute(up[c], 'shard', backward)]
    ppermute x2 -> x4, waiting for transfers between devices: 18.2 us -> 35.4 us  [shards(): early[k] = lax.ppermute(early[k], 'shard', backward if k % 2 else forward)]
    ppermute x9, waiting for transfers between devices: 19.7 us -> 34.8 us  [exchange(): others.append(lax.ppermute(value, axis, [(i, i ^ mask) for i in range(n)]))]
    ppermute x20, starting transfers between devices: 37.1 us -> 31.1 us  [shards(): up[c] = lax.ppermute(up[c], 'shard', backward)]
  transfers between devices with their start and end apart: 51 -> 53, of which waited for: 39 -> 31; matrix products, arithmetic and copies ran while one was open for 0% -> 0% of each run, Pallas kernels for 9% -> 8%
where the time goes in v5:
time: 238 us
  waiting for transfers between devices  160 us (67%)
  starting transfers between devices  52.1 us (22%)
  Pallas kernels  24.7 us (10%)
    ppermute x20, waiting for transfers between devices, shards(): gate[c] = lax.ppermute(gate[c], 'shard', forward)  60.3 us
    ppermute x4, waiting for transfers between devices, shards(): early[k] = lax.ppermute(early[k], 'shard', backward if k % 2 else forward)  35.4 us
    ppermute x9, waiting for transfers between devices, exchange(): others.append(lax.ppermute(value, axis, [(i, i ^ mask) for i in range(n)]))  34.8 us
    ppermute x20, starting transfers between devices, shards(): up[c] = lax.ppermute(up[c], 'shard', backward)  31.1 us
    ppermute x20, waiting for transfers between devices, shards(): up[c] = lax.ppermute(up[c], 'shard', backward)  29 us
    pallas_call x21, Pallas kernels, put(): pl.pallas_call(functools.partial(put_kernel, step, lo, rows, n), in_specs...  18.7 us
    ppermute x9, starting transfers between devices, exchange(): others.append(lax.ppermute(value, axis, [(i, i ^ mask) for i in range(n)]))  11.4 us
    ppermute x20, starting transfers between devices, shards(): gate[c] = lax.ppermute(gate[c], 'shard', forward)  6.19 us
  transfers between devices with their start and end apart: 53, of which 31 were waited for; matrix products, arithmetic and copies ran while one was open for 0% of the time, Pallas kernels for 8%

profile of v5, /device:TPU:0, one launch (start us, length us, event | category | flops | bytes accessed | tf_op | source)
XLA Modules:
  0.0 238.0 jit_solution(7538113184038162597)
XLA Ops:
  0.7 3.7 %sums.1 = (f32[256,2048]{1,0:T(8,128)S(1)}, f32[256,2048]{1,0:T(8,128)S(1)}, f32[2,2048]{1,0:T(2,128)S(1)}, f32[16,2048]{1,0:T(8,128)S(1)}, f32[16,2048]{1,0:T(8...) custom-call(f32[1,256]{1,0:T(1,128)} %bitcast.7, f32[256,2048]{1,0:T(8,128)} %one_g.1, f32[256,2048]{1,0:T(8,128)} %other_g.1, ...), custom_call_target="tpu_custom_call" | custom-call | tf_op jit(solution)/shard_map/sums/pallas_call | solution.py:72
  4.3 3.0 %collective-permute-start = (f32[2,2048]{1,0:T(2,128)S(1)}, f32[2,2048]{1,0:T(2,128)S(1)}, u32[]{:S(2)}, u32[]{:S(2)}) collective-permute-start(f32[2,2048]{1,0:T(2,128)S(1)} %get-tuple-element.68.refs_0_), channel_id=1, source_target_pairs={{0,4},{4,0},{8,12},{12,8},{16,20},{20,16},{24,28},{28,24},{1,5},{5... | collective-permute-start | bytes 49160 | tf_op jit(solution)/shard_map/ppermute | solution.py:257
  7.4 1.7 collective-permute-done.refs_1_
  9.1 2.1 collective-permute-start.1
  11.2 2.6 %collective-permute-start.2 = (f32[2,2048]{1,0:T(2,128)S(1)}, f32[2,2048]{1,0:T(2,128)S(1)}, u32[]{:S(2)}, u32[]{:S(2)}) collective-permute-start(f32[2,2048]{1,0:T(2,128)S(1)} %tree_add.7.refs_0_), channel_id=1, source_target_pairs={{0,16},{4,20},{8,24},{12,28},{16,0},{20,4},{24,8},{28,12},{1,17},{... | collective-permute-start | bytes 49160 | tf_op jit(solution)/shard_map/ppermute | solution.py:257
  13.8 2.0 collective-permute-done.2.refs_2_
  15.8 3.6 %collective-permute-done.3.refs_3_ = f32[2,2048]{1,0:T(2,128)S(1)} collective-permute-done((f32[2,2048]{1,0:T(2,128)S(1)}, f32[2,2048]{1,0:T(2,128)S(1)}, u32[]{:S(2)}, u32[]{:S(2)}) %collective-permute-start.3) | collective-permute-done | bytes 16416 | tf_op jit(solution)/shard_map/ppermute | solution.py:257
  19.8 2.0 collective-permute-start.25
  21.8 2.0 collective-permute-start.11
  23.8 9.3 %collective-permute-done.18.gate = bf16[112,2048]{1,0:T(8,128)(2,1)S(1)} collective-permute-done((bf16[112,2048]{1,0:T(8,128)(2,1)S(1)}, bf16[112,2048]{1,0:T(8,128)(2,1)S(1)}, u32[]{:S(2)}, u32[]{:S(2)}) %collective-permute-start.18) | collective-permute-done | bytes 458784 | tf_op jit(solution)/shard_map/ppermute | solution.py:285
  33.2 2.0 collective-permute-start.26
  35.2 7.8 %collective-permute-done.4.gate = bf16[112,2048]{1,0:T(8,128)(2,1)S(1)} collective-permute-done((bf16[112,2048]{1,0:T(8,128)(2,1)S(1)}, bf16[112,2048]{1,0:T(8,128)(2,1)S(1)}, u32[]{:S(2)}, u32[]{:S(2)}) %collective-permute-start.4) | collective-permute-done | bytes 458784 | tf_op jit(solution)/shard_map/ppermute | solution.py:285
  43.0 2.0 collective-permute-start.12
  45.0 7.8 %collective-permute-done.19.gate = bf16[112,2048]{1,0:T(8,128)(2,1)S(1)} collective-permute-done((bf16[112,2048]{1,0:T(8,128)(2,1)S(1)}, bf16[112,2048]{1,0:T(8,128)(2,1)S(1)}, u32[]{:S(2)}, u32[]{:S(2)}) %collective-permute-start.19) | collective-permute-done | bytes 458784 | tf_op jit(solution)/shard_map/ppermute | solution.py:285
  52.9 2.0 collective-permute-start.27
  54.8 7.8 %collective-permute-done.5.gate = bf16[112,2048]{1,0:T(8,128)(2,1)S(1)} collective-permute-done((bf16[112,2048]{1,0:T(8,128)(2,1)S(1)}, bf16[112,2048]{1,0:T(8,128)(2,1)S(1)}, u32[]{:S(2)}, u32[]{:S(2)}) %collective-permute-start.5) | collective-permute-done | bytes 458784 | tf_op jit(solution)/shard_map/ppermute | solution.py:285
  62.7 2.0 collective-permute-start.13
  64.7 16.3 %collective-permute-done.32.refs_0_ = f32[16,2048]{1,0:T(8,128)S(1)} collective-permute-done((f32[16,2048]{1,0:T(8,128)S(1)}, f32[16,2048]{1,0:T(8,128)S(1)}, u32[]{:S(2)}, u32[]{:S(2)}) %collective-permute-start.32) | collective-permute-done | bytes 131104 | tf_op jit(solution)/shard_map/ppermute | solution.py:270
  81.0 1.6 collective-permute-start.33
  82.6 4.7 %collective-permute-done.33.refs_1_ = f32[16,2048]{1,0:T(8,128)S(1)} collective-permute-done((f32[16,2048]{1,0:T(8,128)S(1)}, f32[16,2048]{1,0:T(8,128)S(1)}, u32[]{:S(2)}, u32[]{:S(2)}) %collective-permute-start.33) | collective-permute-done | bytes 131104 | tf_op jit(solution)/shard_map/ppermute | solution.py:270
  87.4 2.1 collective-permute-start.28
  89.5 2.0 collective-permute-start.14
  91.5 2.2 collective-permute-done.34.refs_2_
  93.7 1.6 collective-permute-start.35
  95.5 12.2 %collective-permute-done.35.refs_3_ = f32[16,2048]{1,0:T(8,128)S(1)} collective-permute-done((f32[16,2048]{1,0:T(8,128)S(1)}, f32[16,2048]{1,0:T(8,128)S(1)}, u32[]{:S(2)}, u32[]{:S(2)}) %collective-permute-start.35) | collective-permute-done | bytes 131104 | tf_op jit(solution)/shard_map/ppermute | solution.py:270
  107.7 1.5 collective-permute-start.48
  109.2 2.1 collective-permute-done.48.refs_1_
  111.3 1.1 collective-permute-start.36
  112.4 5.3 %collective-permute-done.36.gate.refs_2_ = bf16[32,2048]{1,0:T(8,128)(2,1)S(1)} collective-permute-done((bf16[32,2048]{1,0:T(8,128)(2,1)S(1)}, bf16[32,2048]{1,0:T(8,128)(2,1)S(1)}, u32[]{:S(2)}, u32[]{:S(2)}) %collective-permute-start.36) | collective-permute-done | bytes 131104 | tf_op jit(solution)/shard_map/ppermute | solution.py:285
  117.7 1.7 collective-permute-start.42
  119.7 1.7 collective-permute-start.29
  121.8 1.7 collective-permute-start.15
  123.9 1.5 collective-permute-start.49
  125.4 9.6 %collective-permute-done.49.refs_1_ = f32[1,2048]{1,0:T(1,128)S(1)} collective-permute-done((f32[1,2048]{1,0:T(1,128)S(1)}, f32[1,2048]{1,0:T(1,128)S(1)}, u32[]{:S(2)}, u32[]{:S(2)}) %collective-permute-start.49) | collective-permute-done | bytes 8224 | tf_op jit(solution)/shard_map/ppermute | solution.py:257
  135.0 5.0 %collective-permute-done.37.gate.refs_2_ = bf16[32,2048]{1,0:T(8,128)(2,1)S(1)} collective-permute-done((bf16[32,2048]{1,0:T(8,128)(2,1)S(1)}, bf16[32,2048]{1,0:T(8,128)(2,1)S(1)}, u32[]{:S(2)}, u32[]{:S(2)}) %collective-permute-start.37) | collective-permute-done | bytes 131104 | tf_op jit(solution)/shard_map/ppermute | solution.py:285
  140.0 2.2 collective-permute-start.43
  142.1 3.9 %collective-permute-done.43.up = bf16[32,2048]{1,0:T(8,128)(2,1)S(1)} collective-permute-done((bf16[32,2048]{1,0:T(8,128)(2,1)S(1)}, bf16[32,2048]{1,0:T(8,128)(2,1)S(1)}, u32[]{:S(2)}, u32[]{:S(2)}) %collective-permute-start.43) | collective-permute-done | bytes 131104 | tf_op jit(solution)/shard_map/ppermute | solution.py:286
  146.0 3.7 %collective-permute-done.50.refs_1_ = f32[1,2048]{1,0:T(1,128)S(1)} collective-permute-done((f32[1,2048]{1,0:T(1,128)S(1)}, f32[1,2048]{1,0:T(1,128)S(1)}, u32[]{:S(2)}, u32[]{:S(2)}) %collective-permute-start.50) | collective-permute-done | bytes 8224 | tf_op jit(solution)/shard_map/ppermute | solution.py:257
  149.8 6.7 %collective-permute-done.38.gate.refs_2_ = bf16[32,2048]{1,0:T(8,128)(2,1)S(1)} collective-permute-done((bf16[32,2048]{1,0:T(8,128)(2,1)S(1)}, bf16[32,2048]{1,0:T(8,128)(2,1)S(1)}, u32[]{:S(2)}, u32[]{:S(2)}) %collective-permute-start.38) | collective-permute-done | bytes 131104 | tf_op jit(solution)/shard_map/ppermute | solution.py:285
  157.2 1.3 collective-permute-start.23
  159.2 1.3 collective-permute-start.9
  162.1 10.9 %collective-permute-done.51.refs_1_ = f32[1,2048]{1,0:T(1,128)S(1)} collective-permute-done((f32[1,2048]{1,0:T(1,128)S(1)}, f32[1,2048]{1,0:T(1,128)S(1)}, u32[]{:S(2)}, u32[]{:S(2)}) %collective-permute-start.51) | collective-permute-done | bytes 8224 | tf_op jit(solution)/shard_map/ppermute | solution.py:257
  173.7 4.3 %collective-permute-done.39.gate.refs_2_ = bf16[32,2048]{1,0:T(8,128)(2,1)S(1)} collective-permute-done((bf16[32,2048]{1,0:T(8,128)(2,1)S(1)}, bf16[32,2048]{1,0:T(8,128)(2,1)S(1)}, u32[]{:S(2)}, u32[]{:S(2)}) %collective-permute-start.39) | collective-permute-done | bytes 131104 | tf_op jit(solution)/shard_map/ppermute | solution.py:285
  178.0 5.0 %collective-permute-done.45.up = bf16[32,2048]{1,0:T(8,128)(2,1)S(1)} collective-permute-done((bf16[32,2048]{1,0:T(8,128)(2,1)S(1)}, bf16[32,2048]{1,0:T(8,128)(2,1)S(1)}, u32[]{:S(2)}, u32[]{:S(2)}) %collective-permute-start.45) | collective-permute-done | bytes 131104 | tf_op jit(solution)/shard_map/ppermute | solution.py:286
  182.9 1.2 collective-permute-done.52.refs_1_
  184.8 2.0 collective-permute-start.31
  186.9 2.0 collective-permute-start.17
  188.9 1.6 collective-permute-done.40.gate
  190.5 19.3 %collective-permute-done.46.up = bf16[32,2048]{1,0:T(8,128)(2,1)S(1)} collective-permute-done((bf16[32,2048]{1,0:T(8,128)(2,1)S(1)}, bf16[32,2048]{1,0:T(8,128)(2,1)S(1)}, u32[]{:S(2)}, u32[]{:S(2)}) %collective-permute-start.46) | collective-permute-done | bytes 131104 | tf_op jit(solution)/shard_map/ppermute | solution.py:286
  210.1 4.7 %collective-permute-done.41.gate = bf16[32,2048]{1,0:T(8,128)(2,1)S(1)} collective-permute-done((bf16[32,2048]{1,0:T(8,128)(2,1)S(1)}, bf16[32,2048]{1,0:T(8,128)(2,1)S(1)}, u32[]{:S(2)}, u32[]{:S(2)}) %collective-permute-start.41) | collective-permute-done | bytes 131104 | tf_op jit(solution)/shard_map/ppermute | solution.py:285
  214.8 1.7 collective-permute-start.47
  217.1 1.4 start_outputs.1
  219.2 1.0 put.22
  220.2 1.0 put.23
  223.5 1.0 put.26
  225.2 1.0 put.28
  226.2 1.0 put.29
  227.9 1.0 put.31
  228.9 1.0 put.32
  230.6 1.0 put.34
  231.6 1.0 put.35
  233.3 1.0 put.37
  236.0 1.0 put.40
  237.0 1.0 put.41
  (81 shorter events, 15.0 us)
Async XLA Ops:
  0.6 94.7 %copy-start = (f32[64]{0:T(128)S(1)}, f32[64]{0:T(128)}, u32[]{:S(2)}) copy-start(f32[64]{0:T(128)} %param.12) | copy-start | bytes 772
  0.6 94.7 %copy-start.1 = (f32[64]{0:T(128)S(1)}, f32[64]{0:T(128)}, u32[]{:S(2)}) copy-start(f32[64]{0:T(128)} %param.13) | copy-start | bytes 772
  4.3 4.8 %collective-permute-start = (f32[2,2048]{1,0:T(2,128)S(1)}, f32[2,2048]{1,0:T(2,128)S(1)}, u32[]{:S(2)}, u32[]{:S(2)}) collective-permute-start(f32[2,2048]{1,0:T(2,128)S(1)} %get-tuple-element.68.refs_0_), channel_id=1, source_target_pairs={{0,4},{4,0},{8,12},{12,8},{16,20},{20,16},{24,28},{28,24},{1,5},{5... | collective-permute-start | bytes 49160 | tf_op jit(solution)/shard_map/ppermute | solution.py:257
  9.1 4.7 %collective-permute-start.1 = (f32[2,2048]{1,0:T(2,128)S(1)}, f32[2,2048]{1,0:T(2,128)S(1)}, u32[]{:S(2)}, u32[]{:S(2)}) collective-permute-start(f32[2,2048]{1,0:T(2,128)S(1)} %tree_add.7.refs_0_), channel_id=1, source_target_pairs={{0,8},{4,12},{8,0},{12,4},{16,24},{20,28},{24,16},{28,20},{1,9},{5... | collective-permute-start | bytes 49160 | tf_op jit(solution)/shard_map/ppermute | solution.py:257
  11.2 4.6 %collective-permute-start.2 = (f32[2,2048]{1,0:T(2,128)S(1)}, f32[2,2048]{1,0:T(2,128)S(1)}, u32[]{:S(2)}, u32[]{:S(2)}) collective-permute-start(f32[2,2048]{1,0:T(2,128)S(1)} %tree_add.7.refs_0_), channel_id=1, source_target_pairs={{0,16},{4,20},{8,24},{12,28},{16,0},{20,4},{24,8},{28,12},{1,17},{... | collective-permute-start | bytes 49160 | tf_op jit(solution)/shard_map/ppermute | solution.py:257
  13.8 5.7 %collective-permute-start.3 = (f32[2,2048]{1,0:T(2,128)S(1)}, f32[2,2048]{1,0:T(2,128)S(1)}, u32[]{:S(2)}, u32[]{:S(2)}) collective-permute-start(f32[2,2048]{1,0:T(2,128)S(1)} %tree_add.7.refs_0_), channel_id=1, source_target_pairs={{0,24},{4,28},{8,16},{12,20},{16,8},{20,12},{24,0},{28,4},{1,25},{... | collective-permute-start | bytes 49160 | tf_op jit(solution)/shard_map/ppermute | solution.py:257
  19.7 13.4 %collective-permute-start.18 = (bf16[112,2048]{1,0:T(8,128)(2,1)S(1)}, bf16[112,2048]{1,0:T(8,128)(2,1)S(1)}, u32[]{:S(2)}, u32[]{:S(2)}) collective-permute-start(bf16[112,2048]{1,0:T(8,128)(2,1)S(1)} %get-tuple-element.71.refs_1_), channel_id=1, source_target_pairs={{0,8},{8,16},{16,24},{24,28},{28,20},{20,12},{12,4},{4,0},{1,9},{9... | collective-permute-start | bytes 1376264 | tf_op jit(solution)/shard_map/ppermute | solution.py:285
  19.8 13.4 %collective-permute-start.25 = (bf16[112,2048]{1,0:T(8,128)(2,1)S(1)}, bf16[112,2048]{1,0:T(8,128)(2,1)S(1)}, u32[]{:S(2)}, u32[]{:S(2)}) collective-permute-start(bf16[112,2048]{1,0:T(8,128)(2,1)S(1)} %get-tuple-element.72.refs_4_), channel_id=1, source_target_pairs={{8,0},{16,8},{24,16},{28,24},{20,28},{12,20},{4,12},{0,4},{9,1},{1... | collective-permute-start | bytes 1376264 | tf_op jit(solution)/shard_map/ppermute | solution.py:286
  21.8 21.2 %collective-permute-start.4 = (bf16[112,2048]{1,0:T(8,128)(2,1)S(1)}, bf16[112,2048]{1,0:T(8,128)(2,1)S(1)}, u32[]{:S(2)}, u32[]{:S(2)}) collective-permute-start(bf16[112,2048]{1,0:T(8,128)(2,1)S(1)} %get-tuple-element.69.refs_2_), channel_id=1, source_target_pairs={{0,8},{8,16},{16,24},{24,28},{28,20},{20,12},{12,4},{4,0},{1,9},{9... | collective-permute-start | bytes 1376264 | tf_op jit(solution)/shard_map/ppermute | solution.py:285
  21.8 21.2 %collective-permute-start.11 = (bf16[112,2048]{1,0:T(8,128)(2,1)S(1)}, bf16[112,2048]{1,0:T(8,128)(2,1)S(1)}, u32[]{:S(2)}, u32[]{:S(2)}) collective-permute-start(bf16[112,2048]{1,0:T(8,128)(2,1)S(1)} %get-tuple-element.70.refs_5_), channel_id=1, source_target_pairs={{8,0},{16,8},{24,16},{28,24},{20,28},{12,20},{4,12},{0,4},{9,1},{1... | collective-permute-start | bytes 1376264 | tf_op jit(solution)/shard_map/ppermute | solution.py:286
  33.1 19.7 %collective-permute-start.19 = (bf16[112,2048]{1,0:T(8,128)(2,1)S(1)}, bf16[112,2048]{1,0:T(8,128)(2,1)S(1)}, u32[]{:S(2)}, u32[]{:S(2)}) collective-permute-start(bf16[112,2048]{1,0:T(8,128)(2,1)S(1)} %collective-permute-done.18.gate), channel_id=1, source_target_pairs={{0,8},{8,16},{16,24},{24,28},{28,20},{20,12},{12,4},{4,0},{1,9},{9... | collective-permute-start | bytes 1376264 | tf_op jit(solution)/shard_map/ppermute | solution.py:285
  33.2 19.7 %collective-permute-start.26 = (bf16[112,2048]{1,0:T(8,128)(2,1)S(1)}, bf16[112,2048]{1,0:T(8,128)(2,1)S(1)}, u32[]{:S(2)}, u32[]{:S(2)}) collective-permute-start(bf16[112,2048]{1,0:T(8,128)(2,1)S(1)} %collective-permute-done.25.up), channel_id=1, source_target_pairs={{8,0},{16,8},{24,16},{28,24},{20,28},{12,20},{4,12},{0,4},{9,1},{1... | collective-permute-start | bytes 1376264 | tf_op jit(solution)/shard_map/ppermute | solution.py:286
  43.0 19.7 %collective-permute-start.5 = (bf16[112,2048]{1,0:T(8,128)(2,1)S(1)}, bf16[112,2048]{1,0:T(8,128)(2,1)S(1)}, u32[]{:S(2)}, u32[]{:S(2)}) collective-permute-start(bf16[112,2048]{1,0:T(8,128)(2,1)S(1)} %collective-permute-done.4.gate), channel_id=1, source_target_pairs={{0,8},{8,16},{16,24},{24,28},{28,20},{20,12},{12,4},{4,0},{1,9},{9... | collective-permute-start | bytes 1376264 | tf_op jit(solution)/shard_map/ppermute | solution.py:285
  43.0 19.7 %collective-permute-start.12 = (bf16[112,2048]{1,0:T(8,128)(2,1)S(1)}, bf16[112,2048]{1,0:T(8,128)(2,1)S(1)}, u32[]{:S(2)}, u32[]{:S(2)}) collective-permute-start(bf16[112,2048]{1,0:T(8,128)(2,1)S(1)} %collective-permute-done.11.up), channel_id=1, source_target_pairs={{8,0},{16,8},{24,16},{28,24},{20,28},{12,20},{4,12},{0,4},{9,1},{1... | collective-permute-start | bytes 1376264 | tf_op jit(solution)/shard_map/ppermute | solution.py:286
  52.8 34.6 %collective-permute-start.20 = (bf16[112,2048]{1,0:T(8,128)(2,1)S(1)}, bf16[112,2048]{1,0:T(8,128)(2,1)S(1)}, u32[]{:S(2)}, u32[]{:S(2)}) collective-permute-start(bf16[112,2048]{1,0:T(8,128)(2,1)S(1)} %collective-permute-done.19.gate), channel_id=1, source_target_pairs={{0,8},{8,16},{16,24},{24,28},{28,20},{20,12},{12,4},{4,0},{1,9},{9... | collective-permute-start | bytes 1376264 | tf_op jit(solution)/shard_map/ppermute | solution.py:285
  52.9 34.5 %collective-permute-start.27 = (bf16[112,2048]{1,0:T(8,128)(2,1)S(1)}, bf16[112,2048]{1,0:T(8,128)(2,1)S(1)}, u32[]{:S(2)}, u32[]{:S(2)}) collective-permute-start(bf16[112,2048]{1,0:T(8,128)(2,1)S(1)} %collective-permute-done.26.up), channel_id=1, source_target_pairs={{8,0},{16,8},{24,16},{28,24},{20,28},{12,20},{4,12},{0,4},{9,1},{1... | collective-permute-start | bytes 1376264 | tf_op jit(solution)/shard_map/ppermute | solution.py:286
  62.6 26.8 %collective-permute-start.6 = (bf16[112,2048]{1,0:T(8,128)(2,1)S(1)}, bf16[112,2048]{1,0:T(8,128)(2,1)S(1)}, u32[]{:S(2)}, u32[]{:S(2)}) collective-permute-start(bf16[112,2048]{1,0:T(8,128)(2,1)S(1)} %collective-permute-done.5.gate), channel_id=1, source_target_pairs={{0,8},{8,16},{16,24},{24,28},{28,20},{20,12},{12,4},{4,0},{1,9},{9... | collective-permute-start | bytes 1376264 | tf_op jit(solution)/shard_map/ppermute | solution.py:285
  62.7 26.8 %collective-permute-start.13 = (bf16[112,2048]{1,0:T(8,128)(2,1)S(1)}, bf16[112,2048]{1,0:T(8,128)(2,1)S(1)}, u32[]{:S(2)}, u32[]{:S(2)}) collective-permute-start(bf16[112,2048]{1,0:T(8,128)(2,1)S(1)} %collective-permute-done.12.up), channel_id=1, source_target_pairs={{8,0},{16,8},{24,16},{28,24},{20,28},{12,20},{4,12},{0,4},{9,1},{1... | collective-permute-start | bytes 1376264 | tf_op jit(solution)/shard_map/ppermute | solution.py:286
  64.7 16.3 %collective-permute-start.32 = (f32[16,2048]{1,0:T(8,128)S(1)}, f32[16,2048]{1,0:T(8,128)S(1)}, u32[]{:S(2)}, u32[]{:S(2)}) collective-permute-start(f32[16,2048]{1,0:T(8,128)S(1)} %get-tuple-element.73), channel_id=1, source_target_pairs={{0,8},{8,16},{16,24},{24,28},{28,20},{20,12},{12,4},{4,0},{1,9},{9... | collective-permute-start | bytes 393224 | tf_op jit(solution)/shard_map/ppermute | solution.py:270
  81.0 6.4 %collective-permute-start.33 = (f32[16,2048]{1,0:T(8,128)S(1)}, f32[16,2048]{1,0:T(8,128)S(1)}, u32[]{:S(2)}, u32[]{:S(2)}) collective-permute-start(f32[16,2048]{1,0:T(8,128)S(1)} %get-tuple-element.74), channel_id=1, source_target_pairs={{8,0},{16,8},{24,16},{28,24},{20,28},{12,20},{4,12},{0,4},{9,1},{1... | collective-permute-start | bytes 393224 | tf_op jit(solution)/shard_map/ppermute | solution.py:270
  87.4 6.4 %collective-permute-start.34 = (f32[16,2048]{1,0:T(8,128)S(1)}, f32[16,2048]{1,0:T(8,128)S(1)}, u32[]{:S(2)}, u32[]{:S(2)}) collective-permute-start(f32[16,2048]{1,0:T(8,128)S(1)} %get-tuple-element.75), channel_id=1, source_target_pairs={{0,8},{8,16},{16,24},{24,28},{28,20},{20,12},{12,4},{4,0},{1,9},{9... | collective-permute-start | bytes 393224 | tf_op jit(solution)/shard_map/ppermute | solution.py:270
  87.4 32.0 %collective-permute-start.21 = (bf16[112,2048]{1,0:T(8,128)(2,1)S(1)}, bf16[112,2048]{1,0:T(8,128)(2,1)S(1)}, u32[]{:S(2)}, u32[]{:S(2)}) collective-permute-start(bf16[112,2048]{1,0:T(8,128)(2,1)S(1)} %collective-permute-done.20.gate), channel_id=1, source_target_pairs={{0,8},{8,16},{16,24},{24,28},{28,20},{20,12},{12,4},{4,0},{1,9},{9... | collective-permute-start | bytes 1376264 | tf_op jit(solution)/shard_map/ppermute | solution.py:285
  87.4 32.3 %collective-permute-start.28 = (bf16[112,2048]{1,0:T(8,128)(2,1)S(1)}, bf16[112,2048]{1,0:T(8,128)(2,1)S(1)}, u32[]{:S(2)}, u32[]{:S(2)}) collective-permute-start(bf16[112,2048]{1,0:T(8,128)(2,1)S(1)} %collective-permute-done.27.up), channel_id=1, source_target_pairs={{8,0},{16,8},{24,16},{28,24},{20,28},{12,20},{4,12},{0,4},{9,1},{1... | collective-permute-start | bytes 1376264 | tf_op jit(solution)/shard_map/ppermute | solution.py:286
  89.5 32.0 %collective-permute-start.7 = (bf16[112,2048]{1,0:T(8,128)(2,1)S(1)}, bf16[112,2048]{1,0:T(8,128)(2,1)S(1)}, u32[]{:S(2)}, u32[]{:S(2)}) collective-permute-start(bf16[112,2048]{1,0:T(8,128)(2,1)S(1)} %collective-permute-done.6.gate), channel_id=1, source_target_pairs={{0,8},{8,16},{16,24},{24,28},{28,20},{20,12},{12,4},{4,0},{1,9},{9... | collective-permute-start | bytes 1376264 | tf_op jit(solution)/shard_map/ppermute | solution.py:285
  89.5 32.3 %collective-permute-start.14 = (bf16[112,2048]{1,0:T(8,128)(2,1)S(1)}, bf16[112,2048]{1,0:T(8,128)(2,1)S(1)}, u32[]{:S(2)}, u32[]{:S(2)}) collective-permute-start(bf16[112,2048]{1,0:T(8,128)(2,1)S(1)} %collective-permute-done.13.up), channel_id=1, source_target_pairs={{8,0},{16,8},{24,16},{28,24},{20,28},{12,20},{4,12},{0,4},{9,1},{1... | collective-permute-start | bytes 1376264 | tf_op jit(solution)/shard_map/ppermute | solution.py:286
  93.7 13.9 %collective-permute-start.35 = (f32[16,2048]{1,0:T(8,128)S(1)}, f32[16,2048]{1,0:T(8,128)S(1)}, u32[]{:S(2)}, u32[]{:S(2)}) collective-permute-start(f32[16,2048]{1,0:T(8,128)S(1)} %get-tuple-element.76), channel_id=1, source_target_pairs={{8,0},{16,8},{24,16},{28,24},{20,28},{12,20},{4,12},{0,4},{9,1},{1... | collective-permute-start | bytes 393224 | tf_op jit(solution)/shard_map/ppermute | solution.py:270
  107.7 3.7 %collective-permute-start.48 = (f32[1,2048]{1,0:T(1,128)S(1)}, f32[1,2048]{1,0:T(1,128)S(1)}, u32[]{:S(2)}, u32[]{:S(2)}) collective-permute-start(f32[1,2048]{1,0:T(1,128)S(1)} %slot.1.refs_0_), channel_id=1, source_target_pairs={{0,2},{1,3},{2,0},{3,1},{4,6},{5,7},{6,4},{7,5},{8,10},{9,11},{10,... | collective-permute-start | bytes 24584 | tf_op jit(solution)/shard_map/ppermute | solution.py:257
  111.3 6.4 %collective-permute-start.36 = (bf16[32,2048]{1,0:T(8,128)(2,1)S(1)}, bf16[32,2048]{1,0:T(8,128)(2,1)S(1)}, u32[]{:S(2)}, u32[]{:S(2)}) collective-permute-start(bf16[32,2048]{1,0:T(8,128)(2,1)S(1)} %get-tuple-element.77.gate), channel_id=1, source_target_pairs={{0,8},{8,16},{16,24},{24,28},{28,20},{20,12},{12,4},{4,0},{1,9},{9... | collective-permute-start | bytes 393224 | tf_op jit(solution)/shard_map/ppermute | solution.py:285
  117.7 6.2 %collective-permute-start.42 = (bf16[32,2048]{1,0:T(8,128)(2,1)S(1)}, bf16[32,2048]{1,0:T(8,128)(2,1)S(1)}, u32[]{:S(2)}, u32[]{:S(2)}) collective-permute-start(bf16[32,2048]{1,0:T(8,128)(2,1)S(1)} %get-tuple-element.78.up), channel_id=1, source_target_pairs={{8,0},{16,8},{24,16},{28,24},{20,28},{12,20},{4,12},{0,4},{9,1},{1... | collective-permute-start | bytes 393224 | tf_op jit(solution)/shard_map/ppermute | solution.py:286
  119.4 37.8 %collective-permute-start.22 = (bf16[112,2048]{1,0:T(8,128)(2,1)S(1)}, bf16[112,2048]{1,0:T(8,128)(2,1)S(1)}, u32[]{:S(2)}, u32[]{:S(2)}) collective-permute-start(bf16[112,2048]{1,0:T(8,128)(2,1)S(1)} %collective-permute-done.21.gate), channel_id=1, source_target_pairs={{0,8},{8,16},{16,24},{24,28},{28,20},{20,12},{12,4},{4,0},{1,9},{9... | collective-permute-start | bytes 1376264 | tf_op jit(solution)/shard_map/ppermute | solution.py:285
  119.7 38.8 %collective-permute-start.29 = (bf16[112,2048]{1,0:T(8,128)(2,1)S(1)}, bf16[112,2048]{1,0:T(8,128)(2,1)S(1)}, u32[]{:S(2)}, u32[]{:S(2)}) collective-permute-start(bf16[112,2048]{1,0:T(8,128)(2,1)S(1)} %collective-permute-done.28.up), channel_id=1, source_target_pairs={{8,0},{16,8},{24,16},{28,24},{20,28},{12,20},{4,12},{0,4},{9,1},{1... | collective-permute-start | bytes 1376264 | tf_op jit(solution)/shard_map/ppermute | solution.py:286
  121.5 37.8 %collective-permute-start.8 = (bf16[112,2048]{1,0:T(8,128)(2,1)S(1)}, bf16[112,2048]{1,0:T(8,128)(2,1)S(1)}, u32[]{:S(2)}, u32[]{:S(2)}) collective-permute-start(bf16[112,2048]{1,0:T(8,128)(2,1)S(1)} %collective-permute-done.7.gate), channel_id=1, source_target_pairs={{0,8},{8,16},{16,24},{24,28},{28,20},{20,12},{12,4},{4,0},{1,9},{9... | collective-permute-start | bytes 1376264 | tf_op jit(solution)/shard_map/ppermute | solution.py:285
  121.8 38.8 %collective-permute-start.15 = (bf16[112,2048]{1,0:T(8,128)(2,1)S(1)}, bf16[112,2048]{1,0:T(8,128)(2,1)S(1)}, u32[]{:S(2)}, u32[]{:S(2)}) collective-permute-start(bf16[112,2048]{1,0:T(8,128)(2,1)S(1)} %collective-permute-done.14.up), channel_id=1, source_target_pairs={{8,0},{16,8},{24,16},{28,24},{20,28},{12,20},{4,12},{0,4},{9,1},{1... | collective-permute-start | bytes 1376264 | tf_op jit(solution)/shard_map/ppermute | solution.py:286
  123.9 11.1 %collective-permute-start.49 = (f32[1,2048]{1,0:T(1,128)S(1)}, f32[1,2048]{1,0:T(1,128)S(1)}, u32[]{:S(2)}, u32[]{:S(2)}) collective-permute-start(f32[1,2048]{1,0:T(1,128)S(1)} %tree_add.9.refs_0_), channel_id=1, source_target_pairs={{0,4},{4,0},{8,12},{12,8},{16,20},{20,16},{24,28},{28,24},{1,5},{5... | collective-permute-start | bytes 24584 | tf_op jit(solution)/shard_map/ppermute | solution.py:257
  135.0 5.0 %collective-permute-start.37 = (bf16[32,2048]{1,0:T(8,128)(2,1)S(1)}, bf16[32,2048]{1,0:T(8,128)(2,1)S(1)}, u32[]{:S(2)}, u32[]{:S(2)}) collective-permute-start(bf16[32,2048]{1,0:T(8,128)(2,1)S(1)} %collective-permute-done.36.gate.refs_2_), channel_id=1, source_target_pairs={{0,8},{8,16},{16,24},{24,28},{28,20},{20,12},{12,4},{4,0},{1,9},{9... | collective-permute-start | bytes 393224 | tf_op jit(solution)/shard_map/ppermute | solution.py:285
  140.0 6.1 %collective-permute-start.43 = (bf16[32,2048]{1,0:T(8,128)(2,1)S(1)}, bf16[32,2048]{1,0:T(8,128)(2,1)S(1)}, u32[]{:S(2)}, u32[]{:S(2)}) collective-permute-start(bf16[32,2048]{1,0:T(8,128)(2,1)S(1)} %collective-permute-done.42.up), channel_id=1, source_target_pairs={{8,0},{16,8},{24,16},{28,24},{20,28},{12,20},{4,12},{0,4},{9,1},{1... | collective-permute-start | bytes 393224 | tf_op jit(solution)/shard_map/ppermute | solution.py:286
  146.0 3.7 %collective-permute-start.50 = (f32[1,2048]{1,0:T(1,128)S(1)}, f32[1,2048]{1,0:T(1,128)S(1)}, u32[]{:S(2)}, u32[]{:S(2)}) collective-permute-start(f32[1,2048]{1,0:T(1,128)S(1)} %tree_add.10.refs_0_), channel_id=1, source_target_pairs={{0,8},{4,12},{8,0},{12,4},{16,24},{20,28},{24,16},{28,20},{1,9},{5... | collective-permute-start | bytes 24584 | tf_op jit(solution)/shard_map/ppermute | solution.py:257
  149.8 6.7 %collective-permute-start.38 = (bf16[32,2048]{1,0:T(8,128)(2,1)S(1)}, bf16[32,2048]{1,0:T(8,128)(2,1)S(1)}, u32[]{:S(2)}, u32[]{:S(2)}) collective-permute-start(bf16[32,2048]{1,0:T(8,128)(2,1)S(1)} %collective-permute-done.37.gate.refs_2_), channel_id=1, source_target_pairs={{0,8},{8,16},{16,24},{24,28},{28,20},{20,12},{12,4},{4,0},{1,9},{9... | collective-permute-start | bytes 393224 | tf_op jit(solution)/shard_map/ppermute | solution.py:285
  156.5 5.0 %collective-permute-start.44 = (bf16[32,2048]{1,0:T(8,128)(2,1)S(1)}, bf16[32,2048]{1,0:T(8,128)(2,1)S(1)}, u32[]{:S(2)}, u32[]{:S(2)}) collective-permute-start(bf16[32,2048]{1,0:T(8,128)(2,1)S(1)} %collective-permute-done.43.up), channel_id=1, source_target_pairs={{8,0},{16,8},{24,16},{28,24},{20,28},{12,20},{4,12},{0,4},{9,1},{1... | collective-permute-start | bytes 393224 | tf_op jit(solution)/shard_map/ppermute | solution.py:286
  157.2 27.6 %collective-permute-start.23 = (bf16[112,2048]{1,0:T(8,128)(2,1)S(1)}, bf16[112,2048]{1,0:T(8,128)(2,1)S(1)}, u32[]{:S(2)}, u32[]{:S(2)}) collective-permute-start(bf16[112,2048]{1,0:T(8,128)(2,1)S(1)} %collective-permute-done.22.gate), channel_id=1, source_target_pairs={{0,8},{8,16},{16,24},{24,28},{28,20},{20,12},{12,4},{4,0},{1,9},{9... | collective-permute-start | bytes 1376264 | tf_op jit(solution)/shard_map/ppermute | solution.py:285
  158.5 26.3 %collective-permute-start.30 = (bf16[112,2048]{1,0:T(8,128)(2,1)S(1)}, bf16[112,2048]{1,0:T(8,128)(2,1)S(1)}, u32[]{:S(2)}, u32[]{:S(2)}) collective-permute-start(bf16[112,2048]{1,0:T(8,128)(2,1)S(1)} %collective-permute-done.29.up), channel_id=1, source_target_pairs={{8,0},{16,8},{24,16},{28,24},{20,28},{12,20},{4,12},{0,4},{9,1},{1... | collective-permute-start | bytes 1376264 | tf_op jit(solution)/shard_map/ppermute | solution.py:286
  159.2 27.6 %collective-permute-start.9 = (bf16[112,2048]{1,0:T(8,128)(2,1)S(1)}, bf16[112,2048]{1,0:T(8,128)(2,1)S(1)}, u32[]{:S(2)}, u32[]{:S(2)}) collective-permute-start(bf16[112,2048]{1,0:T(8,128)(2,1)S(1)} %collective-permute-done.8.gate), channel_id=1, source_target_pairs={{0,8},{8,16},{16,24},{24,28},{28,20},{20,12},{12,4},{4,0},{1,9},{9... | collective-permute-start | bytes 1376264 | tf_op jit(solution)/shard_map/ppermute | solution.py:285
  160.6 26.4 %collective-permute-start.16 = (bf16[112,2048]{1,0:T(8,128)(2,1)S(1)}, bf16[112,2048]{1,0:T(8,128)(2,1)S(1)}, u32[]{:S(2)}, u32[]{:S(2)}) collective-permute-start(bf16[112,2048]{1,0:T(8,128)(2,1)S(1)} %collective-permute-done.15.up), channel_id=1, source_target_pairs={{8,0},{16,8},{24,16},{28,24},{20,28},{12,20},{4,12},{0,4},{9,1},{1... | collective-permute-start | bytes 1376264 | tf_op jit(solution)/shard_map/ppermute | solution.py:286
  161.5 11.5 %collective-permute-start.51 = (f32[1,2048]{1,0:T(1,128)S(1)}, f32[1,2048]{1,0:T(1,128)S(1)}, u32[]{:S(2)}, u32[]{:S(2)}) collective-permute-start(f32[1,2048]{1,0:T(1,128)S(1)} %tree_add.11.refs_0_), channel_id=1, source_target_pairs={{0,16},{4,20},{8,24},{12,28},{16,0},{20,4},{24,8},{28,12},{1,17},{... | collective-permute-start | bytes 24584 | tf_op jit(solution)/shard_map/ppermute | solution.py:257
  173.0 5.0 %collective-permute-start.39 = (bf16[32,2048]{1,0:T(8,128)(2,1)S(1)}, bf16[32,2048]{1,0:T(8,128)(2,1)S(1)}, u32[]{:S(2)}, u32[]{:S(2)}) collective-permute-start(bf16[32,2048]{1,0:T(8,128)(2,1)S(1)} %collective-permute-done.38.gate.refs_2_), channel_id=1, source_target_pairs={{0,8},{8,16},{16,24},{24,28},{28,20},{20,12},{12,4},{4,0},{1,9},{9... | collective-permute-start | bytes 393224 | tf_op jit(solution)/shard_map/ppermute | solution.py:285
  178.0 5.0 %collective-permute-start.45 = (bf16[32,2048]{1,0:T(8,128)(2,1)S(1)}, bf16[32,2048]{1,0:T(8,128)(2,1)S(1)}, u32[]{:S(2)}, u32[]{:S(2)}) collective-permute-start(bf16[32,2048]{1,0:T(8,128)(2,1)S(1)} %collective-permute-done.44.up), channel_id=1, source_target_pairs={{8,0},{16,8},{24,16},{28,24},{20,28},{12,20},{4,12},{0,4},{9,1},{1... | collective-permute-start | bytes 393224 | tf_op jit(solution)/shard_map/ppermute | solution.py:286
  182.9 1.2 collective-permute-start.52
  184.1 6.4 %collective-permute-start.40 = (bf16[32,2048]{1,0:T(8,128)(2,1)S(1)}, bf16[32,2048]{1,0:T(8,128)(2,1)S(1)}, u32[]{:S(2)}, u32[]{:S(2)}) collective-permute-start(bf16[32,2048]{1,0:T(8,128)(2,1)S(1)} %collective-permute-done.39.gate.refs_2_), channel_id=1, source_target_pairs={{0,8},{8,16},{16,24},{24,28},{28,20},{20,12},{12,4},{4,0},{1,9},{9... | collective-permute-start | bytes 393224 | tf_op jit(solution)/shard_map/ppermute | solution.py:285
  184.8 51.2 %collective-permute-start.24 = (bf16[112,2048]{1,0:T(8,128)(2,1)S(1)}, bf16[112,2048]{1,0:T(8,128)(2,1)S(1)}, u32[]{:S(2)}, u32[]{:S(2)}) collective-permute-start(bf16[112,2048]{1,0:T(8,128)(2,1)S(1)} %collective-permute-done.23.gate), channel_id=1, source_target_pairs={{0,8},{8,16},{16,24},{24,28},{28,20},{20,12},{12,4},{4,0},{1,9},{9... | collective-permute-start | bytes 1376264 | tf_op jit(solution)/shard_map/ppermute | solution.py:285
  184.8 51.2 %collective-permute-start.31 = (bf16[112,2048]{1,0:T(8,128)(2,1)S(1)}, bf16[112,2048]{1,0:T(8,128)(2,1)S(1)}, u32[]{:S(2)}, u32[]{:S(2)}) collective-permute-start(bf16[112,2048]{1,0:T(8,128)(2,1)S(1)} %collective-permute-done.30.up), channel_id=1, source_target_pairs={{8,0},{16,8},{24,16},{28,24},{20,28},{12,20},{4,12},{0,4},{9,1},{1... | collective-permute-start | bytes 1376264 | tf_op jit(solution)/shard_map/ppermute | solution.py:286
  186.8 50.1 %collective-permute-start.10 = (bf16[112,2048]{1,0:T(8,128)(2,1)S(1)}, bf16[112,2048]{1,0:T(8,128)(2,1)S(1)}, u32[]{:S(2)}, u32[]{:S(2)}) collective-permute-start(bf16[112,2048]{1,0:T(8,128)(2,1)S(1)} %collective-permute-done.9.gate), channel_id=1, source_target_pairs={{0,8},{8,16},{16,24},{24,28},{28,20},{20,12},{12,4},{4,0},{1,9},{9... | collective-permute-start | bytes 1376264 | tf_op jit(solution)/shard_map/ppermute | solution.py:285
  186.9 50.1 %collective-permute-start.17 = (bf16[112,2048]{1,0:T(8,128)(2,1)S(1)}, bf16[112,2048]{1,0:T(8,128)(2,1)S(1)}, u32[]{:S(2)}, u32[]{:S(2)}) collective-permute-start(bf16[112,2048]{1,0:T(8,128)(2,1)S(1)} %collective-permute-done.16.up), channel_id=1, source_target_pairs={{8,0},{16,8},{24,16},{28,24},{20,28},{12,20},{4,12},{0,4},{9,1},{1... | collective-permute-start | bytes 1376264 | tf_op jit(solution)/shard_map/ppermute | solution.py:286
  190.5 19.3 %collective-permute-start.46 = (bf16[32,2048]{1,0:T(8,128)(2,1)S(1)}, bf16[32,2048]{1,0:T(8,128)(2,1)S(1)}, u32[]{:S(2)}, u32[]{:S(2)}) collective-permute-start(bf16[32,2048]{1,0:T(8,128)(2,1)S(1)} %collective-permute-done.45.up), channel_id=1, source_target_pairs={{8,0},{16,8},{24,16},{28,24},{20,28},{12,20},{4,12},{0,4},{9,1},{1... | collective-permute-start | bytes 393224 | tf_op jit(solution)/shard_map/ppermute | solution.py:286
  209.8 5.0 %collective-permute-start.41 = (bf16[32,2048]{1,0:T(8,128)(2,1)S(1)}, bf16[32,2048]{1,0:T(8,128)(2,1)S(1)}, u32[]{:S(2)}, u32[]{:S(2)}) collective-permute-start(bf16[32,2048]{1,0:T(8,128)(2,1)S(1)} %collective-permute-done.40.gate), channel_id=1, source_target_pairs={{0,8},{8,16},{16,24},{24,28},{28,20},{20,12},{12,4},{4,0},{1,9},{9... | collective-permute-start | bytes 393224 | tf_op jit(solution)/shard_map/ppermute | solution.py:285
  214.8 20.4 %collective-permute-start.47 = (bf16[32,2048]{1,0:T(8,128)(2,1)S(1)}, bf16[32,2048]{1,0:T(8,128)(2,1)S(1)}, u32[]{:S(2)}, u32[]{:S(2)}) collective-permute-start(bf16[32,2048]{1,0:T(8,128)(2,1)S(1)} %collective-permute-done.46.up), channel_id=1, source_target_pairs={{8,0},{16,8},{24,16},{28,24},{20,28},{12,20},{4,12},{0,4},{9,1},{1... | collective-permute-start | bytes 393224 | tf_op jit(solution)/shard_map/ppermute | solution.py:286
